TPU v7x, 32 devices: a 4x2x2 block of a 4x4x8 slice. The times are simulated.
32 devices in a mesh: dp: 4 (over y, z), tp: 8 (over x, core).
Axes of the slice: x: 4, y: 2, z: 2, core: 2. Of those that a mesh axis runs over, the one named last changes fastest.
The devices are a block of a 4x4x8 slice.
Arguments:
- token_ids: int32 [8, 2048], P('dp'), parts along dimension 0
- word_table: bfloat16 [51200, 3072], P('tp')
- pos_table: bfloat16 [2048, 3072], replicated
- ln_gain: float32 [3072], replicated
- ln_bias: float32 [3072], replicated
- w_qkv: bfloat16 [3072, 3, 32, 96], P(None, None, 'tp')
- b_qkv: float32 [3, 32, 96], P(None, 'tp')
- w_out: bfloat16 [32, 96, 3072], P('tp')
- b_out: float32 [3072], replicated
Outputs:
- output 1: bfloat16 [8, 2048, 3072], P('dp', 'tp'), parts along dimension 0
- output 2: bfloat16 [8, 2048, 3072], P('dp', 'tp'), parts along dimension 0
There are 4 independent parts. A program takes and returns all parts, laid end to end along the dimension named above; an argument that names none is the same for every part.
All inputs are finite; a program needn't handle non-finite values.
Results may differ from a plain program's by a relative error of at most 0.00775296.
Values are sent between devices in bfloat16 or wider.
A program may use at most 768 MiB of HBM per device.

v0:
```python
import jax
import jax.numpy as jnp
from jax import lax
from jax.sharding import PartitionSpec as P

LN_EPS = 1e-5


def layer_norm(values, gain, bias):
    feat_mean = jnp.mean(values, axis=-1, keepdims=True)
    centered = values - feat_mean
    feat_variance = jnp.mean(centered * centered, axis=-1, keepdims=True)
    return centered * lax.rsqrt(feat_variance + LN_EPS) * gain + bias


def head_outputs(normed, w_qkv, b_qkv, w_out):
    seq_len = normed.shape[1]
    head_dim = w_qkv.shape[-1]
    projected = jnp.einsum("bsd,dche->cbhse", normed, w_qkv, preferred_element_type=jnp.float32)
    projected = (projected + b_qkv[:, None, :, None, :]).astype(jnp.bfloat16)
    attn_scores = jnp.einsum("bhqe,bhke->bhqk", projected[0], projected[1], preferred_element_type=jnp.float32) * head_dim ** -0.5
    causal_mask = lax.broadcasted_iota(jnp.int32, (seq_len, seq_len), 0) >= lax.broadcasted_iota(jnp.int32, (seq_len, seq_len), 1)
    attn_scores = jnp.where(causal_mask, attn_scores, -jnp.inf)
    attn_probs = jax.nn.softmax(attn_scores, axis=-1).astype(jnp.bfloat16)
    context = jnp.einsum("bhqk,bhke->bhqe", attn_probs, projected[2], preferred_element_type=jnp.float32).astype(jnp.bfloat16)
    return jnp.einsum("cirf,ife->cre", context, w_out, preferred_element_type=jnp.float32)


def solution(mesh):
    tp_size = mesh.shape["tp"]

    def local_step(token_ids, word_shard, pos_table, ln_gain, ln_bias, w_qkv, b_qkv, w_out, b_out):
        shard_rows = word_shard.shape[0]
        block_len = token_ids.shape[1] // tp_size
        tp_index = lax.axis_index("tp")
        local_ids = token_ids - tp_index * shard_rows
        in_shard = (local_ids >= 0) & (local_ids < shard_rows)
        table_rows = jnp.take(word_shard, local_ids, axis=0, mode="clip")
        partial_rows = jnp.where(in_shard[:, :, None], table_rows, jnp.zeros((), jnp.bfloat16))
        block_rows = lax.psum_scatter(partial_rows, "tp", scatter_dimension=1, tiled=True)
        pos_block = lax.dynamic_slice_in_dim(pos_table, tp_index * block_len, block_len, axis=0)
        embed = (block_rows.astype(jnp.float32) + pos_block.astype(jnp.float32)[None]).astype(jnp.bfloat16)
        normed_block = layer_norm(embed.astype(jnp.float32), ln_gain, ln_bias).astype(jnp.bfloat16)
        normed = lax.all_gather(normed_block, "tp", axis=1, tiled=True)
        partial_out = head_outputs(normed, w_qkv, b_qkv, w_out)
        out_block = lax.psum_scatter(partial_out, "tp", scatter_dimension=1, tiled=True)
        resid_out = (embed.astype(jnp.float32) + out_block + b_out).astype(jnp.bfloat16)
        return resid_out, embed

    in_specs = (P("dp", None), P("tp", None), P(None, None), P(None), P(None), P(None, None, "tp", None), P(None, "tp", None), P("tp", None, None), P(None))
    out_specs = (P("dp", "tp", None), P("dp", "tp", None))
    return jax.shard_map(local_step, mesh=mesh, in_specs=in_specs, out_specs=out_specs, check_vma=False)
```

profile of v0, /device:TPU:81, one launch (start us, length us, event | category | flops | bytes accessed | tf_op | source)
XLA Modules:
  0.0 1085.0 jit_solution(3109439048630209746)
XLA Ops:
  7.2 0.0 copy-start
  7.2 0.1 reduce-scatter.3.cloned.1.call-start
  7.3 0.9 compare_and_fusion
  8.2 0.7 subtract_bitcast_fusion
  8.9 323.4 %gather_fusion = bf16[4096,3072]{1,0:T(8,128)(2,1)} fusion(bf16[6400,3072]{1,0:T(8,128)(2,1)} %param.10, s32[4096]{0:T(1024)S(1)} %broadcast_clamp_fusion), kind=kCustom, calls=%fused_computation | custom fusion | bytes 50348032 | tf_op jit(solution)/shard_map/jit(_take)/gather | solution.py:38
  332.3 21.1 %broadcast_select_fusion = bf16[2,2048,3072]{2,1,0:T(8,128)(2,1)} fusion(bf16[2,2048,3072]{2,1,0:T(8,128)(2,1)} %bitcast.73, pred[2,2048]{1,0:T(4,128)(4,1)S(1)} %compare_and_fusion), kind=kLoop, calls=%fused_computation.12 | loop fusion | flops 12582912 | bytes 50335744 | tf_op jit(solution)/shard_map/jit(_where)/select_n | solution.py:39
  353.4 0.1 reduce-scatter.3.cloned.1.call-update
  353.5 0.1 all-gather.2.cloned.1.call-start
  353.6 3.4 dynamic-slice_convert_fusion
  357.0 0.0 copy-start.3
  357.0 0.0 copy-start.4
  357.0 159.8 %reduce-scatter.3.cloned.1.call-done = bf16[2,256,3072]{2,1,0:T(8,128)(2,1)} async-done(((bf16[2,2048,3072]{2,1,0:T(8,128)(2,1)}), bf16[2,256,3072]{2,1,0:T(8,128)(2,1)}) %reduce-scatter.3.cloned.1.call-update) | async-done | bytes 3145744 | tf_op jit(solution)/shard_map/reduce_scatter | solution.py:40
  516.8 4.0 convert_reduce_fusion
  520.8 0.0 copy-start.1
  520.8 1.0 fusion.18
  521.8 0.7 copy-done.1
  522.5 0.0 copy-done.3
  522.5 0.0 copy-done.4
  522.5 0.0 copy-start.5
  522.5 3.4 fusion.21
  525.8 0.1 all-gather.2.cloned.1.call-update
  525.9 0.1 reduce-scatter.5.cloned.1.call-start
  526.0 4.2 iota_compare_fusion
  530.2 114.1 %all-gather.2.cloned.1.call-done = bf16[2,2048,3072]{2,1,0:T(8,128)(2,1)} async-done(((bf16[2,256,3072]{2,1,0:T(8,128)(2,1)}), bf16[2,2048,3072]{2,1,0:T(8,128)(2,1)}) %all-gather.2.cloned.1.call-update) | async-done | bytes 25165840 | tf_op jit(solution)/shard_map/all_gather | solution.py:44
  644.3 0.0 copy-done.5
  644.3 36.6 %fusion.10 = bf16[3,2,4,2048,96]{3,4,2,0,1:T(8,128)(2,1)} fusion(f32[3,4,96]{2,1,0:T(4,128)S(1)} %copy-done.5, bf16[3072,3,4,96]{0,3,2,1:T(8,128)(2,1)} %param.14, bf16[2,2048,3072]{2,1,0:T(8,128)(2,1)} %all-gather.2.cloned.1.call-done), kind=kOutput, calls=%fused_computation.20 | convolution fusion | flops 29000466432 | bytes 41685504 | tf_op jit(solution)/shard_map/bsd,dche->cbhse/dot_general | solution.py:19
  680.9 51.8 %fusion.39 = f32[2,4,2048]{2,1,0:T(4,128)S(1)} fusion(pred[2048,2048]{0,1:T(8,128)(4,1)} %iota_compare_fusion, bf16[3,2,4,2048,96]{3,4,2,0,1:T(8,128)(2,1)} %fusion.10), kind=kOutput, calls=%fused_computation.47 | convolution fusion | flops 6576670720 | bytes 10551296 | tf_op jit(solution)/shard_map/sub | solution.py:24
  732.7 69.6 %fusion.28 = bf16[2,4,2048,96]{2,3,1,0:T(8,128)(2,1)} fusion(f32[2,4,2048]{2,1,0:T(4,128)S(1)} %fusion.39, pred[2048,2048]{0,1:T(8,128)(4,1)} %iota_compare_fusion, bf16[3,2,4,2048,96]{3,4,2,0,1:T(8,128)(2,1)} %fusion.10), kind=kOutput, calls=%fused_computation.31 | convolution fusion | flops 13054265344 | bytes 16842752 | tf_op jit(solution)/shard_map/bhqk,bhke->bhqe/dot_general | solution.py:25
  802.2 0.0 copy-done
  802.2 23.2 %convolution_bitcast_fusion = f32[2,2048,3072]{2,1,0:T(8,128)} fusion(bf16[2,4,2048,96]{2,3,1,0:T(8,128)(2,1)} %fusion.28, bf16[4,96,3072]{2,1,0:T(8,128)(2,1)S(1)} %copy-done), kind=kOutput, calls=%fused_computation.13 | convolution fusion | flops 9663676416 | bytes 55836672 | tf_op jit(solution)/shard_map/cirf,ife->cre/dot_general | solution.py:26
  825.4 0.0 copy-start.2
  825.4 0.1 reduce-scatter.5.cloned.1.call-update
  825.5 246.5 %reduce-scatter.5.cloned.1.call-done = f32[2,256,3072]{2,1,0:T(8,128)} async-done(((f32[2,2048,3072]{2,1,0:T(8,128)}), f32[2,256,3072]{2,1,0:T(8,128)}) %reduce-scatter.5.cloned.1.call-update) | async-done | bytes 6291472 | tf_op jit(solution)/shard_map/reduce_scatter | solution.py:46
  1072.0 0.0 copy-done.2
  1072.0 6.4 fusion.23
  (4 shorter events, 0.0 us)
Async XLA Ops:
  7.2 795.1 %copy-start = (bf16[4,96,3072]{2,1,0:T(8,128)(2,1)S(1)}, bf16[4,96,3072]{2,1,0:T(8,128)(2,1)}, u32[]{:S(2)}) copy-start(bf16[4,96,3072]{2,1,0:T(8,128)(2,1)} %param.16) | copy-start | bytes 7077892
  7.2 509.6 %reduce-scatter.3.cloned.1.call-start = ((), (), s32[]{:S(2)}) async-start(), calls=%async_computation.2 | async-start | bytes 28311552 | tf_op jit(solution)/shard_map/reduce_scatter | solution.py:40
  353.5 290.8 %all-gather.2.cloned.1.call-start = ((), (), s32[]{:S(2)}) async-start(), calls=%async_computation.3 | async-start | bytes 28311552 | tf_op jit(solution)/shard_map/all_gather | solution.py:44
  357.0 165.5 %copy-start.3 = (f32[3072]{0:T(1024)S(1)}, f32[3072]{0:T(1024)}, u32[]{:S(2)}) copy-start(f32[3072]{0:T(1024)} %param.13) | copy-start | bytes 36868
  357.0 165.5 %copy-start.4 = (f32[3072]{0:T(1024)S(1)}, f32[3072]{0:T(1024)}, u32[]{:S(2)}) copy-start(f32[3072]{0:T(1024)} %param.12) | copy-start | bytes 36868
  520.8 1.7 copy-start.1
  522.5 121.8 %copy-start.5 = (f32[3,4,96]{2,1,0:T(4,128)S(1)}, f32[3,4,96]{2,1,0:T(4,128)}, u32[]{:S(2)}) copy-start(f32[3,4,96]{2,1,0:T(4,128)} %param.15) | copy-start | bytes 13828
  525.9 546.1 %reduce-scatter.5.cloned.1.call-start = ((), (), s32[]{:S(2)}) async-start(), calls=%async_computation.4 | async-start | bytes 56623104 | tf_op jit(solution)/shard_map/reduce_scatter | solution.py:46
  825.4 246.6 %copy-start.2 = (f32[3072]{0:T(1024)S(1)}, f32[3072]{0:T(1024)}, u32[]{:S(2)}) copy-start(f32[3072]{0:T(1024)} %param.17) | copy-start | bytes 36868
Sparse Core Ops, SparseCore 0:
  353.6 163.1 reduce-scatter.2
  526.0 118.2 all-gather.1
  825.6 246.3 reduce-scatter.4
where the time goes:
time: 1090 us; the launch traced here: 1080 us
  waiting for transfers between devices  521 us (48%)
  local copies, waits for them, and re-layouts  324 us (30%)
  matrix products  181 us (17%)
  other arithmetic  45.1 us (4%)
  between operations  13.8 us (1%)
    gather x1, local copies, waits for them, and re-layouts, local_step(): table_rows = jnp.take(word_shard, local_ids, axis=0, mode='clip')  323 us
    reduce_scatter x1, waiting for transfers between devices, local_step(): lax.psum_scatter(partial_out, 'tp', scatter_dimension=1, tiled=True)  246 us
    reduce_scatter x1, waiting for transfers between devices, local_step(): lax.psum_scatter(partial_rows, 'tp', scatter_dimension=1, tiled=True)  160 us
    all_gather x1, waiting for transfers between devices, local_step(): normed = lax.all_gather(normed_block, 'tp', axis=1, tiled=True)  114 us
    dot_general x1, matrix products, head_outputs(): jnp.einsum('bhqk,bhke->bhqe', attn_probs, projected[2], preferred_element...  69.6 us
    sub x1, matrix products, head_outputs(): attn_probs = jax.nn.softmax(attn_scores, axis=-1).astype(jnp.bfloat16)  51.8 us
    dot_general x1, matrix products, head_outputs(): jnp.einsum('bsd,dche->cbhse', normed, w_qkv, preferred_element_type=jnp.f...  36.6 us
    dot_general x1, matrix products, head_outputs(): jnp.einsum('cirf,ife->cre', context, w_out, preferred_element_type=jnp.fl...  23.2 us
  transfers between devices with their start and end apart: 3, of which 3 were waited for; matrix products, arithmetic and copies ran while one was open for 1% of the time, Pallas kernels for 0%

commit v1 on v0

v1 whole, which is shorter than its diff:
```python
import functools

import jax
import jax.numpy as jnp
from jax import lax
from jax.experimental import pallas as pl
from jax.experimental.pallas import tpu as pltpu
from jax.sharding import PartitionSpec as P

MESH = pl.DeviceIdType.MESH


def gather_all_kernel(n, S, src_ref, all_ref, loc_sem, send_sem, recv_sem):
    cap = src_ref.shape[0]

    def of(d):
        return all_ref.at[pl.ds(d * cap, cap)]
    chips = n // 2
    me = lax.axis_index("tp")
    chip, core = me // 2, lax.rem(me, 2)
    def at(c):
        return lax.rem(c + chips, chips) * 2 + core
    plus, minus, opp = at(chip + 1), at(chip - 1), at(chip + 2)
    partner = me + 1 - 2 * core
    P = 2 * S
    step = src_ref.shape[0] // P

    barrier = pltpu.get_barrier_semaphore()
    for d in (plus, minus, partner):
        pl.semaphore_signal(barrier, inc=1, device_id={"tp": d}, device_id_type=MESH)
    pl.semaphore_wait(barrier, 3)

    started = []
    def rc(src, dst, ch, k, dev):
        return pltpu.make_async_remote_copy(src_ref=src, dst_ref=dst, send_sem=send_sem.at[ch, k], recv_sem=recv_sem.at[ch, k],
                                            device_id={"tp": dev}, device_id_type=MESH)
    def go(src, dst, ch, k, dev):
        c = rc(src, dst, ch, k, dev)
        c.start()
        started.append(c)
    def piece(ref, k):
        return ref.at[pl.ds(k * step, step)]
    first, last = list(range(S)), list(range(S, P))
    for a, b in zip(first, last):
        go(piece(src_ref, a), piece(of(me), a), 0, a, plus)
        go(piece(src_ref, b), piece(of(me), b), 1, b, minus)
    for a, b in zip(first, last):
        go(piece(src_ref, b), piece(of(me), b), 0, b, plus)
        go(piece(src_ref, a), piece(of(me), a), 1, a, minus)
    go(src_ref, of(me), 4, 0, partner)
    loc = pltpu.make_async_copy(src_ref, of(me), loc_sem)
    loc.start()
    def got(owner, ch, k):
        r = piece(of(owner), k)
        rc(r, r, ch, k, partner).wait_recv()
        return r
    for a, b in zip(first, last):
        r = got(minus, 0, a)
        go(r, r, 2, a, plus)
        go(r, r, 5, a, partner)
        r = got(plus, 1, b)
        go(r, r, 3, b, minus)
        go(r, r, 6, b, partner)
    for a, b in zip(first, last):
        r = got(minus, 0, b)
        go(r, r, 5, b, partner)
        r = got(plus, 1, a)
        go(r, r, 6, a, partner)
    for a, b in zip(first, last):
        r = got(opp, 2, a)
        go(r, r, 7, a, partner)
        r = got(opp, 3, b)
        go(r, r, 7, b, partner)
    other = lambda d: d + 1 - 2 * core
    r = of(partner)
    rc(r, r, 4, 0, partner).wait_recv()
    for k in range(P):
        got(other(minus), 5, k)
        got(other(plus), 6, k)
        got(other(opp), 7, k)
    loc.wait()
    for c in started:
        c.wait_send()


def gather_all(n, rows, total, S=2, cid=0):
    return pl.pallas_call(
        functools.partial(gather_all_kernel, n, S),
        out_shape=jax.ShapeDtypeStruct((total,) + rows.shape[1:], rows.dtype),
        in_specs=[pl.BlockSpec(memory_space=pltpu.VMEM)],
        out_specs=pl.BlockSpec(memory_space=pl.ANY),
        scratch_shapes=[pltpu.SemaphoreType.DMA, pltpu.SemaphoreType.DMA((8, 2 * S)), pltpu.SemaphoreType.DMA((8, 2 * S))],
        compiler_params=pltpu.CompilerParams(collective_id=cid, has_side_effects=True),
        name="gather_all",
    )(rows)


def exchange_kernel(n, src_ref, out_ref, loc_sem, send_sem, recv_sem):
    me = lax.axis_index("tp")
    barrier = pltpu.get_barrier_semaphore()
    for s in range(1, n):
        pl.semaphore_signal(barrier, inc=1, device_id={"tp": lax.rem(me + s, n)}, device_id_type=MESH)
    pl.semaphore_wait(barrier, n - 1)
    cs = []
    for s in range(1, n):
        to = lax.rem(me + s, n)
        c = pltpu.make_async_remote_copy(src_ref=src_ref.at[to], dst_ref=out_ref.at[me], send_sem=send_sem.at[s], recv_sem=recv_sem.at[s],
                                         device_id={"tp": to}, device_id_type=MESH)
        c.start()
        cs.append(c)
    loc = pltpu.make_async_copy(src_ref.at[me], out_ref.at[me], loc_sem)
    loc.start()
    loc.wait()
    for s in range(1, n):
        fr = lax.rem(me - s + n, n)
        r = out_ref.at[fr]
        pltpu.make_async_remote_copy(src_ref=r, dst_ref=r, send_sem=send_sem.at[s], recv_sem=recv_sem.at[s],
                                     device_id={"tp": fr}, device_id_type=MESH).wait_recv()
    for c in cs:
        c.wait_send()


def exchange(n, x, cid=1):
    return pl.pallas_call(
        functools.partial(exchange_kernel, n),
        out_shape=jax.ShapeDtypeStruct(x.shape, x.dtype),
        in_specs=[pl.BlockSpec(memory_space=pltpu.VMEM)],
        out_specs=pl.BlockSpec(memory_space=pl.ANY),
        scratch_shapes=[pltpu.SemaphoreType.DMA, pltpu.SemaphoreType.DMA((n,)), pltpu.SemaphoreType.DMA((n,))],
        compiler_params=pltpu.CompilerParams(collective_id=cid, has_side_effects=True),
        name="exchange",
    )(x)


SPAN = 8192


def index_kernel(n, shard_rows, cap, ids_ref, code_ref, list_ref, cnt_ref, col, wcol, first):
    me = lax.axis_index("tp")
    R, L = ids_ref.shape
    G = 8
    lane = lax.broadcasted_iota(jnp.int32, (8, L), 1)
    sub = lax.broadcasted_iota(jnp.int32, (8, L), 0)

    def spread(src, dst):
        @pl.loop(0, R)
        def _(a):
            row = jnp.broadcast_to(src[pl.ds(a, 1), :], (L, L))
            dst[pl.ds(pl.multiple_of(a * L, L), L), :] = row.T
    spread(ids_ref, col)

    for bg in range(R // G):
        rows = [jnp.broadcast_to(ids_ref[bg * G + i:bg * G + i + 1, :], (8, L)) for i in range(G)]
        def body(a, acc):
            acc = list(acc)
            for k in range(L // 8):
                c = col[pl.ds(pl.multiple_of(a * L + k * 8, 8), 8), :]
                for i in range(G):
                    acc[i] = jnp.where(c == rows[i], 1, acc[i])
            return tuple(acc)
        acc = lax.fori_loop(0, bg * G, body, tuple(jnp.zeros((8, L), jnp.int32) for _ in range(G)))
        def diag(a, acc):
            acc = list(acc)
            for k in range(L // 8):
                c = col[pl.ds(pl.multiple_of(a * L + k * 8, 8), 8), :]
                t = a * L + k * 8 + sub
                for i in range(G):
                    s = lane + (bg * G + i) * L
                    acc[i] = jnp.where((c == rows[i]) & (t < s), 1, acc[i])
            return tuple(acc)
        acc = lax.fori_loop(bg * G, bg * G + G, diag, acc)
        for i in range(G):
            first[bg * G + i:bg * G + i + 1, :] = 1 - jnp.max(acc[i], axis=0, keepdims=True)

    ids = ids_ref[...]
    owner = jnp.zeros((R, L), jnp.int32)
    for o in range(1, n):
        owner = owner + jnp.where(ids >= o * shard_rows, 1, 0)
    isf = first[...] == 1
    one = jnp.concatenate([jnp.where(isf & (owner == o), 1.0, 0.0) for o in range(n)], axis=0).astype(jnp.bfloat16)
    up = (lax.broadcasted_iota(jnp.int32, (L, L), 0) < lax.broadcasted_iota(jnp.int32, (L, L), 1)).astype(jnp.float32).astype(jnp.bfloat16)
    prefix = jnp.dot(one, up, preferred_element_type=jnp.float32)
    tot = jnp.dot(one, jnp.ones((L, L), jnp.bfloat16), preferred_element_type=jnp.float32)
    r = lax.broadcasted_iota(jnp.int32, (n * R, n * R), 0)
    c = lax.broadcasted_iota(jnp.int32, (n * R, n * R), 1)
    low = ((r // R == c // R) & (c < r)).astype(jnp.float32).astype(jnp.bfloat16)
    off = jnp.dot(low, tot.astype(jnp.bfloat16), preferred_element_type=jnp.float32)
    pos = prefix + off
    slot = jnp.zeros((R, L), jnp.float32)
    most = jnp.zeros((1, L), jnp.float32)
    for o in range(n):
        slot = jnp.where(owner == o, pos[o * R:(o + 1) * R], slot)
        most = jnp.maximum(most, (off + tot)[(o + 1) * R - 1:(o + 1) * R])
    cnt_ref[...] = most.astype(jnp.int32)
    first[...] = jnp.where(isf, owner * SPAN + slot.astype(jnp.int32) + 1, 0)
    spread(first, wcol)

    for bg in range(R // G):
        rows = [jnp.broadcast_to(ids_ref[bg * G + i:bg * G + i + 1, :], (8, L)) for i in range(G)]
        def body(a, acc):
            acc = list(acc)
            for k in range(L // 8):
                at = pl.ds(pl.multiple_of(a * L + k * 8, 8), 8)
                c, w = col[at, :], wcol[at, :]
                for i in range(G):
                    acc[i] = jnp.where(c == rows[i], jnp.maximum(acc[i], w), acc[i])
            return tuple(acc)
        acc = lax.fori_loop(0, bg * G + G, body, tuple(jnp.zeros((8, L), jnp.int32) for _ in range(G)))
        for i in range(G):
            code_ref[bg * G + i:bg * G + i + 1, :] = jnp.max(acc[i], axis=0, keepdims=True) - 1

    K = list_ref.shape[0]
    want = [me * SPAN + 1 + i * L + lane for i in range(K)]
    def body(a, acc):
        acc = list(acc)
        for k in range(L // 8):
            at = pl.ds(pl.multiple_of(a * L + k * 8, 8), 8)
            c, w = col[at, :], wcol[at, :]
            for i in range(K):
                acc[i] = jnp.where(w == want[i], c, acc[i])
        return tuple(acc)
    acc = lax.fori_loop(0, R, body, tuple(jnp.zeros((8, L), jnp.int32) for _ in range(K)))
    for i in range(K):
        list_ref[i:i + 1, :] = jnp.maximum(jnp.max(acc[i], axis=0, keepdims=True) - me * shard_rows, 0)


def index(n, shard_rows, cap, ids):
    R, L = ids.size // 128, 128
    K = -(-cap // L)
    return pl.pallas_call(
        functools.partial(index_kernel, n, shard_rows, cap),
        out_shape=(jax.ShapeDtypeStruct((R, L), jnp.int32), jax.ShapeDtypeStruct((K, L), jnp.int32), jax.ShapeDtypeStruct((1, L), jnp.int32)),
        scratch_shapes=[pltpu.VMEM((R * L, L), jnp.int32), pltpu.VMEM((R * L, L), jnp.int32), pltpu.VMEM((R, L), jnp.int32)],
        name="index",
    )(ids.reshape(R, L))


def rows_kernel(cap, nb, list_ref, table_ref, out_ref, buf, scr, sem):
    T = table_ref.shape[1] // 128
    U = 8
    def copy(k):
        row = list_ref[k]
        base = pl.multiple_of((row // 8) * 8, 8)
        s = lax.rem(k, nb)
        return pltpu.make_async_copy(table_ref.at[pl.ds(base, 8)], buf.at[s], sem.at[s])
    for k in range(nb):
        copy(k).start()
    @pl.loop(0, cap // U)
    def _(q):
        for u in range(U):
            k = q * U + u
            s = lax.rem(k, nb)
            copy(k).wait()
            for j in range(T):
                scr[u, j * 8:(j + 1) * 8, :] = buf[s, :, j * 128:(j + 1) * 128].astype(jnp.float32)
            r = lax.rem(list_ref[k], 8)
            out_ref[k] = scr[u, pl.ds(r, T, stride=8), :].astype(jnp.bfloat16)
        for u in range(U):
            k = q * U + u
            @pl.when(k + nb < cap)
            def _():
                copy(k + nb).start()


def rows(cap, lst, table, nb=32):
    T = table.shape[1] // 128
    return pl.pallas_call(
        functools.partial(rows_kernel, cap, nb),
        out_shape=jax.ShapeDtypeStruct((cap, T, 128), table.dtype),
        grid_spec=pltpu.PrefetchScalarGridSpec(
            num_scalar_prefetch=1, grid=(),
            in_specs=[pl.BlockSpec(memory_space=pl.ANY)],
            out_specs=pl.BlockSpec(memory_space=pltpu.VMEM),
            scratch_shapes=[pltpu.VMEM((nb, 8, table.shape[1]), table.dtype), pltpu.VMEM((8, T * 8, 128), jnp.float32), pltpu.SemaphoreType.DMA((nb,))]),
        name="rows",
    )(lst, table)


EPS = 1e-5


def project_kernel(cap, span, tb, seq, blk, nsteps, meta, code, u_ref, pos_ref, own_pos_ref, gain_ref, bias_ref, wa_ref, wb_ref, ba_ref, bb_ref,
                   qkv_ref, emb_ref, xs, hs):
    step = pl.program_id(0)
    T = u_ref.shape[1]
    D = T * 128
    inv = 1.0 / D

    def fetch(base, t16):
        for half in range(2):
            for r in range(8):
                c = code[base + t16 * 16 + half * 8 + r]
                at = lax.div(c, span) * cap + lax.rem(c, span)
                xs[half, pl.ds(r, T, stride=8), :] = u_ref[at].astype(jnp.float32)

    def embed(half, p):
        return [(xs[half, j * 8:(j + 1) * 8, :] + p[half * 8:half * 8 + 8, j * 128:(j + 1) * 128].astype(jnp.float32)).astype(jnp.bfloat16) for j in range(T)]

    @pl.when(step < nsteps)
    def _():
        base = meta[1] * seq + step * tb
        @pl.loop(0, tb // 16)
        def _(g):
            fetch(base, g)
            t = pl.multiple_of(g * 16, 16)
            p = pos_ref.at[pl.ds(t, 16), :]
            out = []
            for half in range(2):
                e = [v.astype(jnp.float32) for v in embed(half, p)]
                s = e[0]
                for j in range(1, T):
                    s = s + e[j]
                mean = jnp.sum(s, axis=1, keepdims=True) * inv
                mb = jnp.broadcast_to(mean, (8, 128))
                e = [v - mb for v in e]
                s = e[0] * e[0]
                for j in range(1, T):
                    s = s + e[j] * e[j]
                var = jnp.sum(s, axis=1, keepdims=True) * inv
                rs = jnp.broadcast_to(lax.rsqrt(var + EPS), (8, 128))
                out.append([e[j] * rs * gain_ref[:, j * 128:(j + 1) * 128] + bias_ref[:, j * 128:(j + 1) * 128] for j in range(T)])
            for j in range(T):
                hs[pl.ds(t, 16), j * 128:(j + 1) * 128] = jnp.concatenate([out[0][j], out[1][j]], axis=0).astype(jnp.bfloat16)
        M = 384
        for k, (w, b) in enumerate(((wa_ref, ba_ref), (wb_ref, bb_ref))):
            for m in range(0, w.shape[0], M):
                o = lax.dot_general(w[m:m + M, :], hs[...], (((1,), (1,)), ((), ())), preferred_element_type=jnp.float32)
                qkv_ref[k, m:m + M, :] = (o + b[m:m + M, :]).astype(jnp.bfloat16)

    @pl.when(step == nsteps)
    def _():
        for b in range(2):
            base = b * seq + meta[0] * blk
            @pl.loop(0, blk // 16)
            def _(g):
                fetch(base, g)
                t = pl.multiple_of(g * 16, 16)
                p = own_pos_ref.at[pl.ds(t, 16), :]
                e0, e1 = embed(0, p), embed(1, p)
                for j in range(T):
                    emb_ref[b, pl.ds(t, 16), j * 128:(j + 1) * 128] = jnp.concatenate([e0[j], e1[j]], axis=0)


def project(n, cap, span, meta, code, u, pos, gain, bias, wa, wb, ba, bb, tb=512):
    seq, D = pos.shape
    blk = seq // n
    nsteps = seq // tb
    M = wa.shape[0]
    last = nsteps - 1
    one = lambda shape: pl.BlockSpec(shape, lambda i, *_: (0,) * len(shape), pipeline_mode=pl.Buffered(1))
    return pl.pallas_call(
        functools.partial(project_kernel, cap, span, tb, seq, blk, nsteps),
        out_shape=(jax.ShapeDtypeStruct((2, M, seq), jnp.bfloat16), jax.ShapeDtypeStruct((2, blk, D), jnp.bfloat16)),
        grid_spec=pltpu.PrefetchScalarGridSpec(
            num_scalar_prefetch=2, grid=(nsteps + 1,),
            in_specs=[one(u.shape),
                      pl.BlockSpec((tb, D), lambda i, *_: (jnp.minimum(i, last), 0)),
                      pl.BlockSpec((blk, D), lambda i, meta, code: (meta[0], 0), pipeline_mode=pl.Buffered(1)),
                      one((1, D)), one((1, D)), one(wa.shape), one(wb.shape), one(ba.shape), one(bb.shape)],
            out_specs=(pl.BlockSpec((2, M, tb), lambda i, *_: (0, 0, jnp.minimum(i, last))), pl.BlockSpec((2, blk, D), lambda i, *_: (0, 0, 0), pipeline_mode=pl.Buffered(1))),
            scratch_shapes=[pltpu.VMEM((2, D // 128 * 8, 128), jnp.float32), pltpu.VMEM((tb, D), jnp.bfloat16)]),
        compiler_params=pltpu.CompilerParams(vmem_limit_bytes=60 * 2**20),
        name="project",
    )(meta, code, u, pos, pos, gain, bias, wa, wb, ba, bb)


def attention_kernel(scale, qb, meta, qkv_ref, out_ref, kk, vv, sc):
    E, S = qkv_ref.shape[3:]
    c = scale * 1.4426950408889634
    for t in range(0, S, 128):
        kk[t:t + 128, :] = qkv_ref[0, 1, 0, :, t:t + 128].astype(jnp.float32).T.astype(jnp.bfloat16)
    vv[0:E, :] = qkv_ref[0, 2, 0]
    vv[E:, :] = jnp.where(lax.broadcasted_iota(jnp.int32, (vv.shape[0] - E, S), 0) == 0, 1.0, 0.0).astype(jnp.bfloat16)
    keep = lax.broadcasted_iota(jnp.int32, (qb, qb), 0) <= lax.broadcasted_iota(jnp.int32, (qb, qb), 1)
    for i in range(S // qb):
        n = (i + 1) * qb
        q = qkv_ref[0, 0, 0, :, i * qb:n]
        s = jnp.dot(kk[0:n, :], q, preferred_element_type=jnp.float32)
        d = jnp.where(keep, s[n - qb:n], -jnp.inf)
        s = d if i == 0 else jnp.concatenate([s[:n - qb], d], axis=0)
        m = jnp.max(s, axis=0, keepdims=True) * c
        p = jnp.exp2(s * c - m).astype(jnp.bfloat16)
        o = jnp.dot(vv[:, 0:n], p, preferred_element_type=jnp.float32)
        out_ref[i, 0, 0] = (o[0:E] * (1.0 / o[E:E + 1])).astype(jnp.bfloat16)


def attention(n, meta, qkv, qb=256):
    _, _, H, E, S = qkv.shape
    return pl.pallas_call(
        functools.partial(attention_kernel, E ** -0.5, qb),
        out_shape=jax.ShapeDtypeStruct((n, 2, H, E, S // n), jnp.bfloat16),
        grid_spec=pltpu.PrefetchScalarGridSpec(
            num_scalar_prefetch=1, grid=(2, H),
            in_specs=[pl.BlockSpec((1, 3, 1, E, S), lambda k, h, meta: (k, 0, h, 0, 0))],
            out_specs=pl.BlockSpec((n, 1, 1, E, S // n), lambda k, h, meta: (0, lax.rem(meta[1] + k, 2), h, 0, 0)),
            scratch_shapes=[pltpu.VMEM((S, E), jnp.bfloat16), pltpu.VMEM((E + 16, S), jnp.bfloat16), pltpu.VMEM((S, qb), jnp.float32)]),
        compiler_params=pltpu.CompilerParams(vmem_limit_bytes=48 * 2**20),
        name="attention",
    )(meta, qkv)


def output_kernel(n, nb, owners, lows, meta, ctx_ref, emb_ref, bias_ref, *refs):
    pieces, (out_ref, w, a, sem) = refs[:-4], refs[-4:]
    K, blk = ctx_ref.shape[1:]
    D = w.shape[2]
    def copy(i, j):
        rows = pieces[i].shape[0]
        return pltpu.make_async_copy(pieces[i].at[:, pl.ds(j * nb, nb)], w.at[meta[owners[i]], pl.ds(lows[i], rows), pl.ds(j * nb, nb)], sem.at[i, j])
    for j in range(D // nb):
        for i in range(len(pieces)):
            copy(i, j).start()
    for s in range(n):
        for k in range(0, K, 128):
            for t in range(0, blk, 128):
                a[(s % 2) * blk + t:(s % 2) * blk + t + 128, (s // 2) * K + k:(s // 2) * K + k + 128] = ctx_ref[s, k:k + 128, t:t + 128].astype(jnp.float32).T.astype(jnp.bfloat16)
    for j in range(D // nb):
        for i in range(len(pieces)):
            copy(i, j).wait()
        cols = slice(j * nb, (j + 1) * nb)
        o = jnp.dot(a[...], w[:, :, cols].reshape(n * w.shape[1], nb), preferred_element_type=jnp.float32)
        for b in range(2):
            out_ref[b, :, cols] = (emb_ref[b, :, cols].astype(jnp.float32) + o[b * blk:(b + 1) * blk] + bias_ref[:, cols]).astype(jnp.bfloat16)


def output(n, meta, ctx, emb, bias, pieces, owners, lows, nb=512):
    D = emb.shape[2]
    rows = sum(p.shape[0] for p in pieces) // n
    V = pl.BlockSpec(memory_space=pltpu.VMEM)
    return pl.pallas_call(
        functools.partial(output_kernel, n, nb, owners, lows),
        out_shape=jax.ShapeDtypeStruct(emb.shape, jnp.bfloat16),
        grid_spec=pltpu.PrefetchScalarGridSpec(
            num_scalar_prefetch=1, grid=(),
            in_specs=[V, V, V] + [pl.BlockSpec(memory_space=pl.ANY)] * len(pieces),
            out_specs=V,
            scratch_shapes=[pltpu.VMEM((n, rows, D), jnp.bfloat16), pltpu.VMEM((2 * emb.shape[1], D), jnp.bfloat16), pltpu.SemaphoreType.DMA((len(pieces), D // nb))]),
        compiler_params=pltpu.CompilerParams(vmem_limit_bytes=60 * 2**20),
        name="output",
    )(meta, ctx, emb, bias, *pieces)


CAP = 264


def place_kernel(code_ref, u_ref, x_ref, out_ref, sem):
    @pl.loop(0, code_ref.shape[0])
    def _(t):
        c = code_ref[t]

        @pl.when(c >= 0)
        def _():
            copy = pltpu.make_async_copy(u_ref.at[c], out_ref.at[t], sem)
            copy.start()
            copy.wait()


def place(at, u, x):
    A = pl.BlockSpec(memory_space=pl.ANY)
    return pl.pallas_call(
        place_kernel,
        out_shape=jax.ShapeDtypeStruct(x.shape, x.dtype),
        grid_spec=pltpu.PrefetchScalarGridSpec(num_scalar_prefetch=1, grid=(), in_specs=[A, A], out_specs=A, scratch_shapes=[pltpu.SemaphoreType.DMA]),
        input_output_aliases={2: 0},
        name="place",
    )(at, u, x)


def solution(mesh):
    n = mesh.shape["tp"]
    chips = n // 2

    def ring(step):
        return [((c * 2 + k), ((c + step) % chips) * 2 + k) for c in range(chips) for k in range(2)]

    swap = [(d, d ^ 1) for d in range(n)]
    permute = lambda x, perm: lax.ppermute(x, "tp", perm)

    def local_step(token_ids, word_shard, pos_table, ln_gain, ln_bias, w_qkv, b_qkv, w_out, b_out):
        me = lax.axis_index("tp")
        core = lax.rem(me, 2)
        seq, D = pos_table.shape
        H, E = w_qkv.shape[2:]
        shard_rows = word_shard.shape[0]
        w_own = jnp.transpose(w_qkv, (1, 2, 3, 0)).reshape(3 * H * E, D)
        b_own = b_qkv.reshape(3 * H * E, 1)
        w_par, b_par = permute(w_own, swap), permute(b_own, swap)

        v_own = w_out.reshape(H * E, D)
        half = v_own.shape[0] // 2
        v_minus, v_plus = permute(v_own, ring(1)), permute(v_own, ring(-1))
        v_opp_a, v_opp_b = permute(v_minus[:half], ring(1)), permute(v_plus[half:], ring(-1))
        pieces = [v_own, v_minus, v_plus, v_opp_a, v_opp_b]
        pieces = pieces + [permute(p, swap) for p in pieces]
        owners, lows = [0, 3, 4, 5, 5, 6, 7, 8, 9, 9], [0, 0, 0, 0, half] * 2
        at = lambda c, k: lax.rem(c + chips, chips) * 2 + k
        chip = me // 2
        meta = [me, core, chip] + [at(chip + s, k) for k in (core, 1 - core) for s in (-1, 1, 2)]
        meta = meta[:6] + [me + 1 - 2 * core] + meta[6:]
        meta = jnp.stack(meta).astype(jnp.int32)

        blk = seq // n
        total = max(n * CAP, seq + blk)
        code, rows_list, most = index(n, shard_rows, CAP, token_ids)
        code, most = code.reshape(-1), most[0, 0]
        u = gather_all(n, rows(CAP, rows_list.reshape(-1), word_shard), total)

        rounds = jnp.where(most > CAP, (most + CAP - 1) // CAP, 0)

        def wanted(x):
            x = x.reshape(2, seq)
            own = lax.dynamic_index_in_dim(x, core, 0, keepdims=False)
            other = lax.dynamic_index_in_dim(x, 1 - core, 0, keepdims=False)
            return jnp.concatenate([own, lax.dynamic_slice_in_dim(other, me * blk, blk)])

        def more(carry):
            r, u = carry
            slot = code % SPAN - r * CAP
            hit = (slot >= 0) & (slot < CAP)
            mine = jnp.where(hit & (code // SPAN == me), slot, -1)
            ids = token_ids.reshape(-1) - me * shard_rows
            chosen = jnp.max(jnp.where(mine[None, :] == jnp.arange(rows_list.size)[:, None], ids[None, :], 0), axis=1)
            v = gather_all(n, rows(CAP, chosen, word_shard), total)
            return r + 1, place(wanted(jnp.where(hit, code // SPAN * CAP + slot, -1)), v, u)

        _, u = lax.while_loop(lambda c: c[0] < rounds, more, (jnp.int32(0), u))
        t = jnp.arange(code.size, dtype=jnp.int32)
        t = jnp.where(t // seq == core, t % seq, jnp.clip(t % seq - me * blk, 0, blk - 1) + seq)
        code = jnp.where(rounds > 0, t // CAP * SPAN + t % CAP, code)

        qkv, embed = project(n, CAP, SPAN, meta, code, u, pos_table, ln_gain[None], ln_bias[None], w_own, w_par, b_own, b_par)
        ctx = attention(n, meta, qkv.reshape(2, 3, H, E, seq))
        ctx = exchange(n, ctx.reshape(n, 2 * H * E, seq // n))
        resid_out = output(n, meta, ctx, embed, b_out[None], pieces, owners, lows)
        return resid_out, embed

    in_specs = (P("dp", None), P("tp", None), P(None, None), P(None), P(None), P(None, None, "tp", None), P(None, "tp", None), P("tp", None, None), P(None))
    out_specs = (P("dp", "tp", None), P("dp", "tp", None))
    return jax.shard_map(local_step, mesh=mesh, in_specs=in_specs, out_specs=out_specs, check_vma=False)
```

time: 1090 us -> 363 us (0.33)
  waiting for transfers between devices: 521 us -> 51.4 us
  local copies, waits for them, and re-layouts: 324 us -> 8.64 us
  Pallas kernels: 0 us -> 288 us
  matrix products: 181 us -> 0 us
  other arithmetic: 45.1 us -> 0.63 us
  between operations: 13.8 us -> 2.31 us
    reduce_scatter x2 -> x0, waiting for transfers between devices: 406 us -> none  [the longest x1 246 us: local_step(): lax.psum_scatter(partial_out, 'tp', scatter_dimension=1, tiled=True)]
    gather x1 -> x0, local copies, waits for them, and re-layouts: 323 us -> none  [local_step(): table_rows = jnp.take(word_shard, local_ids, axis=0, mode='clip')]
    pallas_call x0 -> x7, Pallas kernels: none -> 288 us  [the longest x1 89 us: project(): pl.pallas_call(functools.partial(project_kernel, cap, span, tb, seq, blk,...]
    dot_general x3 -> x0, matrix products: 129 us -> none  [the longest x1 69.6 us: head_outputs(): jnp.einsum('bhqk,bhke->bhqe', attn_probs, projected[2], preferred_element...]
    all_gather x1 -> x0, waiting for transfers between devices: 114 us -> none  [local_step(): normed = lax.all_gather(normed_block, 'tp', axis=1, tiled=True)]
    sub x1 -> x0, matrix products: 51.8 us -> none  [head_outputs(): attn_probs = jax.nn.softmax(attn_scores, axis=-1).astype(jnp.bfloat16)]
    ppermute x0 -> x11, waiting for transfers between devices: none -> 51.4 us  [solution(): permute = lambda x, perm: lax.ppermute(x, 'tp', perm)]
    select_n x1 -> x0, other arithmetic: 21.1 us -> none  [local_step(): jnp.where(in_shard[:, :, None], table_rows, jnp.zeros((), jnp.bfloat16))]
  transfers between devices with their start and end apart: 3 -> 11, of which waited for: 3 -> 1; matrix products, arithmetic and copies ran while one was open for 1% -> 2% of each run, Pallas kernels for 0% -> 75%
where the time goes in v1:
time: 363 us; the launch traced here: 361 us
  Pallas kernels  288 us (79%)
  waiting for transfers between devices  51.4 us (14%)
  starting transfers between devices  10.3 us (3%)
  local copies, waits for them, and re-layouts  8.64 us (2%)
    pallas_call x1, Pallas kernels, project(): pl.pallas_call(functools.partial(project_kernel, cap, span, tb, seq, blk,...  89 us
    pallas_call x1, Pallas kernels, gather_all(): pl.pallas_call(functools.partial(gather_all_kernel, n, S), out_shape=jax....  60.3 us
    ppermute x11, waiting for transfers between devices, solution(): permute = lambda x, perm: lax.ppermute(x, 'tp', perm)  51.4 us
    pallas_call x1, Pallas kernels, attention(): pl.pallas_call(functools.partial(attention_kernel, E ** (-0.5), qb), out_...  49 us
    pallas_call x1, Pallas kernels, exchange(): pl.pallas_call(functools.partial(exchange_kernel, n), out_shape=jax.Shape...  39.9 us
    pallas_call x1, Pallas kernels, index(): pl.pallas_call(functools.partial(index_kernel, n, shard_rows, cap), out_s...  18.5 us
    pallas_call x1, Pallas kernels, output(): pl.pallas_call(functools.partial(output_kernel, n, nb, owners, lows), out...  18.4 us
    pallas_call x1, Pallas kernels, rows(): pl.pallas_call(functools.partial(rows_kernel, cap, nb), out_shape=jax.Sha...  12.8 us
  transfers between devices with their start and end apart: 11, of which 1 were waited for; matrix products, arithmetic and copies ran while one was open for 2% of the time, Pallas kernels for 75%

profile of v1, /device:TPU:81, one launch (start us, length us, event | category | flops | bytes accessed | tf_op | source)
XLA Modules:
  0.0 361.1 jit_solution(17652242707682932933)
XLA Ops:
  0.6 0.0 copy-start.5
  0.6 0.0 copy-start.2
  0.6 2.1 collective-permute-start
  2.8 0.8 collective-permute-start.2
  3.5 1.9 collective-permute-start.3
  5.5 51.3 %collective-permute-done.2.refs_1_ = bf16[384,3072]{1,0:T(8,128)(2,1)} collective-permute-done((bf16[384,3072]{1,0:T(8,128)(2,1)}, bf16[384,3072]{1,0:T(8,128)(2,1)}, u32[]{:S(2)}, u32[]{:S(2)}) %collective-permute-start.2) | collective-permute-done | bytes 2359328 | tf_op jit(solution)/shard_map/ppermute | solution.py:476
  56.8 1.3 slice.12
  58.1 0.1 collective-permute-start.4
  58.2 0.0 collective-permute-done.3.refs_2_
  58.3 1.3 slice.13
  59.6 2.7 collective-permute-start.5
  62.3 1.4 collective-permute-start.6
  63.8 0.0 copy-done.5
  63.8 0.1 reshape.150
  63.9 0.0 copy-start.3
  63.9 0.1 collective-permute-start.1
  64.0 0.0 copy-done.2
  64.0 0.6 reshape.146.ids_ref
  64.6 18.5 %index.1 = (s32[32,128]{1,0:T(8,128)S(1)}, s32[3,128]{1,0:T(4,128)}, s32[1,128]{1,0:T(1,128)}) custom-call(s32[32,128]{1,0:T(8,128)} %reshape.146.ids_ref), custom_call_target="tpu_custom_call" | custom-call | tf_op jit(solution)/shard_map/index/pallas_call | solution.py:230
  84.4 0.6 bitcast_negate_fusion
  85.1 12.8 %rows.2.src_ref = bf16[264,24,128]{2,1,0:T(8,128)(2,1)} custom-call(s32[384]{0:T(512)} %bitcast.65, bf16[6400,3072]{1,0:T(8,128)(2,1)} %table_ref.1), custom_call_target="tpu_custom_call" | custom-call | tf_op jit(solution)/shard_map/rows/pallas_call | solution.py:267
  97.8 0.0 copy-done.3
  97.8 60.3 %gather_all.2 = bf16[2304,24,128]{2,1,0:T(8,128)(2,1)} custom-call(bf16[264,24,128]{2,1,0:T(8,128)(2,1)} %rows.2.src_ref), custom_call_target="tpu_custom_call" | custom-call | tf_op jit(solution)/shard_map/gather_all/pallas_call | solution.py:87
  158.2 0.0 collective-permute-done.1
  158.2 0.2 collective-permute-start.7
  158.5 0.0 collective-permute-done.4.refs_3_
  158.5 0.4 collective-permute-start.8
  158.8 0.0 collective-permute-done.5.refs_4_
  158.8 0.1 collective-permute-start.9
  159.0 0.0 collective-permute-done.wb_ref
  159.0 0.4 collective-permute-start.10
  159.3 0.0 copy-start.4
  159.3 0.7 copy-done.4
  160.0 1.1 copy.16.ba_ref
  161.1 0.7 stack.43.meta
  161.8 1.1 copy.17.bb_ref
  162.9 89.0 %project.1 = (bf16[2,1152,2048]{2,1,0:T(8,128)(2,1)}, bf16[2,256,3072]{2,1,0:T(8,128)(2,1)}) custom-call(s32[10]{0:T(128)} %stack.43.meta, s32[4096]{0:T(1024)} %get-tuple-element.348.code, bf16[2304,24,128]{2,1,0:T(8,128)(2,1)} %get-tuple-element.312.u_ref, bf16[2048,3072]{1,0:T(8,128)(2,1)} %own_pos_ref.1, bf16[2048,3072]{1,0:T(8,128)(2,1)} %own_pos_ref.1, ...), custom_call_target="tpu_custom_call" | custom-call | tf_op jit(solution)/shard_map/project/pallas_call | solution.py:351
  251.9 0.0 copy-done.1
  251.9 49.0 %attention.1 = bf16[8,2,4,96,256]{4,3,2,1,0:T(8,128)(2,1)S(1)} custom-call(s32[10]{0:T(128)S(1)} %copy-done.1, bf16[2,3,4,96,2048]{4,3,2,1,0:T(8,128)(2,1)} %bitcast.51), custom_call_target="tpu_custom_call" | custom-call | tf_op jit(solution)/shard_map/attention/pallas_call | solution.py:389
  300.9 0.0 copy-start
  300.9 1.7 copy-done
  302.6 39.9 %exchange.1.ctx_ref = bf16[8,768,256]{2,1,0:T(8,128)(2,1)} custom-call(bf16[8,768,256]{2,1,0:T(8,128)(2,1)} %bitcast.50), custom_call_target="tpu_custom_call" | custom-call | tf_op jit(solution)/shard_map/exchange/pallas_call | solution.py:124
  342.5 0.0 collective-permute-done.6.refs_5_
  342.5 0.0 collective-permute-done.7.refs_6_
  342.5 0.0 collective-permute-done.8.refs_7_
  342.5 0.0 collective-permute-done.9.refs_8_
  342.5 0.0 collective-permute-done.10.refs_9_
  342.6 18.4 %output.1 = bf16[2,256,3072]{2,1,0:T(8,128)(2,1)} custom-call(s32[10]{0:T(128)} %stack.43.meta, bf16[8,768,256]{2,1,0:T(8,128)(2,1)} %exchange.1.ctx_ref, bf16[2,256,3072]{2,1,0:T(8,128)(2,1)} %get-tuple-element.308.emb_ref, f32[1,3072]{1,0:T(1,128)} %bitcast.62, bf16[384,3072]{1,0:T(8,128)(2,1)} %bitcast.28.refs_0_, ...), custom_call_target="tpu_custom_call" | custom-call | tf_op jit(solution)/shard_map/output/pallas_call | solution.py:429
  (6 shorter events, 0.1 us)
Async XLA Ops:
  0.6 63.1 %copy-start.5 = (f32[3,4,96]{2,1,0:T(4,128)S(1)}, f32[3,4,96]{2,1,0:T(4,128)}, u32[]{:S(2)}) copy-start(f32[3,4,96]{2,1,0:T(4,128)} %param.17) | copy-start | bytes 13828
  0.6 63.4 %copy-start.2 = (s32[2,2048]{1,0:T(2,128)S(1)}, s32[2,2048]{1,0:T(2,128)}, u32[]{:S(2)}) copy-start(s32[2,2048]{1,0:T(2,128)} %param.11) | copy-start | bytes 49156
  0.6 158.3 %collective-permute-start = (bf16[1152,3072]{1,0:T(8,128)(2,1)}, bf16[1152,3072]{1,0:T(8,128)(2,1)}, u32[]{:S(2)}, u32[]{:S(2)}) collective-permute-start(bf16[1152,3072]{1,0:T(8,128)(2,1)} %bitcast.52), channel_id=1, source_target_pairs={{0,1},{1,0},{2,3},{3,2},{4,5},{5,4},{6,7},{7,6},{8,9},{9,8},{10,11... | collective-permute-start | bytes 21233672 | tf_op jit(solution)/shard_map/ppermute | solution.py:476
  2.8 54.0 %collective-permute-start.2 = (bf16[384,3072]{1,0:T(8,128)(2,1)}, bf16[384,3072]{1,0:T(8,128)(2,1)}, u32[]{:S(2)}, u32[]{:S(2)}) collective-permute-start(bf16[384,3072]{1,0:T(8,128)(2,1)} %bitcast.28.refs_0_), channel_id=1, source_target_pairs={{0,2},{1,3},{2,4},{3,5},{4,6},{5,7},{6,0},{7,1},{8,10},{9,11},{10,... | collective-permute-start | bytes 7077896 | tf_op jit(solution)/shard_map/ppermute | solution.py:476
  3.5 54.7 %collective-permute-start.3 = (bf16[384,3072]{1,0:T(8,128)(2,1)}, bf16[384,3072]{1,0:T(8,128)(2,1)}, u32[]{:S(2)}, u32[]{:S(2)}) collective-permute-start(bf16[384,3072]{1,0:T(8,128)(2,1)} %bitcast.28.refs_0_), channel_id=1, source_target_pairs={{0,6},{1,7},{2,0},{3,1},{4,2},{5,3},{6,4},{7,5},{8,14},{9,15},{10,... | collective-permute-start | bytes 7077896 | tf_op jit(solution)/shard_map/ppermute | solution.py:476
  58.1 100.3 %collective-permute-start.4 = (bf16[192,3072]{1,0:T(8,128)(2,1)S(1)}, bf16[192,3072]{1,0:T(8,128)(2,1)}, u32[]{:S(2)}, u32[]{:S(2)}) collective-permute-start(bf16[192,3072]{1,0:T(8,128)(2,1)S(1)} %slice.12), channel_id=1, source_target_pairs={{0,2},{1,3},{2,4},{3,5},{4,6},{5,7},{6,0},{7,1},{8,10},{9,11},{10,... | collective-permute-start | bytes 3538952 | tf_op jit(solution)/shard_map/ppermute | solution.py:476
  59.6 99.2 %collective-permute-start.5 = (bf16[192,3072]{1,0:T(8,128)(2,1)S(1)}, bf16[192,3072]{1,0:T(8,128)(2,1)}, u32[]{:S(2)}, u32[]{:S(2)}) collective-permute-start(bf16[192,3072]{1,0:T(8,128)(2,1)S(1)} %slice.13), channel_id=1, source_target_pairs={{0,6},{1,7},{2,0},{3,1},{4,2},{5,3},{6,4},{7,5},{8,14},{9,15},{10,... | collective-permute-start | bytes 3538952 | tf_op jit(solution)/shard_map/ppermute | solution.py:476
  62.3 280.2 %collective-permute-start.6 = (bf16[384,3072]{1,0:T(8,128)(2,1)}, bf16[384,3072]{1,0:T(8,128)(2,1)}, u32[]{:S(2)}, u32[]{:S(2)}) collective-permute-start(bf16[384,3072]{1,0:T(8,128)(2,1)} %bitcast.28.refs_0_), channel_id=1, source_target_pairs={{0,1},{1,0},{2,3},{3,2},{4,5},{5,4},{6,7},{7,6},{8,9},{9,8},{10,11... | collective-permute-start | bytes 7077896 | tf_op jit(solution)/shard_map/ppermute | solution.py:476
  63.9 34.0 %copy-start.3 = (f32[1152,1]{0,1:T(1,128)}, f32[1152,1]{0,1:T(1,128)S(1)}, u32[]{:S(2)}) copy-start(f32[1152,1]{0,1:T(1,128)S(1)} %reshape.150) | copy-start | bytes 13828
  63.9 94.3 %collective-permute-start.1 = (f32[1152,1]{0,1:T(1,128)S(1)}, f32[1152,1]{0,1:T(1,128)S(1)}, u32[]{:S(2)}, u32[]{:S(2)}) collective-permute-start(f32[1152,1]{0,1:T(1,128)S(1)} %reshape.150), channel_id=1, source_target_pairs={{0,1},{1,0},{2,3},{3,2},{4,5},{5,4},{6,7},{7,6},{8,9},{9,8},{10,11... | collective-permute-start | bytes 13832 | tf_op jit(solution)/shard_map/ppermute | solution.py:476
  158.2 184.3 %collective-permute-start.7 = (bf16[384,3072]{1,0:T(8,128)(2,1)}, bf16[384,3072]{1,0:T(8,128)(2,1)}, u32[]{:S(2)}, u32[]{:S(2)}) collective-permute-start(bf16[384,3072]{1,0:T(8,128)(2,1)} %collective-permute-done.2.refs_1_), channel_id=1, source_target_pairs={{0,1},{1,0},{2,3},{3,2},{4,5},{5,4},{6,7},{7,6},{8,9},{9,8},{10,11... | collective-permute-start | bytes 7077896 | tf_op jit(solution)/shard_map/ppermute | solution.py:476
  158.5 184.1 %collective-permute-start.8 = (bf16[384,3072]{1,0:T(8,128)(2,1)}, bf16[384,3072]{1,0:T(8,128)(2,1)}, u32[]{:S(2)}, u32[]{:S(2)}) collective-permute-start(bf16[384,3072]{1,0:T(8,128)(2,1)} %collective-permute-done.3.refs_2_), channel_id=1, source_target_pairs={{0,1},{1,0},{2,3},{3,2},{4,5},{5,4},{6,7},{7,6},{8,9},{9,8},{10,11... | collective-permute-start | bytes 7077896 | tf_op jit(solution)/shard_map/ppermute | solution.py:476
  158.8 183.7 %collective-permute-start.9 = (bf16[192,3072]{1,0:T(8,128)(2,1)}, bf16[192,3072]{1,0:T(8,128)(2,1)}, u32[]{:S(2)}, u32[]{:S(2)}) collective-permute-start(bf16[192,3072]{1,0:T(8,128)(2,1)} %collective-permute-done.4.refs_3_), channel_id=1, source_target_pairs={{0,1},{1,0},{2,3},{3,2},{4,5},{5,4},{6,7},{7,6},{8,9},{9,8},{10,11... | collective-permute-start | bytes 3538952 | tf_op jit(solution)/shard_map/ppermute | solution.py:476
  159.0 183.6 %collective-permute-start.10 = (bf16[192,3072]{1,0:T(8,128)(2,1)}, bf16[192,3072]{1,0:T(8,128)(2,1)}, u32[]{:S(2)}, u32[]{:S(2)}) collective-permute-start(bf16[192,3072]{1,0:T(8,128)(2,1)} %collective-permute-done.5.refs_4_), channel_id=1, source_target_pairs={{0,1},{1,0},{2,3},{3,2},{4,5},{5,4},{6,7},{7,6},{8,9},{9,8},{10,11... | collective-permute-start | bytes 3538952 | tf_op jit(solution)/shard_map/ppermute | solution.py:476
  159.3 0.7 copy-start.4
  162.9 89.0 %copy-start.1 = (s32[10]{0:T(128)S(1)}, s32[10]{0:T(128)}, u32[]{:S(2)}) copy-start(s32[10]{0:T(128)} %stack.43.meta) | copy-start | bytes 124
  300.9 1.7 copy-start

commit v2 on v1

--- a/solution.py
+++ b/solution.py
@@ -279,124 +279,220 @@
 EPS = 1e-5
 
 
-def project_kernel(cap, span, tb, seq, blk, nsteps, meta, code, u_ref, pos_ref, own_pos_ref, gain_ref, bias_ref, wa_ref, wb_ref, ba_ref, bb_ref,
-                   qkv_ref, emb_ref, xs, hs):
+def project_kernel(tb, seq, blk, steps, chunk, meta, code, u_hbm, pos_hbm, gain_ref, bias_ref, wa_hbm, wb_hbm, ba_ref, bb_ref,
+                   qkv_ref, emb_ref, u, w, pos, xs, hs, usem, wsem, psem):
     step = pl.program_id(0)
-    T = u_ref.shape[1]
-    D = T * 128
-    inv = 1.0 / D
-
-    def fetch(base, t16):
+    T = u.shape[1]
+    M = wa_hbm.shape[0]
+    inv = 1.0 / (T * 128)
+    base = meta[1] * seq
+
+    def load_u():
+        return pltpu.make_async_copy(u_hbm, u, usem)
+    def load_w(k):
+        return pltpu.make_async_copy((wa_hbm, wb_hbm)[k], w.at[pl.ds(k * M, M)], wsem.at[k])
+    def load_pos(i):
+        return pltpu.make_async_copy(pos_hbm.at[pl.ds(i * tb, tb)], pos.at[lax.rem(i, 2)], psem.at[lax.rem(i, 2)])
+    def load_own():
+        return pltpu.make_async_copy(pos_hbm.at[pl.ds(meta[0] * blk, blk)], pos.at[steps % 2, pl.ds(0, blk)], psem.at[steps % 2])
+
+    def fetch(slot, first):
+        for r in range(8):
+            xs[slot, pl.ds(r, T, stride=8), :] = u[code[first + r]].astype(jnp.float32)
+
+    def tile(slot, j):
+        return xs[slot, j * 8:(j + 1) * 8, :]
+
+    def lanes(j):
+        return slice(j * 128, (j + 1) * 128)
+
+    def norm(i, g, lane_slot):
+        t = pl.multiple_of(g * 16, 16)
+        out = []
         for half in range(2):
-            for r in range(8):
-                c = code[base + t16 * 16 + half * 8 + r]
-                at = lax.div(c, span) * cap + lax.rem(c, span)
-                xs[half, pl.ds(r, T, stride=8), :] = u_ref[at].astype(jnp.float32)
-
-    def embed(half, p):
-        return [(xs[half, j * 8:(j + 1) * 8, :] + p[half * 8:half * 8 + 8, j * 128:(j + 1) * 128].astype(jnp.float32)).astype(jnp.bfloat16) for j in range(T)]
-
-    @pl.when(step < nsteps)
+            slot = lane_slot * 2 + half
+            fetch(slot, base + i * tb + g * 16 + half * 8)
+            p = pos.at[lax.rem(i, 2), pl.ds(t, 16), :]
+            s = None
+            for j in range(T):
+                e = (tile(slot, j) + p[half * 8:half * 8 + 8, lanes(j)].astype(jnp.float32)).astype(jnp.bfloat16).astype(jnp.float32)
+                xs[slot, j * 8:(j + 1) * 8, :] = e
+                s = e if s is None else s + e
+            mean = jnp.broadcast_to(jnp.sum(s, axis=1, keepdims=True) * inv, (8, 128))
+            s = None
+            for j in range(T):
+                c = tile(slot, j) - mean
+                s = c * c if s is None else s + c * c
+            var = jnp.sum(s, axis=1, keepdims=True) * inv
+            rs = jnp.broadcast_to(lax.rsqrt(var + EPS), (8, 128))
+            out.append((slot, mean, rs))
+        for j in range(T):
+            y = [(tile(slot, j) - mean) * rs * gain_ref[:, lanes(j)] + bias_ref[:, lanes(j)] for slot, mean, rs in out]
+            hs[lax.rem(i, 2), pl.ds(t, 16), lanes(j)] = jnp.concatenate(y, axis=0).astype(jnp.bfloat16)
+
+    def embed(g, lane_slot):
+        per = blk // 16
+        b = lax.div(g, per)
+        t = pl.multiple_of(lax.rem(g, per) * 16, 16)
+        for half in range(2):
+            fetch(lane_slot * 2 + half, b * seq + meta[0] * blk + t + half * 8)
+        p = pos.at[steps % 2, pl.ds(t, 16), :]
+        for j in range(T):
+            e = jnp.concatenate([tile(lane_slot * 2, j), tile(lane_slot * 2 + 1, j)], axis=0) + p[:, lanes(j)].astype(jnp.float32)
+            emb_ref[b, pl.ds(t, 16), lanes(j)] = e.astype(jnp.bfloat16)
+
+    @pl.when(step == 0)
     def _():
-        base = meta[1] * seq + step * tb
-        @pl.loop(0, tb // 16)
+        load_u().start()
+        load_pos(0).start()
+        for k in range(2):
+            load_w(k).start()
+        load_pos(1).start()
+        load_u().wait()
+        load_pos(0).wait()
+        @pl.loop(0, tb // 64)
         def _(g):
-            fetch(base, g)
-            t = pl.multiple_of(g * 16, 16)
-            p = pos_ref.at[pl.ds(t, 16), :]
-            out = []
-            for half in range(2):
-                e = [v.astype(jnp.float32) for v in embed(half, p)]
-                s = e[0]
-                for j in range(1, T):
-                    s = s + e[j]
-                mean = jnp.sum(s, axis=1, keepdims=True) * inv
-                mb = jnp.broadcast_to(mean, (8, 128))
-                e = [v - mb for v in e]
-                s = e[0] * e[0]
-                for j in range(1, T):
-                    s = s + e[j] * e[j]
-                var = jnp.sum(s, axis=1, keepdims=True) * inv
-                rs = jnp.broadcast_to(lax.rsqrt(var + EPS), (8, 128))
-                out.append([e[j] * rs * gain_ref[:, j * 128:(j + 1) * 128] + bias_ref[:, j * 128:(j + 1) * 128] for j in range(T)])
-            for j in range(T):
-                hs[pl.ds(t, 16), j * 128:(j + 1) * 128] = jnp.concatenate([out[0][j], out[1][j]], axis=0).astype(jnp.bfloat16)
-        M = 384
-        for k, (w, b) in enumerate(((wa_ref, ba_ref), (wb_ref, bb_ref))):
-            for m in range(0, w.shape[0], M):
-                o = lax.dot_general(w[m:m + M, :], hs[...], (((1,), (1,)), ((), ())), preferred_element_type=jnp.float32)
-                qkv_ref[k, m:m + M, :] = (o + b[m:m + M, :]).astype(jnp.bfloat16)
-
-    @pl.when(step == nsteps)
+            for j in range(4):
+                norm(0, g * 4 + j, j)
+        for k in range(2):
+            load_w(k).wait()
+
+    def sweep(beside):
+        per = M // chunk
+        h = hs.at[lax.rem(step, 2)]
+        for k, b in enumerate((ba_ref, bb_ref)):
+            @pl.loop(0, per)
+            def _(m):
+                at = pl.multiple_of(m * chunk, 32)
+                o = lax.dot_general(w[pl.ds(k * M + at, chunk), :], h[...], (((1,), (1,)), ((), ())), preferred_element_type=jnp.float32)
+                qkv_ref[k, pl.ds(at, chunk), :] = (o + b[pl.ds(at, chunk), :]).astype(jnp.bfloat16)
+                n = tb // 16 // (2 * per)
+                for j in range(n):
+                    beside((k * per + m) * n + j, j)
+
+    @pl.when(step < steps - 1)
     def _():
-        for b in range(2):
-            base = b * seq + meta[0] * blk
-            @pl.loop(0, blk // 16)
-            def _(g):
-                fetch(base, g)
-                t = pl.multiple_of(g * 16, 16)
-                p = own_pos_ref.at[pl.ds(t, 16), :]
-                e0, e1 = embed(0, p), embed(1, p)
-                for j in range(T):
-                    emb_ref[b, pl.ds(t, 16), j * 128:(j + 1) * 128] = jnp.concatenate([e0[j], e1[j]], axis=0)
-
-
-def project(n, cap, span, meta, code, u, pos, gain, bias, wa, wb, ba, bb, tb=512):
+        load_pos(step + 1).wait()
+        @pl.when(step + 2 < steps)
+        def _():
+            load_pos(step + 2).start()
+        @pl.when(step + 2 == steps)
+        def _():
+            load_own().start()
+        sweep(lambda g, j: norm(step + 1, g, j))
+
+    @pl.when(step == steps - 1)
+    def _():
+        load_own().wait()
+        sweep(embed)
+
+
+def project(n, meta, code, u, pos, gain, bias, wa, wb, ba, bb, tb=512, chunk=288):
     seq, D = pos.shape
     blk = seq // n
-    nsteps = seq // tb
+    steps = seq // tb
     M = wa.shape[0]
-    last = nsteps - 1
+    A = pl.BlockSpec(memory_space=pl.ANY)
     one = lambda shape: pl.BlockSpec(shape, lambda i, *_: (0,) * len(shape), pipeline_mode=pl.Buffered(1))
     return pl.pallas_call(
-        functools.partial(project_kernel, cap, span, tb, seq, blk, nsteps),
+        functools.partial(project_kernel, tb, seq, blk, steps, chunk),
         out_shape=(jax.ShapeDtypeStruct((2, M, seq), jnp.bfloat16), jax.ShapeDtypeStruct((2, blk, D), jnp.bfloat16)),
         grid_spec=pltpu.PrefetchScalarGridSpec(
-            num_scalar_prefetch=2, grid=(nsteps + 1,),
-            in_specs=[one(u.shape),
-                      pl.BlockSpec((tb, D), lambda i, *_: (jnp.minimum(i, last), 0)),
-                      pl.BlockSpec((blk, D), lambda i, meta, code: (meta[0], 0), pipeline_mode=pl.Buffered(1)),
-                      one((1, D)), one((1, D)), one(wa.shape), one(wb.shape), one(ba.shape), one(bb.shape)],
-            out_specs=(pl.BlockSpec((2, M, tb), lambda i, *_: (0, 0, jnp.minimum(i, last))), pl.BlockSpec((2, blk, D), lambda i, *_: (0, 0, 0), pipeline_mode=pl.Buffered(1))),
-            scratch_shapes=[pltpu.VMEM((2, D // 128 * 8, 128), jnp.float32), pltpu.VMEM((tb, D), jnp.bfloat16)]),
-        compiler_params=pltpu.CompilerParams(vmem_limit_bytes=60 * 2**20),
+            num_scalar_prefetch=2, grid=(steps,),
+            in_specs=[A, A, one((1, D)), one((1, D)), A, A, one(ba.shape), one(bb.shape)],
+            out_specs=(pl.BlockSpec((2, M, tb), lambda i, *_: (0, 0, i)), pl.BlockSpec((2, blk, D), lambda i, *_: (0, 0, 0), pipeline_mode=pl.Buffered(1))),
+            scratch_shapes=[pltpu.VMEM(u.shape, u.dtype), pltpu.VMEM((2 * M, D), wa.dtype), pltpu.VMEM((2, tb, D), pos.dtype),
+                            pltpu.VMEM((8, D // 128 * 8, 128), jnp.float32), pltpu.VMEM((2, tb, D), jnp.bfloat16),
+                            pltpu.SemaphoreType.DMA, pltpu.SemaphoreType.DMA((2,)), pltpu.SemaphoreType.DMA((2,))]),
+        compiler_params=pltpu.CompilerParams(vmem_limit_bytes=63 * 2**20),
         name="project",
-    )(meta, code, u, pos, pos, gain, bias, wa, wb, ba, bb)
-
-
-def attention_kernel(scale, qb, meta, qkv_ref, out_ref, kk, vv, sc):
+    )(meta, code, u, pos, gain, bias, wa, wb, ba, bb)
+
+
+def attention_kernel(n, scale, qb, qkv_ref, out_ref, kk, vv, sc, ctx, loc_sem, send_sem, recv_sem):
     E, S = qkv_ref.shape[3:]
+    H = out_ref.shape[2]
+    N = S // qb
     c = scale * 1.4426950408889634
+    me = lax.axis_index("tp")
+    core = lax.rem(me, 2)
+    k_id, h_id = pl.program_id(0), pl.program_id(1)
+    head = lax.rem(k_id + core, 2) * H + h_id
+    first = (k_id == 0) & (h_id == 0)
+    last = (k_id == 1) & (h_id == H - 1)
+
+    @pl.when(first)
+    def _():
+        barrier = pltpu.get_barrier_semaphore()
+        for s in range(1, n):
+            pl.semaphore_signal(barrier, inc=1, device_id={"tp": lax.rem(me + s, n)}, device_id_type=MESH)
+        pl.semaphore_wait(barrier, n - 1)
+        vv[E:, :] = jnp.where(lax.broadcasted_iota(jnp.int32, (vv.shape[0] - E, S), 0) == 0, 1.0, 0.0).astype(jnp.bfloat16)
+
+    def send(s):
+        to = lax.rem(me + s, n)
+        return pltpu.make_async_remote_copy(src_ref=ctx.at[head, to], dst_ref=out_ref.at[me, lax.div(head, H), lax.rem(head, H)],
+                                            send_sem=send_sem.at[s], recv_sem=recv_sem.at[s], device_id={"tp": to}, device_id_type=MESH)
+
     for t in range(0, S, 128):
         kk[t:t + 128, :] = qkv_ref[0, 1, 0, :, t:t + 128].astype(jnp.float32).T.astype(jnp.bfloat16)
     vv[0:E, :] = qkv_ref[0, 2, 0]
-    vv[E:, :] = jnp.where(lax.broadcasted_iota(jnp.int32, (vv.shape[0] - E, S), 0) == 0, 1.0, 0.0).astype(jnp.bfloat16)
     keep = lax.broadcasted_iota(jnp.int32, (qb, qb), 0) <= lax.broadcasted_iota(jnp.int32, (qb, qb), 1)
-    for i in range(S // qb):
-        n = (i + 1) * qb
-        q = qkv_ref[0, 0, 0, :, i * qb:n]
-        s = jnp.dot(kk[0:n, :], q, preferred_element_type=jnp.float32)
-        d = jnp.where(keep, s[n - qb:n], -jnp.inf)
-        s = d if i == 0 else jnp.concatenate([s[:n - qb], d], axis=0)
-        m = jnp.max(s, axis=0, keepdims=True) * c
-        p = jnp.exp2(s * c - m).astype(jnp.bfloat16)
-        o = jnp.dot(vv[:, 0:n], p, preferred_element_type=jnp.float32)
-        out_ref[i, 0, 0] = (o[0:E] * (1.0 / o[E:E + 1])).astype(jnp.bfloat16)
-
-
-def attention(n, meta, qkv, qb=256):
+
+    def scores(i, k, m):
+        s = jnp.dot(kk[k * qb:(k + 1) * qb, :], qkv_ref[0, 0, 0, :, i * qb:(i + 1) * qb], preferred_element_type=jnp.float32)
+        if k == i:
+            s = jnp.where(keep, s, -jnp.inf)
+        sc[i % 2, k * qb:(k + 1) * qb, :] = s
+        top = jnp.max(s.reshape(qb // 8, 8, qb), axis=0)
+        return top if m is None else jnp.maximum(m, top)
+
+    def weigh(i, k, mc, o):
+        s = sc[i % 2, k * qb:(k + 1) * qb, :]
+        p = jnp.exp2(s * c - mc).astype(jnp.bfloat16)
+        d = jnp.dot(vv[:, k * qb:(k + 1) * qb], p, preferred_element_type=jnp.float32)
+        return d if o is None else o + d
+
+    m = scores(0, 0, None)
+    for i in range(N):
+        mc = jnp.max(m, axis=0, keepdims=True) * c
+        o = m = None
+        for k in range(i + 2):
+            if i + 1 < N:
+                m = scores(i + 1, k, m)
+            if k <= i:
+                o = weigh(i, k, mc, o)
+        ctx[head, i] = (o[0:E] * (1.0 / o[E:E + 1])).astype(jnp.bfloat16)
+
+    for s in range(1, n):
+        send(s).start()
+    local = pltpu.make_async_copy(ctx.at[head, me], out_ref.at[me, lax.div(head, H), lax.rem(head, H)], loc_sem)
+    local.start()
+    local.wait()
+
+    @pl.when(last)
+    def _():
+        for s in range(1, n):
+            fr = lax.rem(me - s + n, n)
+            r = out_ref.at[fr]
+            got = pltpu.make_async_remote_copy(src_ref=r, dst_ref=r, send_sem=send_sem.at[s], recv_sem=recv_sem.at[s], device_id={"tp": fr}, device_id_type=MESH)
+            got.wait_recv()
+            got.wait_send()
+
+
+def attention(n, qkv, cid=1, qb=256):
     _, _, H, E, S = qkv.shape
     return pl.pallas_call(
-        functools.partial(attention_kernel, E ** -0.5, qb),
+        functools.partial(attention_kernel, n, E ** -0.5, qb),
         out_shape=jax.ShapeDtypeStruct((n, 2, H, E, S // n), jnp.bfloat16),
-        grid_spec=pltpu.PrefetchScalarGridSpec(
-            num_scalar_prefetch=1, grid=(2, H),
-            in_specs=[pl.BlockSpec((1, 3, 1, E, S), lambda k, h, meta: (k, 0, h, 0, 0))],
-            out_specs=pl.BlockSpec((n, 1, 1, E, S // n), lambda k, h, meta: (0, lax.rem(meta[1] + k, 2), h, 0, 0)),
-            scratch_shapes=[pltpu.VMEM((S, E), jnp.bfloat16), pltpu.VMEM((E + 16, S), jnp.bfloat16), pltpu.VMEM((S, qb), jnp.float32)]),
-        compiler_params=pltpu.CompilerParams(vmem_limit_bytes=48 * 2**20),
+        grid=(2, H),
+        in_specs=[pl.BlockSpec((1, 3, 1, E, S), lambda k, h: (k, 0, h, 0, 0))],
+        out_specs=pl.BlockSpec(memory_space=pl.ANY),
+        scratch_shapes=[pltpu.VMEM((S, E), jnp.bfloat16), pltpu.VMEM((E + 16, S), jnp.bfloat16), pltpu.VMEM((2, S, qb), jnp.float32),
+                        pltpu.VMEM((2 * H, n, E, qb), jnp.bfloat16), pltpu.SemaphoreType.DMA, pltpu.SemaphoreType.DMA((n,)), pltpu.SemaphoreType.DMA((n,))],
+        compiler_params=pltpu.CompilerParams(collective_id=cid, has_side_effects=True, vmem_limit_bytes=48 * 2**20),
         name="attention",
-    )(meta, qkv)
+    )(qkv)
 
 
 def output_kernel(n, nb, owners, lows, meta, ctx_ref, emb_ref, bias_ref, *refs):
@@ -492,9 +588,9 @@
         pieces = [v_own, v_minus, v_plus, v_opp_a, v_opp_b]
         pieces = pieces + [permute(p, swap) for p in pieces]
         owners, lows = [0, 3, 4, 5, 5, 6, 7, 8, 9, 9], [0, 0, 0, 0, half] * 2
-        at = lambda c, k: lax.rem(c + chips, chips) * 2 + k
+        place_of = lambda c, k: lax.rem(c + chips, chips) * 2 + k
         chip = me // 2
-        meta = [me, core, chip] + [at(chip + s, k) for k in (core, 1 - core) for s in (-1, 1, 2)]
+        meta = [me, core, chip] + [place_of(chip + s, k) for k in (core, 1 - core) for s in (-1, 1, 2)]
         meta = meta[:6] + [me + 1 - 2 * core] + meta[6:]
         meta = jnp.stack(meta).astype(jnp.int32)
 
@@ -525,11 +621,10 @@
         _, u = lax.while_loop(lambda c: c[0] < rounds, more, (jnp.int32(0), u))
         t = jnp.arange(code.size, dtype=jnp.int32)
         t = jnp.where(t // seq == core, t % seq, jnp.clip(t % seq - me * blk, 0, blk - 1) + seq)
-        code = jnp.where(rounds > 0, t // CAP * SPAN + t % CAP, code)
-
-        qkv, embed = project(n, CAP, SPAN, meta, code, u, pos_table, ln_gain[None], ln_bias[None], w_own, w_par, b_own, b_par)
-        ctx = attention(n, meta, qkv.reshape(2, 3, H, E, seq))
-        ctx = exchange(n, ctx.reshape(n, 2 * H * E, seq // n))
+        at = jnp.where(rounds > 0, t, code // SPAN * CAP + jnp.minimum(code % SPAN, CAP - 1))
+
+        qkv, embed = project(n, meta, at, u, pos_table, ln_gain[None], ln_bias[None], w_own, w_par, b_own, b_par)
+        ctx = attention(n, qkv.reshape(2, 3, H, E, seq)).reshape(n, 2 * H * E, seq // n)
         resid_out = output(n, meta, ctx, embed, b_out[None], pieces, owners, lows)
         return resid_out, embed
 

time: 363 us -> 289 us (0.80)
  Pallas kernels: 288 us -> 215 us
    pallas_call x3 -> x2, Pallas kernels: 178 us -> 105 us  [the longest x1 61.5 us: project(): pl.pallas_call(functools.partial(project_kernel, tb, seq, blk, steps, chu...]
  transfers between devices with their start and end apart: 11 -> 11, of which waited for: 1 -> 1; matrix products, arithmetic and copies ran while one was open for 2% -> 2% of each run, Pallas kernels for 75% -> 68%
where the time goes in v2:
time: 289 us; the launch traced here: 288 us
  Pallas kernels  215 us (74%)
  waiting for transfers between devices  51.4 us (18%)
  starting transfers between devices  10.3 us (4%)
  local copies, waits for them, and re-layouts  8.59 us (3%)
    pallas_call x1, Pallas kernels, project(): pl.pallas_call(functools.partial(project_kernel, tb, seq, blk, steps, chu...  61.5 us
    pallas_call x1, Pallas kernels, gather_all(): pl.pallas_call(functools.partial(gather_all_kernel, n, S), out_shape=jax....  60.3 us
    ppermute x11, waiting for transfers between devices, solution(): permute = lambda x, perm: lax.ppermute(x, 'tp', perm)  51.4 us
    pallas_call x1, Pallas kernels, attention(): pl.pallas_call(functools.partial(attention_kernel, n, E ** (-0.5), qb), o...  43.5 us
    pallas_call x1, Pallas kernels, index(): pl.pallas_call(functools.partial(index_kernel, n, shard_rows, cap), out_s...  18.5 us
    pallas_call x1, Pallas kernels, output(): pl.pallas_call(functools.partial(output_kernel, n, nb, owners, lows), out...  18.4 us
    pallas_call x1, Pallas kernels, rows(): pl.pallas_call(functools.partial(rows_kernel, cap, nb), out_shape=jax.Sha...  12.9 us
    ppermute x11, starting transfers between devices, solution(): permute = lambda x, perm: lax.ppermute(x, 'tp', perm)  10.3 us
  transfers between devices with their start and end apart: 11, of which 1 were waited for; matrix products, arithmetic and copies ran while one was open for 2% of the time, Pallas kernels for 68%

profile of v2, /device:TPU:81, one launch (start us, length us, event | category | flops | bytes accessed | tf_op | source)
XLA Modules:
  0.0 288.2 jit_solution(8787789348273079056)
XLA Ops:
  0.6 0.0 copy-start.4
  0.6 0.0 copy-start.1
  0.6 2.1 collective-permute-start
  2.8 0.8 collective-permute-start.2
  3.5 1.9 collective-permute-start.3
  5.5 51.3 %collective-permute-done.2.refs_1_ = bf16[384,3072]{1,0:T(8,128)(2,1)} collective-permute-done((bf16[384,3072]{1,0:T(8,128)(2,1)}, bf16[384,3072]{1,0:T(8,128)(2,1)}, u32[]{:S(2)}, u32[]{:S(2)}) %collective-permute-start.2) | collective-permute-done | bytes 2359328 | tf_op jit(solution)/shard_map/ppermute | solution.py:572
  56.8 1.3 slice.12
  58.1 0.1 collective-permute-start.4
  58.2 0.0 collective-permute-done.3.refs_2_
  58.3 1.3 slice.13
  59.6 2.7 collective-permute-start.5
  62.3 1.4 collective-permute-start.6
  63.8 0.0 copy-done.4
  63.8 0.1 reshape.150
  63.9 0.0 copy-start.2
  63.9 0.1 collective-permute-start.1
  64.0 0.0 copy-done.1
  64.0 0.6 reshape.146.ids_ref
  64.6 18.5 %index.1 = (s32[32,128]{1,0:T(8,128)S(1)}, s32[3,128]{1,0:T(4,128)}, s32[1,128]{1,0:T(1,128)}) custom-call(s32[32,128]{1,0:T(8,128)} %reshape.146.ids_ref), custom_call_target="tpu_custom_call" | custom-call | tf_op jit(solution)/shard_map/index/pallas_call | solution.py:230
  84.5 0.6 bitcast_negate_fusion
  85.1 12.9 %rows.2.src_ref = bf16[264,24,128]{2,1,0:T(8,128)(2,1)} custom-call(s32[384]{0:T(512)} %bitcast.65, bf16[6400,3072]{1,0:T(8,128)(2,1)} %table_ref.1), custom_call_target="tpu_custom_call" | custom-call | tf_op jit(solution)/shard_map/rows/pallas_call | solution.py:267
  98.0 0.0 copy-done.2
  98.0 60.3 %gather_all.2 = bf16[2304,24,128]{2,1,0:T(8,128)(2,1)} custom-call(bf16[264,24,128]{2,1,0:T(8,128)(2,1)} %rows.2.src_ref), custom_call_target="tpu_custom_call" | custom-call | tf_op jit(solution)/shard_map/gather_all/pallas_call | solution.py:87
  158.4 0.0 collective-permute-done.1
  158.4 0.2 collective-permute-start.7
  158.7 0.0 collective-permute-done.4.refs_3_
  158.7 0.4 collective-permute-start.8
  159.0 0.0 collective-permute-done.5.refs_4_
  159.0 0.1 collective-permute-start.9
  159.2 0.0 collective-permute-done.wb_hbm
  159.2 0.4 collective-permute-start.10
  159.5 0.0 copy-start.3
  159.5 0.7 copy-done.3
  160.2 1.1 copy.16.ba_ref
  161.3 0.7 stack.43.meta
  162.0 1.1 copy.17.bb_ref
  163.0 61.5 %project.1 = (bf16[2,1152,2048]{2,1,0:T(8,128)(2,1)}, bf16[2,256,3072]{2,1,0:T(8,128)(2,1)}) custom-call(s32[10]{0:T(128)} %stack.43.meta, s32[4096]{0:T(1024)} %get-tuple-element.348.code, bf16[2304,24,128]{2,1,0:T(8,128)(2,1)} %get-tuple-element.312.u_hbm, bf16[2048,3072]{1,0:T(8,128)(2,1)} %pos_hbm.1, f32[1,3072]{1,0:T(1,128)} %bitcast.63, ...), custom_call_target="tpu_custom_call" | custom-call | tf_op jit(solution)/shard_map/project/pallas_call | solution.py:397
  224.5 43.5 %attention.1 = bf16[8,2,4,96,256]{4,3,2,1,0:T(8,128)(2,1)S(1)} custom-call(bf16[2,3,4,96,2048]{4,3,2,1,0:T(8,128)(2,1)} %bitcast.51), custom_call_target="tpu_custom_call" | custom-call | tf_op jit(solution)/shard_map/attention/pallas_call | solution.py:485
  268.0 0.0 copy-start
  268.0 1.6 copy-done
  269.6 0.0 collective-permute-done.6.refs_5_
  269.6 0.0 collective-permute-done.7.refs_6_
  269.6 0.0 collective-permute-done.8.refs_7_
  269.6 0.0 collective-permute-done.9.refs_8_
  269.6 0.0 collective-permute-done.10.refs_9_
  269.6 18.4 %output.1 = bf16[2,256,3072]{2,1,0:T(8,128)(2,1)} custom-call(s32[10]{0:T(128)} %stack.43.meta, bf16[8,768,256]{2,1,0:T(8,128)(2,1)} %bitcast.50, bf16[2,256,3072]{2,1,0:T(8,128)(2,1)} %get-tuple-element.308.emb_ref, f32[1,3072]{1,0:T(1,128)} %bitcast.62, bf16[384,3072]{1,0:T(8,128)(2,1)} %bitcast.28.refs_0_, ...), custom_call_target="tpu_custom_call" | custom-call | tf_op jit(solution)/shard_map/output/pallas_call | solution.py:525
  (5 shorter events, 0.0 us)
Async XLA Ops:
  0.6 63.1 %copy-start.4 = (f32[3,4,96]{2,1,0:T(4,128)S(1)}, f32[3,4,96]{2,1,0:T(4,128)}, u32[]{:S(2)}) copy-start(f32[3,4,96]{2,1,0:T(4,128)} %param.17) | copy-start | bytes 13828
  0.6 63.4 %copy-start.1 = (s32[2,2048]{1,0:T(2,128)S(1)}, s32[2,2048]{1,0:T(2,128)}, u32[]{:S(2)}) copy-start(s32[2,2048]{1,0:T(2,128)} %param.11) | copy-start | bytes 49156
  0.6 158.5 %collective-permute-start = (bf16[1152,3072]{1,0:T(8,128)(2,1)}, bf16[1152,3072]{1,0:T(8,128)(2,1)}, u32[]{:S(2)}, u32[]{:S(2)}) collective-permute-start(bf16[1152,3072]{1,0:T(8,128)(2,1)} %bitcast.52), channel_id=1, source_target_pairs={{0,1},{1,0},{2,3},{3,2},{4,5},{5,4},{6,7},{7,6},{8,9},{9,8},{10,11... | collective-permute-start | bytes 21233672 | tf_op jit(solution)/shard_map/ppermute | solution.py:572
  2.8 54.0 %collective-permute-start.2 = (bf16[384,3072]{1,0:T(8,128)(2,1)}, bf16[384,3072]{1,0:T(8,128)(2,1)}, u32[]{:S(2)}, u32[]{:S(2)}) collective-permute-start(bf16[384,3072]{1,0:T(8,128)(2,1)} %bitcast.28.refs_0_), channel_id=1, source_target_pairs={{0,2},{1,3},{2,4},{3,5},{4,6},{5,7},{6,0},{7,1},{8,10},{9,11},{10,... | collective-permute-start | bytes 7077896 | tf_op jit(solution)/shard_map/ppermute | solution.py:572
  3.5 54.7 %collective-permute-start.3 = (bf16[384,3072]{1,0:T(8,128)(2,1)}, bf16[384,3072]{1,0:T(8,128)(2,1)}, u32[]{:S(2)}, u32[]{:S(2)}) collective-permute-start(bf16[384,3072]{1,0:T(8,128)(2,1)} %bitcast.28.refs_0_), channel_id=1, source_target_pairs={{0,6},{1,7},{2,0},{3,1},{4,2},{5,3},{6,4},{7,5},{8,14},{9,15},{10,... | collective-permute-start | bytes 7077896 | tf_op jit(solution)/shard_map/ppermute | solution.py:572
  58.1 100.5 %collective-permute-start.4 = (bf16[192,3072]{1,0:T(8,128)(2,1)S(1)}, bf16[192,3072]{1,0:T(8,128)(2,1)}, u32[]{:S(2)}, u32[]{:S(2)}) collective-permute-start(bf16[192,3072]{1,0:T(8,128)(2,1)S(1)} %slice.12), channel_id=1, source_target_pairs={{0,2},{1,3},{2,4},{3,5},{4,6},{5,7},{6,0},{7,1},{8,10},{9,11},{10,... | collective-permute-start | bytes 3538952 | tf_op jit(solution)/shard_map/ppermute | solution.py:572
  59.6 99.4 %collective-permute-start.5 = (bf16[192,3072]{1,0:T(8,128)(2,1)S(1)}, bf16[192,3072]{1,0:T(8,128)(2,1)}, u32[]{:S(2)}, u32[]{:S(2)}) collective-permute-start(bf16[192,3072]{1,0:T(8,128)(2,1)S(1)} %slice.13), channel_id=1, source_target_pairs={{0,6},{1,7},{2,0},{3,1},{4,2},{5,3},{6,4},{7,5},{8,14},{9,15},{10,... | collective-permute-start | bytes 3538952 | tf_op jit(solution)/shard_map/ppermute | solution.py:572
  62.3 207.3 %collective-permute-start.6 = (bf16[384,3072]{1,0:T(8,128)(2,1)}, bf16[384,3072]{1,0:T(8,128)(2,1)}, u32[]{:S(2)}, u32[]{:S(2)}) collective-permute-start(bf16[384,3072]{1,0:T(8,128)(2,1)} %bitcast.28.refs_0_), channel_id=1, source_target_pairs={{0,1},{1,0},{2,3},{3,2},{4,5},{5,4},{6,7},{7,6},{8,9},{9,8},{10,11... | collective-permute-start | bytes 7077896 | tf_op jit(solution)/shard_map/ppermute | solution.py:572
  63.9 34.2 %copy-start.2 = (f32[1152,1]{0,1:T(1,128)}, f32[1152,1]{0,1:T(1,128)S(1)}, u32[]{:S(2)}) copy-start(f32[1152,1]{0,1:T(1,128)S(1)} %reshape.150) | copy-start | bytes 13828
  63.9 94.5 %collective-permute-start.1 = (f32[1152,1]{0,1:T(1,128)S(1)}, f32[1152,1]{0,1:T(1,128)S(1)}, u32[]{:S(2)}, u32[]{:S(2)}) collective-permute-start(f32[1152,1]{0,1:T(1,128)S(1)} %reshape.150), channel_id=1, source_target_pairs={{0,1},{1,0},{2,3},{3,2},{4,5},{5,4},{6,7},{7,6},{8,9},{9,8},{10,11... | collective-permute-start | bytes 13832 | tf_op jit(solution)/shard_map/ppermute | solution.py:572
  158.4 111.2 %collective-permute-start.7 = (bf16[384,3072]{1,0:T(8,128)(2,1)}, bf16[384,3072]{1,0:T(8,128)(2,1)}, u32[]{:S(2)}, u32[]{:S(2)}) collective-permute-start(bf16[384,3072]{1,0:T(8,128)(2,1)} %collective-permute-done.2.refs_1_), channel_id=1, source_target_pairs={{0,1},{1,0},{2,3},{3,2},{4,5},{5,4},{6,7},{7,6},{8,9},{9,8},{10,11... | collective-permute-start | bytes 7077896 | tf_op jit(solution)/shard_map/ppermute | solution.py:572
  158.7 111.0 %collective-permute-start.8 = (bf16[384,3072]{1,0:T(8,128)(2,1)}, bf16[384,3072]{1,0:T(8,128)(2,1)}, u32[]{:S(2)}, u32[]{:S(2)}) collective-permute-start(bf16[384,3072]{1,0:T(8,128)(2,1)} %collective-permute-done.3.refs_2_), channel_id=1, source_target_pairs={{0,1},{1,0},{2,3},{3,2},{4,5},{5,4},{6,7},{7,6},{8,9},{9,8},{10,11... | collective-permute-start | bytes 7077896 | tf_op jit(solution)/shard_map/ppermute | solution.py:572
  159.0 110.6 %collective-permute-start.9 = (bf16[192,3072]{1,0:T(8,128)(2,1)}, bf16[192,3072]{1,0:T(8,128)(2,1)}, u32[]{:S(2)}, u32[]{:S(2)}) collective-permute-start(bf16[192,3072]{1,0:T(8,128)(2,1)} %collective-permute-done.4.refs_3_), channel_id=1, source_target_pairs={{0,1},{1,0},{2,3},{3,2},{4,5},{5,4},{6,7},{7,6},{8,9},{9,8},{10,11... | collective-permute-start | bytes 3538952 | tf_op jit(solution)/shard_map/ppermute | solution.py:572
  159.2 110.5 %collective-permute-start.10 = (bf16[192,3072]{1,0:T(8,128)(2,1)}, bf16[192,3072]{1,0:T(8,128)(2,1)}, u32[]{:S(2)}, u32[]{:S(2)}) collective-permute-start(bf16[192,3072]{1,0:T(8,128)(2,1)} %collective-permute-done.5.refs_4_), channel_id=1, source_target_pairs={{0,1},{1,0},{2,3},{3,2},{4,5},{5,4},{6,7},{7,6},{8,9},{9,8},{10,11... | collective-permute-start | bytes 3538952 | tf_op jit(solution)/shard_map/ppermute | solution.py:572
  159.5 0.7 copy-start.3
  268.0 1.6 copy-start

commit v3 on v2

v3 whole, which is shorter than its diff:
```python
import functools

import jax
import jax.numpy as jnp
from jax import lax
from jax.experimental import pallas as pl
from jax.experimental.pallas import tpu as pltpu
from jax.sharding import PartitionSpec as P

MESH = pl.DeviceIdType.MESH


class Peers:
    def __init__(self, n):
        self.n = n
        self.me = lax.axis_index("tp")
        self.chip, self.core = lax.div(self.me, 2), lax.rem(self.me, 2)
        self.plus, self.minus, self.opp = self.near(1), self.near(-1), self.near(2)
        self.partner = self.other(self.me)

    def near(self, s):
        chips = self.n // 2
        return lax.rem(self.chip + s + chips, chips) * 2 + self.core

    def other(self, d):
        return d + 1 - 2 * self.core

    def greet(self, devices):
        barrier = pltpu.get_barrier_semaphore()
        for d in devices:
            pl.semaphore_signal(barrier, inc=1, device_id={"tp": d}, device_id_type=MESH)
        pl.semaphore_wait(barrier, len(devices))


def gather_all_kernel(n, S, src_ref, all_ref, loc_sem, send_sem, recv_sem):
    cap = src_ref.shape[0]

    def of(d):
        return all_ref.at[pl.ds(d * cap, cap)]
    chips = n // 2
    me = lax.axis_index("tp")
    chip, core = me // 2, lax.rem(me, 2)
    def at(c):
        return lax.rem(c + chips, chips) * 2 + core
    plus, minus, opp = at(chip + 1), at(chip - 1), at(chip + 2)
    partner = me + 1 - 2 * core
    P = 2 * S
    step = src_ref.shape[0] // P

    barrier = pltpu.get_barrier_semaphore()
    for d in (plus, minus, partner):
        pl.semaphore_signal(barrier, inc=1, device_id={"tp": d}, device_id_type=MESH)
    pl.semaphore_wait(barrier, 3)

    started = []
    def rc(src, dst, ch, k, dev):
        return pltpu.make_async_remote_copy(src_ref=src, dst_ref=dst, send_sem=send_sem.at[ch, k], recv_sem=recv_sem.at[ch, k],
                                            device_id={"tp": dev}, device_id_type=MESH)
    def go(src, dst, ch, k, dev):
        c = rc(src, dst, ch, k, dev)
        c.start()
        started.append(c)
    def piece(ref, k):
        return ref.at[pl.ds(k * step, step)]
    first, last = list(range(S)), list(range(S, P))
    for a, b in zip(first, last):
        go(piece(src_ref, a), piece(of(me), a), 0, a, plus)
        go(piece(src_ref, b), piece(of(me), b), 1, b, minus)
    for a, b in zip(first, last):
        go(piece(src_ref, b), piece(of(me), b), 0, b, plus)
        go(piece(src_ref, a), piece(of(me), a), 1, a, minus)
    go(src_ref, of(me), 4, 0, partner)
    loc = pltpu.make_async_copy(src_ref, of(me), loc_sem)
    loc.start()
    def got(owner, ch, k):
        r = piece(of(owner), k)
        rc(r, r, ch, k, partner).wait_recv()
        return r
    for a, b in zip(first, last):
        r = got(minus, 0, a)
        go(r, r, 2, a, plus)
        go(r, r, 5, a, partner)
        r = got(plus, 1, b)
        go(r, r, 3, b, minus)
        go(r, r, 6, b, partner)
    for a, b in zip(first, last):
        r = got(minus, 0, b)
        go(r, r, 5, b, partner)
        r = got(plus, 1, a)
        go(r, r, 6, a, partner)
    for a, b in zip(first, last):
        r = got(opp, 2, a)
        go(r, r, 7, a, partner)
        r = got(opp, 3, b)
        go(r, r, 7, b, partner)
    other = lambda d: d + 1 - 2 * core
    r = of(partner)
    rc(r, r, 4, 0, partner).wait_recv()
    for k in range(P):
        got(other(minus), 5, k)
        got(other(plus), 6, k)
        got(other(opp), 7, k)
    loc.wait()
    for c in started:
        c.wait_send()


def gather_all(n, rows, total, S=2, cid=0):
    return pl.pallas_call(
        functools.partial(gather_all_kernel, n, S),
        out_shape=jax.ShapeDtypeStruct((total,) + rows.shape[1:], rows.dtype),
        in_specs=[pl.BlockSpec(memory_space=pltpu.VMEM)],
        out_specs=pl.BlockSpec(memory_space=pl.ANY),
        scratch_shapes=[pltpu.SemaphoreType.DMA, pltpu.SemaphoreType.DMA((8, 2 * S)), pltpu.SemaphoreType.DMA((8, 2 * S))],
        compiler_params=pltpu.CompilerParams(collective_id=cid, has_side_effects=True),
        name="gather_all",
    )(rows)


SPAN_BITS = 13
SPAN = 1 << SPAN_BITS


def pick_kernel(n, shard_rows, cap, nb, ids_ref, table_ref, code_ref, at_ref, cnt_ref, out_ref,
                ids, col, wcol, first, wanted, list_ref, buf, scr, list_sem, sem):
    me = lax.axis_index("tp")
    R, L = ids.shape
    G, Q = 8, 4
    lane = lax.broadcasted_iota(jnp.int32, (8, L), 1)
    sub = lax.broadcasted_iota(jnp.int32, (8, L), 0)
    for r in range(R):
        b, o = divmod(r * L, ids_ref.shape[1])
        ids[r:r + 1, :] = ids_ref[b:b + 1, o:o + L]

    def columns(*pairs):
        @pl.loop(0, R // Q)
        def _(g):
            for k in range(Q):
                a = g * Q + k
                for src, dst in pairs:
                    dst[pl.ds(pl.multiple_of(a * L, L), L), :] = jnp.broadcast_to(src[pl.ds(a, 1), :], (L, L)).T

    def against(bg, start, step):
        acc = start
        def body(a, acc):
            acc = list(acc)
            for k in range(L // 8):
                at = pl.ds(pl.multiple_of(a * L + k * 8, 8), 8)
                step(acc, at, k, range(G), -1)
            return tuple(acc)
        acc = list(lax.fori_loop(0, bg * G, body, tuple(acc)))
        for d in range(G):
            for k in range(L // 8):
                step(acc, pl.ds((bg * G + d) * L + k * 8, 8), k, range(d, G), d)
        return acc

    def wide(ref, bg):
        return [jnp.broadcast_to(ref[bg * G + i:bg * G + i + 1, :], (8, L)) for i in range(G)]

    columns((ids, col))
    for bg in range(R // G):
        rows = wide(ids, bg)
        def seen(acc, at, k, which, same):
            c = col[at, :]
            for i in which:
                hit = c == rows[i]
                if i == same:
                    hit = hit & (k * 8 + sub < lane)
                acc[i] = jnp.where(hit, 1, acc[i])
        acc = against(bg, [jnp.zeros((8, L), jnp.int32)] * G, seen)
        for i in range(G):
            first[bg * G + i:bg * G + i + 1, :] = 1 - jnp.max(acc[i], axis=0, keepdims=True)

    x = ids[...]
    owner = jnp.zeros((R, L), jnp.int32)
    for o in range(1, n):
        owner = owner + jnp.where(x >= o * shard_rows, 1, 0)
    isf = first[...] == 1
    one = jnp.concatenate([jnp.where(isf & (owner == o), 1.0, 0.0) for o in range(n)], axis=0).astype(jnp.bfloat16)
    up = (lax.broadcasted_iota(jnp.int32, (L, L), 0) < lax.broadcasted_iota(jnp.int32, (L, L), 1)).astype(jnp.float32).astype(jnp.bfloat16)
    prefix = jnp.dot(one, up, preferred_element_type=jnp.float32)
    tot = jnp.dot(one, jnp.ones((L, L), jnp.bfloat16), preferred_element_type=jnp.float32)
    r = lax.broadcasted_iota(jnp.int32, (n * R, n * R), 0)
    c = lax.broadcasted_iota(jnp.int32, (n * R, n * R), 1)
    low = ((r // R == c // R) & (c < r)).astype(jnp.float32).astype(jnp.bfloat16)
    off = jnp.dot(low, tot.astype(jnp.bfloat16), preferred_element_type=jnp.float32)
    pos = prefix + off
    slot = jnp.zeros((R, L), jnp.float32)
    most = jnp.zeros((1, L), jnp.float32)
    for o in range(n):
        slot = jnp.where(owner == o, pos[o * R:(o + 1) * R], slot)
        most = jnp.maximum(most, (off + tot)[(o + 1) * R - 1:(o + 1) * R])
    cnt_ref[...] = most.astype(jnp.int32)
    code_ref[...] = jnp.where(isf, owner * SPAN + slot.astype(jnp.int32), -1)
    first[...] = jnp.where(isf, x, -1)
    columns((first, col), (code_ref, wcol))

    for bg in range(R // G):
        rows = wide(ids, bg)
        def take(acc, at, k, which, same):
            c, w = col[at, :], wcol[at, :]
            for i in which:
                acc[i] = jnp.where(c == rows[i], w, acc[i])
        acc = against(bg, [jnp.zeros((8, L), jnp.int32)] * G, take)
        for i in range(G):
            code_ref[bg * G + i:bg * G + i + 1, :] = jnp.max(acc[i], axis=0, keepdims=True)
    code = code_ref[...]
    at_ref[...] = lax.shift_right_logical(code, SPAN_BITS) * cap + jnp.minimum(lax.bitwise_and(code, SPAN - 1), cap - 1)

    K = wanted.shape[0]
    want = [me * SPAN + i * L + lane for i in range(K)]
    def body(a, acc):
        acc = list(acc)
        for k in range(L // 8):
            at = pl.ds(pl.multiple_of(a * L + k * 8, 8), 8)
            c, w = col[at, :], wcol[at, :]
            for i in range(K):
                acc[i] = jnp.where(w == want[i], c, acc[i])
        return tuple(acc)
    acc = lax.fori_loop(0, R, body, tuple(jnp.zeros((8, L), jnp.int32) for _ in range(K)))
    for i in range(K):
        wanted[i:i + 1, :] = jnp.maximum(jnp.max(acc[i], axis=0, keepdims=True) - me * shard_rows, 0)
    listed = pltpu.make_async_copy(wanted, list_ref, list_sem)
    listed.start()
    listed.wait()
    take_rows(cap, nb, lambda k: list_ref[lax.shift_right_logical(k, 7), lax.bitwise_and(k, L - 1)], table_ref, out_ref, buf, scr, sem)


def take_rows(cap, nb, row_of, table_ref, out_ref, buf, scr, sem):
    T = table_ref.shape[1] // 128
    U = 8

    def copy(k):
        base = pl.multiple_of(lax.bitwise_and(row_of(k), -8), 8)
        s = lax.bitwise_and(k, nb - 1)
        return pltpu.make_async_copy(table_ref.at[pl.ds(base, 8)], buf.at[s], sem.at[s])

    @pl.loop(0, nb)
    def _(k):
        copy(k).start()

    def group(q, more):
        for u in range(U):
            k = q * U + u
            s = lax.bitwise_and(k, nb - 1)
            copy(k).wait()
            for j in range(T):
                scr[u, j * 8:(j + 1) * 8, :] = buf[s, :, j * 128:(j + 1) * 128].astype(jnp.float32)
            r = lax.bitwise_and(row_of(k), 7)
            out_ref[k] = scr[u, pl.ds(r, T, stride=8), :].astype(jnp.bfloat16)
        if more:
            for u in range(U):
                copy(q * U + u + nb).start()

    pl.loop(0, (cap - nb) // U)(lambda q: group(q, True))
    pl.loop((cap - nb) // U, cap // U)(lambda q: group(q, False))


def pick(n, shard_rows, cap, ids, table, nb=32):
    R, L = ids.size // 128, 128
    K = -(-cap // L)
    T = table.shape[1] // 128
    V = pl.BlockSpec(memory_space=pltpu.VMEM)
    i32 = lambda *shape: jax.ShapeDtypeStruct(shape, jnp.int32)
    vm = lambda *shape: pltpu.VMEM(shape, jnp.int32)
    return pl.pallas_call(
        functools.partial(pick_kernel, n, shard_rows, cap, nb),
        out_shape=(i32(R, L), i32(R, L), i32(1, L), jax.ShapeDtypeStruct((cap, T, 128), table.dtype)),
        in_specs=[V, pl.BlockSpec(memory_space=pl.ANY)],
        out_specs=(V, V, V, V),
        scratch_shapes=[vm(R, L), vm(R * L, L), vm(R * L, L), vm(R, L), vm(K, L), pltpu.SMEM((K, L), jnp.int32),
                        pltpu.VMEM((nb, 8, T * 128), table.dtype), pltpu.VMEM((8, T * 8, 128), jnp.float32), pltpu.SemaphoreType.DMA, pltpu.SemaphoreType.DMA((nb,))],
        cost_estimate=pl.CostEstimate(flops=2 * 10**10, bytes_accessed=cap * 8 * T * 256, transcendentals=0),
        name="pick",
    )(ids, table)


def rows_kernel(cap, nb, list_ref, table_ref, out_ref, buf, scr, sem):
    take_rows(cap, nb, lambda k: list_ref[k], table_ref, out_ref, buf, scr, sem)


def rows(cap, lst, table, nb=32):
    T = table.shape[1] // 128
    return pl.pallas_call(
        functools.partial(rows_kernel, cap, nb),
        out_shape=jax.ShapeDtypeStruct((cap, T, 128), table.dtype),
        grid_spec=pltpu.PrefetchScalarGridSpec(
            num_scalar_prefetch=1, grid=(),
            in_specs=[pl.BlockSpec(memory_space=pl.ANY)],
            out_specs=pl.BlockSpec(memory_space=pltpu.VMEM),
            scratch_shapes=[pltpu.VMEM((nb, 8, table.shape[1]), table.dtype), pltpu.VMEM((8, T * 8, 128), jnp.float32), pltpu.SemaphoreType.DMA((nb,))]),
        name="rows",
    )(lst, table)


EPS = 1e-5


def project_kernel(n, tb, seq, blk, steps, chunk, code, u_hbm, pos_hbm, gain_ref, bias_ref, wa_hbm, wb_hbm, ba_ref, bb_ref,
                   qkv_ref, emb_ref, u, w, bc, pos, xs, hs, usem, wsem, psem):
    step = pl.program_id(0)
    q = Peers(n)
    me = q.me
    base = q.core * seq
    T = u.shape[1]
    M = wa_hbm.shape[0]
    inv = 1.0 / (T * 128)

    def load_u():
        return pltpu.make_async_copy(u_hbm, u, usem)
    def load_w(k):
        return pltpu.make_async_copy((wa_hbm, wb_hbm)[k], w.at[lax.rem(q.core + k, 2)], wsem.at[k])
    def load_pos(i):
        return pltpu.make_async_copy(pos_hbm.at[pl.ds(i * tb, tb)], pos.at[lax.rem(i, 2)], psem.at[lax.rem(i, 2)])
    def load_own():
        return pltpu.make_async_copy(pos_hbm.at[pl.ds(me * blk, blk)], pos.at[steps % 2, pl.ds(0, blk)], psem.at[steps % 2])

    def fetch(slot, first):
        for r in range(8):
            xs[slot, pl.ds(r, T, stride=8), :] = u[code[first + r]].astype(jnp.float32)

    def tile(slot, j):
        return xs[slot, j * 8:(j + 1) * 8, :]

    def lanes(j):
        return slice(j * 128, (j + 1) * 128)

    def norm(i, g, lane_slot):
        t = pl.multiple_of(g * 16, 16)
        out = []
        for half in range(2):
            slot = lane_slot * 2 + half
            fetch(slot, base + i * tb + g * 16 + half * 8)
            p = pos.at[lax.rem(i, 2), pl.ds(t, 16), :]
            s = None
            for j in range(T):
                e = (tile(slot, j) + p[half * 8:half * 8 + 8, lanes(j)].astype(jnp.float32)).astype(jnp.bfloat16).astype(jnp.float32)
                xs[slot, j * 8:(j + 1) * 8, :] = e
                s = e if s is None else s + e
            mean = jnp.broadcast_to(jnp.sum(s, axis=1, keepdims=True) * inv, (8, 128))
            s = None
            for j in range(T):
                c = tile(slot, j) - mean
                s = c * c if s is None else s + c * c
            var = jnp.sum(s, axis=1, keepdims=True) * inv
            rs = jnp.broadcast_to(lax.rsqrt(var + EPS), (8, 128))
            out.append((slot, mean, rs))
        for j in range(T):
            y = [(tile(slot, j) - mean) * rs * gain_ref[:, lanes(j)] + bias_ref[:, lanes(j)] for slot, mean, rs in out]
            hs[lax.rem(i, 2), pl.ds(t, 16), lanes(j)] = jnp.concatenate(y, axis=0).astype(jnp.bfloat16)

    def embed(g, lane_slot):
        per = blk // 16
        b = lax.div(g, per)
        t = pl.multiple_of(lax.rem(g, per) * 16, 16)
        for half in range(2):
            fetch(lane_slot * 2 + half, b * seq + me * blk + t + half * 8)
        p = pos.at[steps % 2, pl.ds(t, 16), :]
        for j in range(T):
            e = jnp.concatenate([tile(lane_slot * 2, j), tile(lane_slot * 2 + 1, j)], axis=0) + p[:, lanes(j)].astype(jnp.float32)
            emb_ref[b, pl.ds(t, 16), lanes(j)] = e.astype(jnp.bfloat16)

    @pl.when(step == 0)
    def _():
        load_u().start()
        heads, E = 12, M // 12
        for k, b in enumerate((ba_ref, bb_ref)):
            for r in range(heads):
                bc[lax.rem(q.core + k, 2), r * E:(r + 1) * E, :] = jnp.broadcast_to(b[r:r + 1, :], (128, 128)).T[0:E, :]
        load_pos(0).start()
        for k in range(2):
            load_w(k).start()
        load_pos(1).start()
        load_u().wait()
        load_pos(0).wait()
        @pl.loop(0, tb // 64)
        def _(g):
            for j in range(4):
                norm(0, g * 4 + j, j)
        for k in range(2):
            load_w(k).wait()

    def sweep(beside):
        per = M // chunk
        h = hs.at[lax.rem(step, 2)]
        for k in range(2):
            @pl.loop(0, per)
            def _(m):
                at = pl.multiple_of(m * chunk, 32)
                o = lax.dot_general(w[k, pl.ds(at, chunk), :], h[...], (((1,), (1,)), ((), ())), preferred_element_type=jnp.float32)
                b = jnp.concatenate([bc[k, pl.ds(at, chunk), :]] * (tb // 128), axis=1)
                qkv_ref[k, pl.ds(at, chunk), :] = (o + b).astype(jnp.bfloat16)
                n = tb // 16 // (2 * per)
                for j in range(n):
                    beside((k * per + m) * n + j, j % 4)

    @pl.when(step < steps - 1)
    def _():
        load_pos(step + 1).wait()
        @pl.when(step + 2 < steps)
        def _():
            load_pos(step + 2).start()
        @pl.when(step + 2 == steps)
        def _():
            load_own().start()
        sweep(lambda g, j: norm(step + 1, g, j))

    @pl.when(step == steps - 1)
    def _():
        load_own().wait()
        sweep(embed)


def project(n, at, u, pos, gain, bias, wa, wb, ba, bb, tb=512, chunk=288):
    seq, D = pos.shape
    blk = seq // n
    steps = seq // tb
    M = wa.shape[0]
    A = pl.BlockSpec(memory_space=pl.ANY)
    one = lambda shape: pl.BlockSpec(shape, lambda i, *_: (0,) * len(shape), pipeline_mode=pl.Buffered(1))
    return pl.pallas_call(
        functools.partial(project_kernel, n, tb, seq, blk, steps, chunk),
        out_shape=(jax.ShapeDtypeStruct((2, M, seq), jnp.bfloat16), jax.ShapeDtypeStruct((2, blk, D), jnp.bfloat16)),
        grid_spec=pltpu.PrefetchScalarGridSpec(
            num_scalar_prefetch=1, grid=(steps,),
            in_specs=[A, A, one((1, D)), one((1, D)), A, A, one(ba.shape), one(bb.shape)],
            out_specs=(pl.BlockSpec((2, M, tb), lambda i, *_: (0, 0, i)), pl.BlockSpec((2, blk, D), lambda i, *_: (0, 0, 0), pipeline_mode=pl.Buffered(1))),
            scratch_shapes=[pltpu.VMEM(u.shape, u.dtype), pltpu.VMEM((2, M, D), wa.dtype), pltpu.VMEM((2, M, 128), jnp.float32), pltpu.VMEM((2, tb, D), pos.dtype),
                            pltpu.VMEM((8, D // 128 * 8, 128), jnp.float32), pltpu.VMEM((2, tb, D), jnp.bfloat16),
                            pltpu.SemaphoreType.DMA, pltpu.SemaphoreType.DMA((2,)), pltpu.SemaphoreType.DMA((2,))]),
        compiler_params=pltpu.CompilerParams(vmem_limit_bytes=63 * 2**20),
        cost_estimate=pl.CostEstimate(flops=4 * seq * M * D, bytes_accessed=50 * 2**20, transcendentals=0),
        name="project",
    )(at, u, pos, gain, bias, wa, wb, ba, bb)


def attend_kernel(n, scale, qb, nb, early, where, qkv_ref, emb_hbm, bias_ref, *refs):
    pieces, (out_ref, kk, vv, sc, ctx, got, w, a, acc, emb, load_sem, pass_send, pass_recv, emb_sem, send_sem, recv_sem) = refs[:len(where)], refs[len(where):]
    E, S = qkv_ref.shape[3:]
    heads = got.shape[1] // E
    N = S // qb
    c = scale * 1.4426950408889634
    q = Peers(n)
    me, core = q.me, q.core
    head = pl.program_id(0)
    cut = early * E // 256 * 256
    owners = {0: me, 1: q.plus, 2: q.opp, -1: q.minus}

    def loads():
        cs = []
        for i, (ref, (away, low)) in enumerate(zip(pieces, where)):
            dst = w.at[owners[away], pl.ds(low, ref.shape[0])]
            cs.append(pltpu.make_async_copy(ref, dst, load_sem.at[i]))
            cs.append(pltpu.make_async_remote_copy(src_ref=ref, dst_ref=dst, send_sem=pass_send.at[i], recv_sem=pass_recv.at[i], device_id={"tp": q.partner}, device_id_type=MESH))
        return cs

    def send(h, s):
        to = lax.rem(me + s, n)
        return pltpu.make_async_remote_copy(src_ref=ctx.at[h, to], dst_ref=got.at[me, pl.ds(pl.multiple_of(h * E, 32), E)],
                                            send_sem=send_sem.at[s], recv_sem=recv_sem.at[lax.div(h, early), s], device_id={"tp": to}, device_id_type=MESH)

    load_emb = pltpu.make_async_copy(emb_hbm, emb, emb_sem)

    @pl.when(head == 0)
    def _():
        q.greet([lax.rem(me + s, n) for s in range(1, n)])
        vv[E:, :] = jnp.where(lax.broadcasted_iota(jnp.int32, (vv.shape[0] - E, S), 0) == 0, 1.0, 0.0).astype(jnp.bfloat16)

    @pl.when(head > 0)
    def _():
        for s in range(1, n):
            send(head - 1, s).start()

    @pl.when(head == 1)
    def _():
        for c_ in loads():
            c_.start()
        load_emb.start()

    for t in range(0, S, 128):
        kk[t:t + 128, :] = qkv_ref[0, 1, 0, :, t:t + 128].astype(jnp.float32).T.astype(jnp.bfloat16)
    vv[0:E, :] = qkv_ref[0, 2, 0]
    keep = lax.broadcasted_iota(jnp.int32, (qb, qb), 0) <= lax.broadcasted_iota(jnp.int32, (qb, qb), 1)

    def scores(i, k, m):
        s = jnp.dot(kk[k * qb:(k + 1) * qb, :], qkv_ref[0, 0, 0, :, i * qb:(i + 1) * qb], preferred_element_type=jnp.float32)
        if k == i:
            s = jnp.where(keep, s, -jnp.inf)
        sc[i % 2, k * qb:(k + 1) * qb, :] = s
        top = jnp.max(s.reshape(qb // 8, 8, qb), axis=0)
        return top if m is None else jnp.maximum(m, top)

    def weigh(i, k, mc, o):
        s = sc[i % 2, k * qb:(k + 1) * qb, :]
        p = jnp.exp2(s * c - mc).astype(jnp.bfloat16)
        d = jnp.dot(vv[:, k * qb:(k + 1) * qb], p, preferred_element_type=jnp.float32)
        return d if o is None else o + d

    m = scores(0, 0, None)
    for i in range(N):
        mc = jnp.max(m, axis=0, keepdims=True) * c
        o = m = None
        for k in range(i + 2):
            if i + 1 < N:
                m = scores(i + 1, k, m)
            if k <= i:
                o = weigh(i, k, mc, o)
        ctx[head, i] = (o[0:E] * (1.0 / o[E:E + 1])).astype(jnp.bfloat16)
    got[me, pl.ds(pl.multiple_of(head * E, 32), E), :] = ctx[head, me]

    @pl.when(head == heads - 1)
    def _():
        for s in range(1, n):
            send(head, s).start()
        K = got.shape[1]

        def arrive(group, low, high):
            for s in range(1, n):
                fr = lax.rem(me - s + n, n)
                r = got.at[fr, pl.ds(low, high - low)]
                pltpu.make_async_remote_copy(src_ref=r, dst_ref=r, send_sem=send_sem.at[s], recv_sem=recv_sem.at[group, s], device_id={"tp": fr}, device_id_type=MESH).wait_recv()

        def turn_over(low, high):
            for s in range(n):
                for k in range(low, high, 128):
                    for t in range(0, qb, 128):
                        a[(s % 2) * qb + t:(s % 2) * qb + t + 128, (s // 2) * K + k:(s // 2) * K + k + 128] = got[s, k:k + 128, t:t + 128].astype(jnp.float32).T.astype(jnp.bfloat16)

        def part(low, high, cols):
            o = None
            for i in range(n // 2):
                d = jnp.dot(a[:, i * K + low:i * K + high], w[2 * i:2 * i + 2, :, cols].reshape(K, nb)[low:high], preferred_element_type=jnp.float32)
                o = d if o is None else o + d
            return o

        arrive(0, 0, early * E)
        turn_over(0, cut)
        for c_ in loads():
            c_.wait()
        load_emb.wait()

        @pl.loop(0, w.shape[2] // nb)
        def _(j):
            cols = pl.ds(pl.multiple_of(j * nb, nb), nb)
            acc[:, cols] = part(0, cut, cols) + bias_ref[:, cols]

        arrive(1, early * E, K)
        turn_over(cut, K)

        @pl.loop(0, w.shape[2] // nb)
        def _(j):
            cols = pl.ds(pl.multiple_of(j * nb, nb), nb)
            o = part(cut, K, cols) + acc[:, cols]
            for b in range(2):
                out_ref[b, :, cols] = (emb[b, :, cols].astype(jnp.float32) + o[b * qb:(b + 1) * qb]).astype(jnp.bfloat16)

        for s in range(1, n):
            r = got.at[lax.rem(me - s + n, n)]
            pltpu.make_async_remote_copy(src_ref=r, dst_ref=r, send_sem=send_sem.at[s], recv_sem=recv_sem.at[0, s], device_id={"tp": q.partner}, device_id_type=MESH).wait_send()


def attend(n, qkv, pieces, where, emb, bias, early=6, nb=256, cid=1, qb=256):
    heads, E, S = 2 * qkv.shape[2], *qkv.shape[3:]
    H = heads // 2
    D = emb.shape[2]
    A = pl.BlockSpec(memory_space=pl.ANY)
    one = lambda shape: pl.BlockSpec(shape, lambda h: (0,) * len(shape), pipeline_mode=pl.Buffered(1))
    bf = jnp.bfloat16
    return pl.pallas_call(
        functools.partial(attend_kernel, n, E ** -0.5, qb, nb, early, where),
        out_shape=jax.ShapeDtypeStruct(emb.shape, bf),
        grid=(heads,),
        in_specs=[pl.BlockSpec((1, 3, 1, E, S), lambda h: (h // H, 0, h % H, 0, 0)), A, one(bias.shape)] + [A] * len(pieces),
        out_specs=one(emb.shape),
        scratch_shapes=[pltpu.VMEM((S, E), bf), pltpu.VMEM((E + 16, S), bf), pltpu.VMEM((2, S, qb), jnp.float32),
                        pltpu.VMEM((heads, n, E, qb), bf), pltpu.VMEM((n, heads * E, qb), bf), pltpu.VMEM((n, H * E, D), bf), pltpu.VMEM((2 * qb, n * H * E), bf),
                        pltpu.VMEM((2 * qb, D), jnp.float32), pltpu.VMEM(emb.shape, bf),
                        *[pltpu.SemaphoreType.DMA((len(pieces),))] * 3, pltpu.SemaphoreType.DMA, pltpu.SemaphoreType.DMA((n,)), pltpu.SemaphoreType.DMA((2, n))],
        compiler_params=pltpu.CompilerParams(collective_id=cid, has_side_effects=True, vmem_limit_bytes=62 * 2**20),
        name="attend",
    )(qkv, emb, bias, *pieces)


CAP = 264


def place_kernel(code_ref, u_ref, x_ref, out_ref, sem):
    @pl.loop(0, code_ref.shape[0])
    def _(t):
        c = code_ref[t]

        @pl.when(c >= 0)
        def _():
            copy = pltpu.make_async_copy(u_ref.at[c], out_ref.at[t], sem)
            copy.start()
            copy.wait()


def place(at, u, x):
    A = pl.BlockSpec(memory_space=pl.ANY)
    return pl.pallas_call(
        place_kernel,
        out_shape=jax.ShapeDtypeStruct(x.shape, x.dtype),
        grid_spec=pltpu.PrefetchScalarGridSpec(num_scalar_prefetch=1, grid=(), in_specs=[A, A], out_specs=A, scratch_shapes=[pltpu.SemaphoreType.DMA]),
        input_output_aliases={2: 0},
        name="place",
    )(at, u, x)


def solution(mesh):
    n = mesh.shape["tp"]
    def local_step(token_ids, word_shard, pos_table, ln_gain, ln_bias, w_qkv, b_qkv, w_out, b_out):
        me = lax.axis_index("tp")
        core = lax.rem(me, 2)
        seq, D = pos_table.shape
        H, E = w_qkv.shape[2:]
        shard_rows = word_shard.shape[0]
        w_own = jnp.transpose(w_qkv, (1, 2, 3, 0)).reshape(3 * H * E, D)
        b_own = jnp.pad(b_qkv.reshape(3 * H, E), ((0, 4), (0, 128 - E)))
        v_own = w_out.reshape(H * E, D)
        swap = [(d, d ^ 1) for d in range(n)]
        ring = lambda step: [(d, (d + 2 * step) % n) for d in range(n)]
        w_par, b_par = lax.ppermute(w_own, "tp", swap), lax.ppermute(b_own, "tp", swap)
        send = lambda x, step: lax.ppermute(x, "tp", ring(step))
        v0, v1, v2 = w_out[0], w_out[1], w_out[2:].reshape((H - 2) * E, D)
        minus0, plus0, minus1, plus1 = send(v0, 1), send(v0, -1), send(v1, 1), send(v1, -1)
        blk = seq // n
        total = max(n * CAP, seq + blk)
        code, at, most, u = pick(n, shard_rows, CAP, token_ids, word_shard)
        code, at, most = code.reshape(-1), at.reshape(-1), most[0, 0]
        u = gather_all(n, u, total)

        rounds = jnp.where(most > CAP, (most + CAP - 1) // CAP, 0)

        def wanted(x):
            x = x.reshape(2, seq)
            own = lax.dynamic_index_in_dim(x, core, 0, keepdims=False)
            other = lax.dynamic_index_in_dim(x, 1 - core, 0, keepdims=False)
            return jnp.concatenate([own, lax.dynamic_slice_in_dim(other, me * blk, blk)])

        t = jnp.arange(2 * seq, dtype=jnp.int32)
        t = jnp.where(t // seq == core, t % seq, jnp.clip(t % seq - me * blk, 0, blk - 1) + seq)

        def more(carry):
            r, u, _ = carry
            slot = code % SPAN - r * CAP
            hit = (slot >= 0) & (slot < CAP)
            mine = jnp.where(hit & (code // SPAN == me), slot, -1)
            ids = token_ids.reshape(-1) - me * shard_rows
            chosen = jnp.max(jnp.where(mine[None, :] == jnp.arange(CAP)[:, None], ids[None, :], 0), axis=1)
            v = gather_all(n, rows(CAP, chosen, word_shard), total)
            return r + 1, place(wanted(jnp.where(hit, code // SPAN * CAP + slot, -1)), v, u), t

        _, u, at = lax.while_loop(lambda c: c[0] < rounds, more, (jnp.int32(0), u, at))

        v2, minus0_, plus1_, u = lax.optimization_barrier((v2, minus0, plus1, u))
        minus2, plus2, opp0, opp1, opp2 = send(v2, 1), send(v2, -1), send(minus0_, 1), send(plus1_, -1), send(v2, 2)
        pieces = [v_own, minus0, plus0, minus1, plus1, minus2, plus2, opp0, opp1, opp2]
        where = ((0, 0), (-1, 0), (1, 0), (-1, E), (1, E), (-1, 2 * E), (1, 2 * E), (2, 0), (2, E), (2, 2 * E))
        qkv, embed = project(n, at, u, pos_table, ln_gain[None], ln_bias[None], w_own, w_par, b_own, b_par)
        resid_out = attend(n, qkv.reshape(2, 3, H, E, seq), pieces, where, embed, b_out[None])
        return resid_out, embed

    in_specs = (P("dp", None), P("tp", None), P(None, None), P(None), P(None), P(None, None, "tp", None), P(None, "tp", None), P("tp", None, None), P(None))
    out_specs = (P("dp", "tp", None), P("dp", "tp", None))
    return jax.shard_map(local_step, mesh=mesh, in_specs=in_specs, out_specs=out_specs, check_vma=False)
```

time: 289 us -> 225 us (0.78)
  waiting for transfers between devices: 51.4 us -> 0.03 us
  Pallas kernels: 215 us -> 199 us
  starting transfers between devices: 10.3 us -> 13.5 us
    ppermute x11, waiting for transfers between devices: 51.4 us -> 0.03 us  [the longest x9 0.02 us: local_step(): send = lambda x, step: lax.ppermute(x, 'tp', ring(step))]
    pallas_call x5 -> x3, Pallas kernels: 155 us -> 138 us  [the longest x1 61.9 us: project(): pl.pallas_call(functools.partial(project_kernel, n, tb, seq, blk, steps,...]
    ppermute x11, starting transfers between devices: 10.3 us -> 13.5 us  [the longest x9 11.1 us: local_step(): send = lambda x, step: lax.ppermute(x, 'tp', ring(step))]
    unnamed x10 -> x13, local copies, waits for them, and re-layouts: 2.33 us -> 5.44 us
  transfers between devices with their start and end apart: 11 -> 11, of which waited for: 1 -> 0; matrix products, arithmetic and copies ran while one was open for 2% -> 1% of each run, Pallas kernels for 68% -> 65%
where the time goes in v3:
time: 225 us; the launch traced here: 224 us
  Pallas kernels  199 us (88%)
  starting transfers between devices  13.5 us (6%)
  local copies, waits for them, and re-layouts  8.94 us (4%)
  between operations  2.25 us (1%)
    pallas_call x1, Pallas kernels, project(): pl.pallas_call(functools.partial(project_kernel, n, tb, seq, blk, steps,...  61.9 us
    pallas_call x1, Pallas kernels, gather_all(): pl.pallas_call(functools.partial(gather_all_kernel, n, S), out_shape=jax....  61.2 us
    pallas_call x1, Pallas kernels, attend(): pl.pallas_call(functools.partial(attend_kernel, n, E ** (-0.5), qb, nb, e...  54.2 us
    pallas_call x1, Pallas kernels, pick(): pl.pallas_call(functools.partial(pick_kernel, n, shard_rows, cap, nb), ou...  21.5 us
    ppermute x9, starting transfers between devices, local_step(): send = lambda x, step: lax.ppermute(x, 'tp', ring(step))  11.1 us
    unnamed x13, local copies, waits for them, and re-layouts  5.44 us
  transfers between devices with their start and end apart: 11, of which 0 were waited for; matrix products, arithmetic and copies ran while one was open for 1% of the time, Pallas kernels for 65%

profile of v3, /device:TPU:81, one launch (start us, length us, event | category | flops | bytes accessed | tf_op | source)
XLA Modules:
  0.0 223.5 jit_solution(5113008450114172763)
XLA Ops:
  0.6 2.3 %slice_bitcast_fusion = (bf16[96,3072]{1,0:T(8,128)(2,1)}, bf16[96,3072]{1,0:T(8,128)(2,1)}) fusion(bf16[4,96,3072]{2,1,0:T(8,128)(2,1)} %param.18), kind=kLoop, calls=%fused_computation.42 | loop fusion | bytes 2359296 | tf_op jit(solution)/shard_map/squeeze | solution.py:625
  3.0 2.2 collective-permute-start
  5.1 1.5 collective-permute-start.4
  6.7 1.5 collective-permute-start.1
  8.2 0.0 collective-permute-start.5
  8.2 2.1 collective-permute-start.2
  10.3 21.5 %pick.1 = (s32[32,128]{1,0:T(8,128)S(1)}, s32[32,128]{1,0:T(8,128)}, s32[1,128]{1,0:T(1,128)}, bf16[264,24,128]{2,1,0:T(8,128)(2,1)}) custom-call(s32[2,2048]{1,0:T(2,128)} %ids_ref.1, bf16[6400,3072]{1,0:T(8,128)(2,1)} %table_ref.1), custom_call_target="tpu_custom_call" | custom-call | flops 20000000000 | bytes 12976128 | tf_op jit(solution)/shard_map/pick/pallas_call | solution.py:266
  33.3 0.0 copy-start.4
  33.3 0.0 copy-start.2
  33.3 61.2 %gather_all.2 = bf16[2304,24,128]{2,1,0:T(8,128)(2,1)} custom-call(bf16[264,24,128]{2,1,0:T(8,128)(2,1)} %get-tuple-element.345.src_ref), custom_call_target="tpu_custom_call" | custom-call | tf_op jit(solution)/shard_map/gather_all/pallas_call | solution.py:109
  94.5 0.0 copy-done.4
  94.6 0.0 copy-start.3
  94.6 0.0 collective-permute-done.refs_1_
  94.6 0.0 copy-start.1
  94.6 0.2 collective-permute-start.3
  94.9 0.0 copy-done.2
  94.9 0.0 copy-start
  94.9 0.3 copy-done.3
  95.2 1.4 copy-done
  96.5 1.1 slice.13
  97.6 0.0 collective-permute-done.1.refs_4_
  97.6 0.6 collective-permute-start.10
  98.2 0.0 collective-permute-done.3.bb_ref
  98.2 0.0 copy-start.5
  98.2 1.2 collective-permute-start.6
  99.5 0.0 collective-permute-done.4.refs_2_
  99.5 1.4 collective-permute-start.7
  100.9 0.0 collective-permute-done.5.refs_3_
  100.9 0.0 copy-done.1
  100.9 0.0 collective-permute-start.8
  101.0 0.0 collective-permute-done.2.wb_hbm
  101.0 2.6 %collective-permute-start.9 = (bf16[96,3072]{1,0:T(8,128)(2,1)}, bf16[96,3072]{1,0:T(8,128)(2,1)}, u32[]{:S(2)}, u32[]{:S(2)}) collective-permute-start(bf16[96,3072]{1,0:T(8,128)(2,1)} %collective-permute-done.1.refs_4_), channel_id=1, source_target_pairs={{0,6},{1,7},{2,0},{3,1},{4,2},{5,3},{6,4},{7,5},{8,14},{9,15},{10,... | collective-permute-start | bytes 1769480 | tf_op jit(solution)/shard_map/ppermute | solution.py:624
  103.6 0.0 copy-done.5
  103.6 61.9 %project.1 = (bf16[2,1152,2048]{2,1,0:T(8,128)(2,1)}, bf16[2,256,3072]{2,1,0:T(8,128)(2,1)}) custom-call(s32[4096]{0:T(1024)} %get-tuple-element.349.code, bf16[2304,24,128]{2,1,0:T(8,128)(2,1)} %get-tuple-element.351.u_hbm, bf16[2048,3072]{1,0:T(8,128)(2,1)} %pos_hbm.1, f32[1,3072]{1,0:T(1,128)} %bitcast.56, f32[1,3072]{1,0:T(1,128)} %bitcast.57, ...), custom_call_target="tpu_custom_call" | custom-call | flops 28991029248 | bytes 52428800 | tf_op jit(solution)/shard_map/project/pallas_call | solution.py:421
  165.5 0.0 collective-permute-done.8.refs_7_
  165.5 0.0 collective-permute-done.9.refs_8_
  165.5 0.0 collective-permute-done.10.refs_9_
  165.5 0.0 collective-permute-done.6.refs_5_
  165.5 0.0 collective-permute-done.7.refs_6_
  165.6 54.2 %attend.1 = bf16[2,256,3072]{2,1,0:T(8,128)(2,1)} custom-call(bf16[2,3,4,96,2048]{4,3,2,1,0:T(8,128)(2,1)} %bitcast.44, bf16[2,256,3072]{2,1,0:T(8,128)(2,1)} %get-tuple-element.714.emb_hbm, f32[1,3072]{1,0:T(1,128)} %bitcast.53, bf16[384,3072]{1,0:T(8,128)(2,1)} %bitcast.43, bf16[96,3072]{1,0:T(8,128)(2,1)} %copy-done.1, ...), custom_call_target="tpu_custom_call" | custom-call | tf_op jit(solution)/shard_map/attend/pallas_call | solution.py:569
  219.8 3.8 %copy.29 = bf16[2,256,3072]{2,1,0:T(8,128)(2,1)} copy(bf16[2,256,3072]{2,1,0:T(8,128)(2,1)} %attend.1) | data formatting | bytes 6291456
  (8 shorter events, 0.1 us)
Async XLA Ops:
  3.0 91.6 %collective-permute-start = (bf16[96,3072]{1,0:T(8,128)(2,1)}, bf16[96,3072]{1,0:T(8,128)(2,1)S(1)}, u32[]{:S(2)}, u32[]{:S(2)}) collective-permute-start(bf16[96,3072]{1,0:T(8,128)(2,1)} %get-tuple-element.440), channel_id=1, source_target_pairs={{0,2},{1,3},{2,4},{3,5},{4,6},{5,7},{6,0},{7,1},{8,10},{9,11},{10,... | collective-permute-start | bytes 1769480 | tf_op jit(solution)/shard_map/ppermute | solution.py:624
  5.1 94.3 %collective-permute-start.4 = (bf16[96,3072]{1,0:T(8,128)(2,1)}, bf16[96,3072]{1,0:T(8,128)(2,1)}, u32[]{:S(2)}, u32[]{:S(2)}) collective-permute-start(bf16[96,3072]{1,0:T(8,128)(2,1)} %get-tuple-element.440), channel_id=1, source_target_pairs={{0,6},{1,7},{2,0},{3,1},{4,2},{5,3},{6,4},{7,5},{8,14},{9,15},{10,... | collective-permute-start | bytes 1769480 | tf_op jit(solution)/shard_map/ppermute | solution.py:624
  6.7 91.0 %collective-permute-start.1 = (bf16[96,3072]{1,0:T(8,128)(2,1)}, bf16[96,3072]{1,0:T(8,128)(2,1)}, u32[]{:S(2)}, u32[]{:S(2)}) collective-permute-start(bf16[96,3072]{1,0:T(8,128)(2,1)} %get-tuple-element.439), channel_id=1, source_target_pairs={{0,6},{1,7},{2,0},{3,1},{4,2},{5,3},{6,4},{7,5},{8,14},{9,15},{10,... | collective-permute-start | bytes 1769480 | tf_op jit(solution)/shard_map/ppermute | solution.py:624
  8.2 92.8 %collective-permute-start.5 = (bf16[96,3072]{1,0:T(8,128)(2,1)}, bf16[96,3072]{1,0:T(8,128)(2,1)}, u32[]{:S(2)}, u32[]{:S(2)}) collective-permute-start(bf16[96,3072]{1,0:T(8,128)(2,1)} %get-tuple-element.439), channel_id=1, source_target_pairs={{0,2},{1,3},{2,4},{3,5},{4,6},{5,7},{6,0},{7,1},{8,10},{9,11},{10,... | collective-permute-start | bytes 1769480 | tf_op jit(solution)/shard_map/ppermute | solution.py:624
  8.2 92.8 %collective-permute-start.2 = (bf16[1152,3072]{1,0:T(8,128)(2,1)}, bf16[1152,3072]{1,0:T(8,128)(2,1)}, u32[]{:S(2)}, u32[]{:S(2)}) collective-permute-start(bf16[1152,3072]{1,0:T(8,128)(2,1)} %bitcast.54), channel_id=1, source_target_pairs={{0,1},{1,0},{2,3},{3,2},{4,5},{5,4},{6,7},{7,6},{8,9},{9,8},{10,11... | collective-permute-start | bytes 21233672 | tf_op jit(solution)/shard_map/ppermute | solution.py:623
  33.3 61.3 %copy-start.4 = (f32[3,4,96]{2,1,0:T(4,128)S(1)}, f32[3,4,96]{2,1,0:T(4,128)}, u32[]{:S(2)}) copy-start(f32[3,4,96]{2,1,0:T(4,128)} %param.17) | copy-start | bytes 13828
  33.3 61.6 %copy-start.2 = (s32[2,2048]{1,0:T(2,128)S(1)}, s32[2,2048]{1,0:T(2,128)}, u32[]{:S(2)}) copy-start(s32[2,2048]{1,0:T(2,128)} %ids_ref.1) | copy-start | bytes 49156
  94.6 0.6 copy-start.3
  94.6 6.3 %copy-start.1 = (bf16[96,3072]{1,0:T(8,128)(2,1)}, bf16[96,3072]{1,0:T(8,128)(2,1)S(1)}, u32[]{:S(2)}) copy-start(bf16[96,3072]{1,0:T(8,128)(2,1)S(1)} %collective-permute-done.refs_1_) | copy-start | bytes 1769476
  94.6 3.6 %collective-permute-start.3 = (f32[16,128]{1,0:T(8,128)S(1)}, f32[16,128]{1,0:T(8,128)S(1)}, u32[]{:S(2)}, u32[]{:S(2)}) collective-permute-start(f32[16,128]{1,0:T(8,128)S(1)} %pad.4.ba_ref), channel_id=1, source_target_pairs={{0,1},{1,0},{2,3},{3,2},{4,5},{5,4},{6,7},{7,6},{8,9},{9,8},{10,11... | collective-permute-start | bytes 24584 | tf_op jit(solution)/shard_map/ppermute | solution.py:623
  94.9 1.7 copy-start
  97.6 67.9 %collective-permute-start.10 = (bf16[192,3072]{1,0:T(8,128)(2,1)}, bf16[192,3072]{1,0:T(8,128)(2,1)}, u32[]{:S(2)}, u32[]{:S(2)}) collective-permute-start(bf16[192,3072]{1,0:T(8,128)(2,1)} %bitcast.7), channel_id=1, source_target_pairs={{0,4},{1,5},{2,6},{3,7},{4,0},{5,1},{6,2},{7,3},{8,12},{9,13},{10,... | collective-permute-start | bytes 3538952 | tf_op jit(solution)/shard_map/ppermute | solution.py:624
  98.2 5.4 %copy-start.5 = (f32[16,128]{1,0:T(8,128)}, f32[16,128]{1,0:T(8,128)S(1)}, u32[]{:S(2)}) copy-start(f32[16,128]{1,0:T(8,128)S(1)} %collective-permute-done.3.bb_ref) | copy-start | bytes 24580
  98.2 67.3 %collective-permute-start.6 = (bf16[192,3072]{1,0:T(8,128)(2,1)}, bf16[192,3072]{1,0:T(8,128)(2,1)}, u32[]{:S(2)}, u32[]{:S(2)}) collective-permute-start(bf16[192,3072]{1,0:T(8,128)(2,1)} %bitcast.7), channel_id=1, source_target_pairs={{0,2},{1,3},{2,4},{3,5},{4,6},{5,7},{6,0},{7,1},{8,10},{9,11},{10,... | collective-permute-start | bytes 3538952 | tf_op jit(solution)/shard_map/ppermute | solution.py:624
  99.5 66.0 %collective-permute-start.7 = (bf16[192,3072]{1,0:T(8,128)(2,1)}, bf16[192,3072]{1,0:T(8,128)(2,1)}, u32[]{:S(2)}, u32[]{:S(2)}) collective-permute-start(bf16[192,3072]{1,0:T(8,128)(2,1)} %bitcast.7), channel_id=1, source_target_pairs={{0,6},{1,7},{2,0},{3,1},{4,2},{5,3},{6,4},{7,5},{8,14},{9,15},{10,... | collective-permute-start | bytes 3538952 | tf_op jit(solution)/shard_map/ppermute | solution.py:624
  100.9 64.6 %collective-permute-start.8 = (bf16[96,3072]{1,0:T(8,128)(2,1)S(1)}, bf16[96,3072]{1,0:T(8,128)(2,1)}, u32[]{:S(2)}, u32[]{:S(2)}) collective-permute-start(bf16[96,3072]{1,0:T(8,128)(2,1)S(1)} %collective-permute-done.refs_1_), channel_id=1, source_target_pairs={{0,2},{1,3},{2,4},{3,5},{4,6},{5,7},{6,0},{7,1},{8,10},{9,11},{10,... | collective-permute-start | bytes 1769480 | tf_op jit(solution)/shard_map/ppermute | solution.py:624
  101.0 64.5 %collective-permute-start.9 = (bf16[96,3072]{1,0:T(8,128)(2,1)}, bf16[96,3072]{1,0:T(8,128)(2,1)}, u32[]{:S(2)}, u32[]{:S(2)}) collective-permute-start(bf16[96,3072]{1,0:T(8,128)(2,1)} %collective-permute-done.1.refs_4_), channel_id=1, source_target_pairs={{0,6},{1,7},{2,0},{3,1},{4,2},{5,3},{6,4},{7,5},{8,14},{9,15},{10,... | collective-permute-start | bytes 1769480 | tf_op jit(solution)/shard_map/ppermute | solution.py:624

commit v4 on v3

--- a/solution.py
+++ b/solution.py
@@ -8,6 +8,7 @@
 from jax.sharding import PartitionSpec as P
 
 MESH = pl.DeviceIdType.MESH
+VMEM = 63 * 2**20
 
 
 class Peers:
@@ -30,6 +31,52 @@
         for d in devices:
             pl.semaphore_signal(barrier, inc=1, device_id={"tp": d}, device_id_type=MESH)
         pl.semaphore_wait(barrier, len(devices))
+
+
+class Spread:
+    CHANNELS = 9
+
+    def __init__(self, peers, own, place, send_sem, recv_sem):
+        self.q, self.own, self.place, self.send_sem, self.recv_sem = peers, own, place, send_sem, recv_sem
+
+    def half(self, ref, i):
+        rows = ref.shape[0] // 2
+        return ref.at[pl.ds(i * rows, rows)]
+
+    def copy(self, channel, p, src, dst, to):
+        return pltpu.make_async_remote_copy(src_ref=src, dst_ref=dst, send_sem=self.send_sem.at[channel, p], recv_sem=self.recv_sem.at[channel, p],
+                                            device_id={"tp": to}, device_id_type=MESH)
+
+    def got(self, channel, p, ref):
+        self.copy(channel, p, ref, ref, self.q.partner).wait_recv()
+
+    def begin(self, p):
+        q = self.q
+        for channel, to in ((0, q.plus), (1, q.minus), (4, q.partner)):
+            self.copy(channel, p, self.own(p), self.place(q.me, p), to).start()
+
+    def turn(self, p):
+        q = self.q
+        for i, (d, to) in enumerate(((q.minus, q.plus), (q.plus, q.minus))):
+            ref = self.place(d, p)
+            self.got(i, p, ref)
+            self.copy(2 + i, p, self.half(ref, i), self.half(ref, i), to).start()
+            self.copy(5 + i, p, ref, ref, q.partner).start()
+
+    def last(self, p):
+        q = self.q
+        for i in range(2):
+            c = self.half(self.place(q.opp, p), i)
+            self.got(2 + i, p, c)
+            self.copy(7 + i, p, c, c, q.partner).start()
+
+    def finish(self, p):
+        q = self.q
+        own, a, b, c = (self.place(d, p) for d in (q.partner, q.other(q.minus), q.other(q.plus), q.other(q.opp)))
+        for channel, ref in ((4, own), (5, a), (6, b), (7, self.half(c, 0)), (8, self.half(c, 1))):
+            self.got(channel, p, ref)
+        for channel, ref in ((0, own), (1, own), (4, own), (5, a), (6, b), (2, self.half(c, 0)), (3, self.half(c, 1)), (7, self.half(c, 0)), (8, self.half(c, 1))):
+            self.copy(channel, p, ref, ref, q.partner).wait_send()
 
 
 def gather_all_kernel(n, S, src_ref, all_ref, loc_sem, send_sem, recv_sem):
@@ -121,7 +168,7 @@
 SPAN = 1 << SPAN_BITS
 
 
-def pick_kernel(n, shard_rows, cap, nb, ids_ref, table_ref, code_ref, at_ref, cnt_ref, out_ref,
+def pick_kernel(n, shard_rows, cap, soon, early, nb, ids_ref, table_ref, code_ref, at_ref, cnt_ref, out_ref,
                 ids, col, wcol, first, wanted, list_ref, buf, scr, list_sem, sem):
     me = lax.axis_index("tp")
     R, L = ids.shape
@@ -129,8 +176,8 @@
     lane = lax.broadcasted_iota(jnp.int32, (8, L), 1)
     sub = lax.broadcasted_iota(jnp.int32, (8, L), 0)
     for r in range(R):
-        b, o = divmod(r * L, ids_ref.shape[1])
-        ids[r:r + 1, :] = ids_ref[b:b + 1, o:o + L]
+        o, b = divmod(r, ids_ref.shape[0])
+        ids[r:r + 1, :] = ids_ref[b:b + 1, o * L:(o + 1) * L]
 
     def columns(*pairs):
         @pl.loop(0, R // Q)
@@ -190,7 +237,7 @@
     for o in range(n):
         slot = jnp.where(owner == o, pos[o * R:(o + 1) * R], slot)
         most = jnp.maximum(most, (off + tot)[(o + 1) * R - 1:(o + 1) * R])
-    cnt_ref[...] = most.astype(jnp.int32)
+    cnt_ref[0:1, :] = most.astype(jnp.int32)
     code_ref[...] = jnp.where(isf, owner * SPAN + slot.astype(jnp.int32), -1)
     first[...] = jnp.where(isf, x, -1)
     columns((first, col), (code_ref, wcol))
@@ -205,7 +252,10 @@
         for i in range(G):
             code_ref[bg * G + i:bg * G + i + 1, :] = jnp.max(acc[i], axis=0, keepdims=True)
     code = code_ref[...]
-    at_ref[...] = lax.shift_right_logical(code, SPAN_BITS) * cap + jnp.minimum(lax.bitwise_and(code, SPAN - 1), cap - 1)
+    who, slot = lax.shift_right_logical(code, SPAN_BITS), lax.bitwise_and(code, SPAN - 1)
+    at_ref[...] = jnp.where(slot < soon, who * soon + slot, n * soon + who * (cap - soon) + jnp.minimum(slot, cap - 1) - soon)
+    seen = jnp.max(slot[0:early // L * ids_ref.shape[0], :], axis=0, keepdims=True)
+    cnt_ref[1:2, :] = jnp.broadcast_to(jnp.max(seen, axis=1, keepdims=True) + 1, (1, L))
 
     K = wanted.shape[0]
     want = [me * SPAN + i * L + lane for i in range(K)]
@@ -256,7 +306,7 @@
     pl.loop((cap - nb) // U, cap // U)(lambda q: group(q, False))
 
 
-def pick(n, shard_rows, cap, ids, table, nb=32):
+def pick(n, shard_rows, cap, soon, early, ids, table, nb=32):
     R, L = ids.size // 128, 128
     K = -(-cap // L)
     T = table.shape[1] // 128
@@ -264,12 +314,13 @@
     i32 = lambda *shape: jax.ShapeDtypeStruct(shape, jnp.int32)
     vm = lambda *shape: pltpu.VMEM(shape, jnp.int32)
     return pl.pallas_call(
-        functools.partial(pick_kernel, n, shard_rows, cap, nb),
-        out_shape=(i32(R, L), i32(R, L), i32(1, L), jax.ShapeDtypeStruct((cap, T, 128), table.dtype)),
+        functools.partial(pick_kernel, n, shard_rows, cap, soon, early, nb),
+        out_shape=(i32(R, L), i32(R, L), i32(2, L), jax.ShapeDtypeStruct((cap, T, 128), table.dtype)),
         in_specs=[V, pl.BlockSpec(memory_space=pl.ANY)],
         out_specs=(V, V, V, V),
         scratch_shapes=[vm(R, L), vm(R * L, L), vm(R * L, L), vm(R, L), vm(K, L), pltpu.SMEM((K, L), jnp.int32),
                         pltpu.VMEM((nb, 8, T * 128), table.dtype), pltpu.VMEM((8, T * 8, 128), jnp.float32), pltpu.SemaphoreType.DMA, pltpu.SemaphoreType.DMA((nb,))],
+        compiler_params=pltpu.CompilerParams(vmem_limit_bytes=VMEM),
         cost_estimate=pl.CostEstimate(flops=2 * 10**10, bytes_accessed=cap * 8 * T * 256, transcendentals=0),
         name="pick",
     )(ids, table)
@@ -294,144 +345,274 @@
 
 
 EPS = 1e-5
-
-
-def project_kernel(n, tb, seq, blk, steps, chunk, code, u_hbm, pos_hbm, gain_ref, bias_ref, wa_hbm, wb_hbm, ba_ref, bb_ref,
-                   qkv_ref, emb_ref, u, w, bc, pos, xs, hs, usem, wsem, psem):
-    step = pl.program_id(0)
-    q = Peers(n)
-    me = q.me
-    base = q.core * seq
-    T = u.shape[1]
-    M = wa_hbm.shape[0]
-    inv = 1.0 / (T * 128)
-
-    def load_u():
-        return pltpu.make_async_copy(u_hbm, u, usem)
-    def load_w(k):
-        return pltpu.make_async_copy((wa_hbm, wb_hbm)[k], w.at[lax.rem(q.core + k, 2)], wsem.at[k])
-    def load_pos(i):
-        return pltpu.make_async_copy(pos_hbm.at[pl.ds(i * tb, tb)], pos.at[lax.rem(i, 2)], psem.at[lax.rem(i, 2)])
-    def load_own():
-        return pltpu.make_async_copy(pos_hbm.at[pl.ds(me * blk, blk)], pos.at[steps % 2, pl.ds(0, blk)], psem.at[steps % 2])
-
-    def fetch(slot, first):
+TOKENS = 256
+
+
+class Norm:
+    def __init__(self, me, core, at, pos_hbm, gain_ref, bias_ref, h_ref, emb_ref, pos, xs, out, pos_sem, out_sem):
+        self.me, self.core, self.at = me, core, at
+        self.pos_hbm, self.gain_ref, self.bias_ref, self.h_ref, self.emb_ref = pos_hbm, gain_ref, bias_ref, h_ref, emb_ref
+        self.pos, self.xs, self.out, self.pos_sem, self.out_sem = pos, xs, out, pos_sem, out_sem
+        self.T = xs.shape[1] // 8
+        self.blocks = h_ref.shape[0] // TOKENS
+
+    def load(self, i):
+        block = jnp.where(i < self.blocks, i, self.me)
+        s = lax.rem(i, 2)
+        return pltpu.make_async_copy(self.pos_hbm.at[pl.ds(pl.multiple_of(block * TOKENS, TOKENS), TOKENS)], self.pos.at[s], self.pos_sem.at[s])
+
+    def store(self, i):
+        s = lax.rem(i, 2)
+        return pltpu.make_async_copy(self.out.at[s], self.h_ref.at[pl.ds(pl.multiple_of(i * TOKENS, TOKENS), TOKENS)], self.out_sem.at[s])
+
+    def store_own(self, b):
+        return pltpu.make_async_copy(self.out.at[b], self.emb_ref.at[b], self.out_sem.at[b])
+
+    def tile(self, slot, j):
+        return self.xs[slot, j * 8:(j + 1) * 8, :]
+
+    def fetch(self, slot, seq, t, row_of):
+        first = (lax.shift_right_logical(t, 7) * 2 + seq) * 128 + lax.bitwise_and(t, 127)
         for r in range(8):
-            xs[slot, pl.ds(r, T, stride=8), :] = u[code[first + r]].astype(jnp.float32)
-
-    def tile(slot, j):
-        return xs[slot, j * 8:(j + 1) * 8, :]
-
-    def lanes(j):
+            self.xs[slot, pl.ds(r, self.T, stride=8), :] = row_of(self.at[first + r]).astype(jnp.float32)
+
+    def lanes(self, j):
         return slice(j * 128, (j + 1) * 128)
 
-    def norm(i, g, lane_slot):
+    def norm(self, i, g, lane_slot, row_of):
+        T, xs = self.T, self.xs
+        inv = 1.0 / (T * 128)
         t = pl.multiple_of(g * 16, 16)
         out = []
         for half in range(2):
             slot = lane_slot * 2 + half
-            fetch(slot, base + i * tb + g * 16 + half * 8)
-            p = pos.at[lax.rem(i, 2), pl.ds(t, 16), :]
+            self.fetch(slot, self.core, i * TOKENS + g * 16 + half * 8, row_of)
+            p = self.pos.at[lax.rem(i, 2), pl.ds(t, 16), :]
             s = None
             for j in range(T):
-                e = (tile(slot, j) + p[half * 8:half * 8 + 8, lanes(j)].astype(jnp.float32)).astype(jnp.bfloat16).astype(jnp.float32)
+                e = (self.tile(slot, j) + p[half * 8:half * 8 + 8, self.lanes(j)].astype(jnp.float32)).astype(jnp.bfloat16).astype(jnp.float32)
                 xs[slot, j * 8:(j + 1) * 8, :] = e
                 s = e if s is None else s + e
             mean = jnp.broadcast_to(jnp.sum(s, axis=1, keepdims=True) * inv, (8, 128))
             s = None
             for j in range(T):
-                c = tile(slot, j) - mean
+                c = self.tile(slot, j) - mean
                 s = c * c if s is None else s + c * c
             var = jnp.sum(s, axis=1, keepdims=True) * inv
-            rs = jnp.broadcast_to(lax.rsqrt(var + EPS), (8, 128))
-            out.append((slot, mean, rs))
+            out.append((slot, mean, jnp.broadcast_to(lax.rsqrt(var + EPS), (8, 128))))
         for j in range(T):
-            y = [(tile(slot, j) - mean) * rs * gain_ref[:, lanes(j)] + bias_ref[:, lanes(j)] for slot, mean, rs in out]
-            hs[lax.rem(i, 2), pl.ds(t, 16), lanes(j)] = jnp.concatenate(y, axis=0).astype(jnp.bfloat16)
-
-    def embed(g, lane_slot):
-        per = blk // 16
-        b = lax.div(g, per)
-        t = pl.multiple_of(lax.rem(g, per) * 16, 16)
+            y = [(self.tile(slot, j) - mean) * rs * self.gain_ref[:, self.lanes(j)] + self.bias_ref[:, self.lanes(j)] for slot, mean, rs in out]
+            self.out[lax.rem(i, 2), pl.ds(t, 16), self.lanes(j)] = jnp.concatenate(y, axis=0).astype(jnp.bfloat16)
+
+    def embed(self, b, g, lane_slot, row_of):
+        t = pl.multiple_of(g * 16, 16)
         for half in range(2):
-            fetch(lane_slot * 2 + half, b * seq + me * blk + t + half * 8)
-        p = pos.at[steps % 2, pl.ds(t, 16), :]
-        for j in range(T):
-            e = jnp.concatenate([tile(lane_slot * 2, j), tile(lane_slot * 2 + 1, j)], axis=0) + p[:, lanes(j)].astype(jnp.float32)
-            emb_ref[b, pl.ds(t, 16), lanes(j)] = e.astype(jnp.bfloat16)
+            self.fetch(lane_slot * 2 + half, b, self.me * TOKENS + t + half * 8, row_of)
+        p = self.pos.at[self.blocks % 2, pl.ds(t, 16), :]
+        for j in range(self.T):
+            e = jnp.concatenate([self.tile(lane_slot * 2, j), self.tile(lane_slot * 2 + 1, j)], axis=0) + p[:, self.lanes(j)].astype(jnp.float32)
+            self.out[b, pl.ds(t, 16), self.lanes(j)] = e.astype(jnp.bfloat16)
+
+    def run(self, low, high, row_of):
+        @pl.loop(low, high)
+        def _(i):
+            self.load(i).wait()
+            self.load(i + 1).start()
+
+            @pl.when(i >= 2)
+            def _():
+                self.store(i - 2).wait()
+
+            @pl.loop(0, TOKENS // 64)
+            def _(g):
+                for j in range(4):
+                    self.norm(i, g * 4 + j, j, row_of)
+            self.store(i).start()
+
+    def close(self, row_of):
+        self.load(self.blocks).wait()
+        for b in range(2):
+            self.store(self.blocks - 2 + b).wait()
+
+            @pl.loop(0, TOKENS // 64)
+            def _(g):
+                for j in range(4):
+                    self.embed(b, g * 4 + j, j, row_of)
+            self.store_own(b).start()
+        for b in range(2):
+            self.store_own(b).wait()
+
+    @staticmethod
+    def scratch(D):
+        return [pltpu.VMEM((2, TOKENS, D), jnp.bfloat16), pltpu.VMEM((8, D // 128 * 8, 128), jnp.float32), pltpu.VMEM((2, TOKENS, D), jnp.bfloat16),
+                pltpu.SemaphoreType.DMA((2,)), pltpu.SemaphoreType.DMA((2,))]
+
+
+def broadcast_kernel(n, soon, early, at, rows_ref, pos_hbm, gain_ref, bias_ref, v_ref, w_ref, b_ref,
+                     h_ref, emb_ref, minus_ref, plus_ref, w_par_ref, b_par_ref, ua, ub, *rest):
+    send_sem, recv_sem, pass_send, pass_recv = rest[-4:]
+    q = Peers(n)
+    me = q.me
+    work = Norm(me, q.core, at, pos_hbm, gain_ref, bias_ref, h_ref, emb_ref, *rest[:-4])
+    cap = rows_ref.shape[0]
+    late = cap - soon
+    spans = ((ua, soon, 0, soon // 2), (ua, soon, soon // 2, soon // 2), (ub, late, 0, late))
+
+    def own(p):
+        ref, _, low, size = spans[p]
+        return rows_ref.at[pl.ds(low + (soon if ref is ub else 0), size)]
+
+    def place(d, p):
+        ref, per, low, size = spans[p]
+        return ref.at[pl.ds(d * per + low, size)]
+
+    moves = Spread(q, own, place, send_sem, recv_sem)
+    last_rows = v_ref.at[pl.ds(v_ref.shape[0] - minus_ref.shape[0], minus_ref.shape[0])]
+    passed = [pltpu.make_async_remote_copy(src_ref=src, dst_ref=dst, send_sem=pass_send.at[i], recv_sem=pass_recv.at[i], device_id={"tp": to}, device_id_type=MESH)
+              for i, (src, dst, to) in enumerate(((last_rows, minus_ref, q.plus), (last_rows, plus_ref, q.minus), (w_ref, w_par_ref, q.partner), (b_ref, b_par_ref, q.partner)))]
+    work.load(0).start()
+    q.greet((q.plus, q.minus, q.partner))
+    moves.begin(0)
+    moves.begin(1)
+    for ref, low, size in ((ua, 0, soon), (ub, soon, late)):
+        @pl.loop(0, size // 8)
+        def _(k):
+            for r in range(8):
+                ref[me * size + k * 8 + r] = rows_ref[low + k * 8 + r]
+    for c in passed[2:]:
+        c.start()
+    moves.turn(0)
+    moves.turn(1)
+    moves.begin(2)
+    for p in range(2):
+        moves.last(p)
+    for p in range(2):
+        moves.finish(p)
+
+    def first(i):
+        return ua[i]
+
+    def any_(i):
+        here = i < n * soon
+        a, b = ua[jnp.minimum(i, n * soon - 1)], ub[jnp.maximum(i - n * soon, 0)]
+        return jnp.where(here, a.astype(jnp.float32), b.astype(jnp.float32))
+
+    blocks = early // TOKENS
+    work.run(0, blocks - 2, first)
+    moves.turn(2)
+    for c in passed[:2]:
+        c.start()
+    work.run(blocks - 2, blocks, first)
+    moves.last(2)
+    moves.finish(2)
+    work.run(blocks, work.blocks, any_)
+    work.close(any_)
+    for c in passed:
+        c.wait()
+
+
+def broadcast(n, soon, early, at, rows, pos, gain, bias, v, last, w, b, cid=3):
+    seq, D = pos.shape
+    cap, T, L = rows.shape
+    A = pl.BlockSpec(memory_space=pl.ANY)
+    V = pl.BlockSpec(memory_space=pltpu.VMEM)
+    sems = pltpu.SemaphoreType.DMA((Spread.CHANNELS, 3))
+    of = lambda r: jax.ShapeDtypeStruct((r, D), v.dtype)
+    return pl.pallas_call(
+        functools.partial(broadcast_kernel, n, soon, early),
+        out_shape=(jax.ShapeDtypeStruct((seq, D), jnp.bfloat16), jax.ShapeDtypeStruct((2, seq // n, D), jnp.bfloat16),
+                   of(last), of(last), jax.ShapeDtypeStruct(w.shape, w.dtype), jax.ShapeDtypeStruct(b.shape, b.dtype)),
+        grid_spec=pltpu.PrefetchScalarGridSpec(
+            num_scalar_prefetch=1, grid=(), in_specs=[V, A, V, V, A, A, V], out_specs=(A, A, A, A, A, V),
+            scratch_shapes=[pltpu.VMEM((n * soon, T, L), rows.dtype), pltpu.VMEM((n * (cap - soon), T, L), rows.dtype), *Norm.scratch(D), sems, sems, *[pltpu.SemaphoreType.DMA((4,))] * 2]),
+        compiler_params=pltpu.CompilerParams(vmem_limit_bytes=VMEM, collective_id=cid, has_side_effects=True),
+        name="broadcast",
+    )(at, rows, pos, gain, bias, v, w, b)
+
+
+def norm_kernel(at, x_hbm, pos_hbm, gain_ref, bias_ref, h_ref, emb_ref, x, sem, *rest):
+    me = lax.axis_index("tp")
+    work = Norm(me, lax.rem(me, 2), at, pos_hbm, gain_ref, bias_ref, h_ref, emb_ref, *rest)
+    work.load(0).start()
+    c = pltpu.make_async_copy(x_hbm, x, sem)
+    c.start()
+    c.wait()
+    work.run(0, work.blocks, lambda i: x[i])
+    work.close(lambda i: x[i])
+
+
+def norm(n, at, x, pos, gain, bias):
+    seq, D = pos.shape
+    A = pl.BlockSpec(memory_space=pl.ANY)
+    V = pl.BlockSpec(memory_space=pltpu.VMEM)
+    return pl.pallas_call(
+        norm_kernel,
+        out_shape=(jax.ShapeDtypeStruct((seq, D), jnp.bfloat16), jax.ShapeDtypeStruct((2, seq // n, D), jnp.bfloat16)),
+        grid_spec=pltpu.PrefetchScalarGridSpec(
+            num_scalar_prefetch=1, grid=(), in_specs=[A, A, V, V], out_specs=(A, A),
+            scratch_shapes=[pltpu.VMEM(x.shape, x.dtype), pltpu.SemaphoreType.DMA, *Norm.scratch(D)]),
+        compiler_params=pltpu.CompilerParams(vmem_limit_bytes=VMEM),
+        name="norm",
+    )(at, x, pos, gain, bias)
+
+
+def project_kernel(chunk, wa_hbm, wb_hbm, ba_ref, bb_ref, emb_hbm, h_ref, qkv_ref, emb_out, w, bc, emb, wsem, esem):
+    step = pl.program_id(0)
+    core = lax.rem(lax.axis_index("tp"), 2)
+    M = wa_hbm.shape[0]
+    tb = h_ref.shape[0]
+
+    def load(k):
+        return pltpu.make_async_copy((wa_hbm, wb_hbm)[k], w.at[lax.rem(core + k, 2)], wsem.at[lax.rem(core + k, 2)])
+
+    def loaded(k):
+        return pltpu.make_async_copy(wa_hbm, w.at[k], wsem.at[k])
 
     @pl.when(step == 0)
     def _():
-        load_u().start()
-        heads, E = 12, M // 12
+        for k in range(2):
+            load(k).start()
+        pltpu.make_async_copy(emb_hbm, emb, esem).start()
+        _, H, E = ba_ref.shape
         for k, b in enumerate((ba_ref, bb_ref)):
-            for r in range(heads):
-                bc[lax.rem(q.core + k, 2), r * E:(r + 1) * E, :] = jnp.broadcast_to(b[r:r + 1, :], (128, 128)).T[0:E, :]
-        load_pos(0).start()
-        for k in range(2):
-            load_w(k).start()
-        load_pos(1).start()
-        load_u().wait()
-        load_pos(0).wait()
-        @pl.loop(0, tb // 64)
-        def _(g):
-            for j in range(4):
-                norm(0, g * 4 + j, j)
-        for k in range(2):
-            load_w(k).wait()
-
-    def sweep(beside):
-        per = M // chunk
-        h = hs.at[lax.rem(step, 2)]
-        for k in range(2):
-            @pl.loop(0, per)
-            def _(m):
-                at = pl.multiple_of(m * chunk, 32)
-                o = lax.dot_general(w[k, pl.ds(at, chunk), :], h[...], (((1,), (1,)), ((), ())), preferred_element_type=jnp.float32)
-                b = jnp.concatenate([bc[k, pl.ds(at, chunk), :]] * (tb // 128), axis=1)
-                qkv_ref[k, pl.ds(at, chunk), :] = (o + b).astype(jnp.bfloat16)
-                n = tb // 16 // (2 * per)
-                for j in range(n):
-                    beside((k * per + m) * n + j, j % 4)
-
-    @pl.when(step < steps - 1)
+            for r in range(3 * H):
+                bc[lax.rem(core + k, 2), r * E:(r + 1) * E, :] = jnp.broadcast_to(b[r // H, r % H:r % H + 1, :], (128, E)).T
+
+    @pl.when(step == 1)
     def _():
-        load_pos(step + 1).wait()
-        @pl.when(step + 2 < steps)
+        pltpu.make_async_copy(emb_hbm, emb, esem).wait()
+        pltpu.make_async_copy(emb, emb_out, esem).start()
+
+    @pl.when(step == pl.num_programs(0) - 1)
+    def _():
+        pltpu.make_async_copy(emb, emb_out, esem).wait()
+
+    for k in range(2):
+        @pl.when(step == 0)
         def _():
-            load_pos(step + 2).start()
-        @pl.when(step + 2 == steps)
-        def _():
-            load_own().start()
-        sweep(lambda g, j: norm(step + 1, g, j))
-
-    @pl.when(step == steps - 1)
-    def _():
-        load_own().wait()
-        sweep(embed)
-
-
-def project(n, at, u, pos, gain, bias, wa, wb, ba, bb, tb=512, chunk=288):
-    seq, D = pos.shape
-    blk = seq // n
-    steps = seq // tb
+            loaded(k).wait()
+        for m in range(0, M, chunk):
+            o = lax.dot_general(w[k, m:m + chunk, :], h_ref[...], (((1,), (1,)), ((), ())), preferred_element_type=jnp.float32)
+            b = jnp.concatenate([bc[k, m:m + chunk, :]] * (tb // 128), axis=1)
+            qkv_ref[k, m:m + chunk, :] = (o + b).astype(jnp.bfloat16)
+
+
+def project(h, emb, wa, wb, ba, bb, tb=512, chunk=384):
+    seq, D = h.shape
     M = wa.shape[0]
     A = pl.BlockSpec(memory_space=pl.ANY)
-    one = lambda shape: pl.BlockSpec(shape, lambda i, *_: (0,) * len(shape), pipeline_mode=pl.Buffered(1))
+    one = lambda shape: pl.BlockSpec(shape, lambda i: (0,) * len(shape), pipeline_mode=pl.Buffered(1))
     return pl.pallas_call(
-        functools.partial(project_kernel, n, tb, seq, blk, steps, chunk),
-        out_shape=(jax.ShapeDtypeStruct((2, M, seq), jnp.bfloat16), jax.ShapeDtypeStruct((2, blk, D), jnp.bfloat16)),
-        grid_spec=pltpu.PrefetchScalarGridSpec(
-            num_scalar_prefetch=1, grid=(steps,),
-            in_specs=[A, A, one((1, D)), one((1, D)), A, A, one(ba.shape), one(bb.shape)],
-            out_specs=(pl.BlockSpec((2, M, tb), lambda i, *_: (0, 0, i)), pl.BlockSpec((2, blk, D), lambda i, *_: (0, 0, 0), pipeline_mode=pl.Buffered(1))),
-            scratch_shapes=[pltpu.VMEM(u.shape, u.dtype), pltpu.VMEM((2, M, D), wa.dtype), pltpu.VMEM((2, M, 128), jnp.float32), pltpu.VMEM((2, tb, D), pos.dtype),
-                            pltpu.VMEM((8, D // 128 * 8, 128), jnp.float32), pltpu.VMEM((2, tb, D), jnp.bfloat16),
-                            pltpu.SemaphoreType.DMA, pltpu.SemaphoreType.DMA((2,)), pltpu.SemaphoreType.DMA((2,))]),
-        compiler_params=pltpu.CompilerParams(vmem_limit_bytes=63 * 2**20),
+        functools.partial(project_kernel, chunk),
+        out_shape=(jax.ShapeDtypeStruct((2, M, seq), jnp.bfloat16), jax.ShapeDtypeStruct(emb.shape, emb.dtype)),
+        grid=(seq // tb,),
+        in_specs=[A, A, one(ba.shape), one(bb.shape), A, pl.BlockSpec((tb, D), lambda i: (i, 0))],
+        out_specs=(pl.BlockSpec((2, M, tb), lambda i: (0, 0, i)), A),
+        scratch_shapes=[pltpu.VMEM((2, M, D), wa.dtype), pltpu.VMEM((2, M, 128), jnp.float32), pltpu.VMEM(emb.shape, emb.dtype), pltpu.SemaphoreType.DMA((2,)), pltpu.SemaphoreType.DMA],
+        compiler_params=pltpu.CompilerParams(vmem_limit_bytes=VMEM),
         cost_estimate=pl.CostEstimate(flops=4 * seq * M * D, bytes_accessed=50 * 2**20, transcendentals=0),
         name="project",
-    )(at, u, pos, gain, bias, wa, wb, ba, bb)
+    )(wa, wb, ba, bb, emb, h)
 
 
 def attend_kernel(n, scale, qb, nb, early, where, qkv_ref, emb_hbm, bias_ref, *refs):
@@ -524,14 +705,12 @@
             for s in range(n):
                 for k in range(low, high, 128):
                     for t in range(0, qb, 128):
-                        a[(s % 2) * qb + t:(s % 2) * qb + t + 128, (s // 2) * K + k:(s // 2) * K + k + 128] = got[s, k:k + 128, t:t + 128].astype(jnp.float32).T.astype(jnp.bfloat16)
+                        at = s // 2 * (high - low) + (k - low) + (n // 2) * low
+                        a[(s % 2) * qb + t:(s % 2) * qb + t + 128, at:at + 128] = got[s, k:k + 128, t:t + 128].astype(jnp.float32).T.astype(jnp.bfloat16)
 
         def part(low, high, cols):
-            o = None
-            for i in range(n // 2):
-                d = jnp.dot(a[:, i * K + low:i * K + high], w[2 * i:2 * i + 2, :, cols].reshape(K, nb)[low:high], preferred_element_type=jnp.float32)
-                o = d if o is None else o + d
-            return o
+            rows = [w[2 * i:2 * i + 2, :, cols].reshape(K, nb)[low:high] for i in range(n // 2)]
+            return jnp.dot(a[:, n // 2 * low:n // 2 * high], jnp.concatenate(rows, axis=0), preferred_element_type=jnp.float32)
 
         arrive(0, 0, early * E)
         turn_over(0, cut)
@@ -559,7 +738,7 @@
             pltpu.make_async_remote_copy(src_ref=r, dst_ref=r, send_sem=send_sem.at[s], recv_sem=recv_sem.at[0, s], device_id={"tp": q.partner}, device_id_type=MESH).wait_send()
 
 
-def attend(n, qkv, pieces, where, emb, bias, early=6, nb=256, cid=1, qb=256):
+def attend(n, qkv, pieces, where, emb, bias, early=6, nb=1024, cid=1, qb=256):
     heads, E, S = 2 * qkv.shape[2], *qkv.shape[3:]
     H = heads // 2
     D = emb.shape[2]
@@ -576,12 +755,13 @@
                         pltpu.VMEM((heads, n, E, qb), bf), pltpu.VMEM((n, heads * E, qb), bf), pltpu.VMEM((n, H * E, D), bf), pltpu.VMEM((2 * qb, n * H * E), bf),
                         pltpu.VMEM((2 * qb, D), jnp.float32), pltpu.VMEM(emb.shape, bf),
                         *[pltpu.SemaphoreType.DMA((len(pieces),))] * 3, pltpu.SemaphoreType.DMA, pltpu.SemaphoreType.DMA((n,)), pltpu.SemaphoreType.DMA((2, n))],
-        compiler_params=pltpu.CompilerParams(collective_id=cid, has_side_effects=True, vmem_limit_bytes=62 * 2**20),
+        compiler_params=pltpu.CompilerParams(collective_id=cid, has_side_effects=True, vmem_limit_bytes=VMEM),
         name="attend",
     )(qkv, emb, bias, *pieces)
 
 
 CAP = 264
+SOON, EARLY = 200, 1280
 
 
 def place_kernel(code_ref, u_ref, x_ref, out_ref, sem):
@@ -616,48 +796,54 @@
         H, E = w_qkv.shape[2:]
         shard_rows = word_shard.shape[0]
         w_own = jnp.transpose(w_qkv, (1, 2, 3, 0)).reshape(3 * H * E, D)
-        b_own = jnp.pad(b_qkv.reshape(3 * H, E), ((0, 4), (0, 128 - E)))
         v_own = w_out.reshape(H * E, D)
-        swap = [(d, d ^ 1) for d in range(n)]
         ring = lambda step: [(d, (d + 2 * step) % n) for d in range(n)]
-        w_par, b_par = lax.ppermute(w_own, "tp", swap), lax.ppermute(b_own, "tp", swap)
         send = lambda x, step: lax.ppermute(x, "tp", ring(step))
-        v0, v1, v2 = w_out[0], w_out[1], w_out[2:].reshape((H - 2) * E, D)
-        minus0, plus0, minus1, plus1 = send(v0, 1), send(v0, -1), send(v1, 1), send(v1, -1)
+        v_head = w_out[:2].reshape(2 * E, D)
+        minus0, plus0 = send(v_head, 1), send(v_head, -1)
         blk = seq // n
+        gain, bias = ln_gain[None], ln_bias[None]
+        code, at, counts, mine = pick(n, shard_rows, CAP, SOON, EARLY, token_ids, word_shard)
+        h, embed, minus1, plus1, w_par, b_par = broadcast(n, SOON, EARLY, at.reshape(-1), mine, pos_table, gain, bias, v_own, (H - 2) * E, w_own, b_qkv)
+        counts, h = lax.optimization_barrier((counts, h))
+
+        rounds = jnp.where((counts[0, 0] > CAP) | (counts[1, 0] > SOON), (counts[0, 0] + CAP - 1) // CAP, 0)
         total = max(n * CAP, seq + blk)
-        code, at, most, u = pick(n, shard_rows, CAP, token_ids, word_shard)
-        code, at, most = code.reshape(-1), at.reshape(-1), most[0, 0]
-        u = gather_all(n, u, total)
-
-        rounds = jnp.where(most > CAP, (most + CAP - 1) // CAP, 0)
+
+        def by_token(x):
+            return x.reshape(seq // 128, 2, 128).transpose(1, 0, 2)
 
         def wanted(x):
-            x = x.reshape(2, seq)
             own = lax.dynamic_index_in_dim(x, core, 0, keepdims=False)
             other = lax.dynamic_index_in_dim(x, 1 - core, 0, keepdims=False)
             return jnp.concatenate([own, lax.dynamic_slice_in_dim(other, me * blk, blk)])
 
-        t = jnp.arange(2 * seq, dtype=jnp.int32)
-        t = jnp.where(t // seq == core, t % seq, jnp.clip(t % seq - me * blk, 0, blk - 1) + seq)
-
         def more(carry):
-            r, u, _ = carry
-            slot = code % SPAN - r * CAP
-            hit = (slot >= 0) & (slot < CAP)
-            mine = jnp.where(hit & (code // SPAN == me), slot, -1)
-            ids = token_ids.reshape(-1) - me * shard_rows
-            chosen = jnp.max(jnp.where(mine[None, :] == jnp.arange(CAP)[:, None], ids[None, :], 0), axis=1)
-            v = gather_all(n, rows(CAP, chosen, word_shard), total)
-            return r + 1, place(wanted(jnp.where(hit, code // SPAN * CAP + slot, -1)), v, u), t
-
-        _, u, at = lax.while_loop(lambda c: c[0] < rounds, more, (jnp.int32(0), u, at))
-
-        v2, minus0_, plus1_, u = lax.optimization_barrier((v2, minus0, plus1, u))
-        minus2, plus2, opp0, opp1, opp2 = send(v2, 1), send(v2, -1), send(minus0_, 1), send(plus1_, -1), send(v2, 2)
-        pieces = [v_own, minus0, plus0, minus1, plus1, minus2, plus2, opp0, opp1, opp2]
-        where = ((0, 0), (-1, 0), (1, 0), (-1, E), (1, E), (-1, 2 * E), (1, 2 * E), (2, 0), (2, E), (2, 2 * E))
-        qkv, embed = project(n, at, u, pos_table, ln_gain[None], ln_bias[None], w_own, w_par, b_own, b_par)
+            def one_round(carry):
+                r, x = carry
+                codes = by_token(code).reshape(2, seq)
+                slot = codes % SPAN - r * CAP
+                hit = (slot >= 0) & (slot < CAP)
+                here = jnp.where(hit & (codes // SPAN == me), slot, -1).reshape(-1)
+                ids = token_ids.reshape(-1) - me * shard_rows
+                chosen = jnp.max(jnp.where(here[None, :] == jnp.arange(CAP)[:, None], ids[None, :], 0), axis=1)
+                v = gather_all(n, rows(CAP, chosen, word_shard), total)
+                return r + 1, place(wanted(jnp.where(hit, codes // SPAN * CAP + slot, -1)), v, x)
+
+            x = jnp.zeros((total,) + mine.shape[1:], mine.dtype)
+            _, x = lax.while_loop(lambda c: c[0] < rounds, one_round, (jnp.int32(0), x))
+            t = jnp.arange(seq, dtype=jnp.int32)
+            t = jnp.stack([jnp.where(core == b, t, jnp.clip(t - me * blk, 0, blk - 1) + seq) for b in range(2)])
+            t = t.reshape(2, seq // 128, 128).transpose(1, 0, 2).reshape(-1)
+            return (jnp.int32(0),) + tuple(norm(n, t, x, pos_table, gain, bias))
+
+        _, h, embed = lax.while_loop(lambda c: c[0] > 0, more, (rounds, h, embed))
+
+        minus0, h = lax.optimization_barrier((minus0, h))
+        opp0, opp1 = send(minus0, 1), send(plus1, -1)
+        pieces = [v_own, minus0, plus0, minus1, plus1, opp0, opp1]
+        where = ((0, 0), (-1, 0), (1, 0), (-1, 2 * E), (1, 2 * E), (2, 0), (2, 2 * E))
+        qkv, embed = project(h, embed, w_own, w_par, b_qkv, b_par)
         resid_out = attend(n, qkv.reshape(2, 3, H, E, seq), pieces, where, embed, b_out[None])
         return resid_out, embed
 

time: 225 us -> 218 us (0.969)
  starting transfers between devices: 13.5 us -> 5.6 us
  local copies, waits for them, and re-layouts: 8.94 us -> 6.67 us
    pallas_call x3, Pallas kernels: 145 us -> 151 us  [the longest x1 89.6 us: broadcast(): pl.pallas_call(functools.partial(broadcast_kernel, n, soon, early), out_s...]
    ppermute x9 -> x4, starting transfers between devices: 11.1 us -> 5.6 us  [local_step(): send = lambda x, step: lax.ppermute(x, 'tp', ring(step))]
    pallas_call x1, Pallas kernels: 54.2 us -> 50 us  [attend(): pl.pallas_call(functools.partial(attend_kernel, n, E ** (-0.5), qb, nb, e...]
    ppermute x2 -> x0, starting transfers between devices: 2.36 us -> none  [the longest x1 2.11 us: local_step(): lax.ppermute(w_own, 'tp', swap)]
    squeeze x1 -> x0, local copies, waits for them, and re-layouts: 2.34 us -> none  [local_step(): v0, v1, v2 = (w_out[0], w_out[1], w_out[2:].reshape((H - 2) * E, D))]
    unnamed x13 -> x9, local copies, waits for them, and re-layouts: 5.44 us -> 3.77 us
  transfers between devices with their start and end apart: 11 -> 4, of which waited for: 0 -> 0; matrix products, arithmetic and copies ran while one was open for 1% -> 0% of each run, Pallas kernels for 65% -> 70%
where the time goes in v4:
time: 218 us; the launch traced here: 216 us
  Pallas kernels  201 us (92%)
  local copies, waits for them, and re-layouts  6.67 us (3%)
  starting transfers between devices  5.6 us (3%)
  between operations  2.74 us (1%)
    pallas_call x1, Pallas kernels, broadcast(): pl.pallas_call(functools.partial(broadcast_kernel, n, soon, early), out_s...  89.6 us
    pallas_call x1, Pallas kernels, attend(): pl.pallas_call(functools.partial(attend_kernel, n, E ** (-0.5), qb, nb, e...  50 us
    pallas_call x1, Pallas kernels, project(): pl.pallas_call(functools.partial(project_kernel, chunk), out_shape=(jax.S...  39.6 us
    pallas_call x1, Pallas kernels, pick(): pl.pallas_call(functools.partial(pick_kernel, n, shard_rows, cap, soon, e...  22 us
    ppermute x4, starting transfers between devices, local_step(): send = lambda x, step: lax.ppermute(x, 'tp', ring(step))  5.6 us
  transfers between devices with their start and end apart: 4, of which 0 were waited for; matrix products, arithmetic and copies ran while one was open for 0% of the time, Pallas kernels for 70%

profile of v4, /device:TPU:81, one launch (start us, length us, event | category | flops | bytes accessed | tf_op | source)
XLA Modules:
  0.0 216.2 jit_solution(4767795653167726931)
XLA Ops:
  0.6 2.4 %slice.12 = bf16[2,96,3072]{2,1,0:T(8,128)(2,1)} slice(bf16[4,96,3072]{2,1,0:T(8,128)(2,1)} %param.20), slice={[0:2], [0:96], [0:3072]} | slice | bytes 2359296 | tf_op jit(solution)/shard_map/slice | solution.py:802
  3.0 0.0 copy-start.1
  3.0 0.0 copy-start.2
  3.0 2.2 %collective-permute-start = (bf16[192,3072]{1,0:T(8,128)(2,1)}, bf16[192,3072]{1,0:T(8,128)(2,1)}, u32[]{:S(2)}, u32[]{:S(2)}) collective-permute-start(bf16[192,3072]{1,0:T(8,128)(2,1)} %bitcast.30), channel_id=1, source_target_pairs={{0,2},{1,3},{2,4},{3,5},{4,6},{5,7},{6,0},{7,1},{8,10},{9,11},{10,... | collective-permute-start | bytes 3538952 | tf_op jit(solution)/shard_map/ppermute | solution.py:801
  5.2 1.6 collective-permute-start.1
  6.8 22.0 %pick.1 = (s32[32,128]{1,0:T(8,128)S(1)}, s32[32,128]{1,0:T(8,128)}, s32[2,128]{1,0:T(2,128)}, bf16[264,24,128]{2,1,0:T(8,128)(2,1)}) custom-call(s32[2,2048]{1,0:T(2,128)} %ids_ref.1, bf16[6400,3072]{1,0:T(8,128)(2,1)} %table_ref.1), custom_call_target="tpu_custom_call" | custom-call | flops 20000000000 | bytes 12976128 | tf_op jit(solution)/shard_map/pick/pallas_call | solution.py:316
  28.8 0.0 copy-done.1
  28.8 0.0 copy-done.2
  28.8 0.0 copy-start.3
  28.8 0.0 copy-start
  28.8 89.6 %broadcast.321 = (bf16[2048,3072]{1,0:T(8,128)(2,1)}, bf16[2,256,3072]{2,1,0:T(8,128)(2,1)}, bf16[192,3072]{1,0:T(8,128)(2,1)}, bf16[192,3072]{1,0:T(8,128)(2,1)...) custom-call(s32[4096]{0:T(1024)} %bitcast.97, bf16[264,24,128]{2,1,0:T(8,128)(2,1)} %get-tuple-element.420.rows_ref, ...), custom_call_target="tpu_custom_call" | custom-call | tf_op jit(solution)/shard_map/broadcast/pallas_call | solution.py:521
  118.5 0.1 collective-permute-start.3
  118.6 0.0 copy-done.3
  118.6 0.5 fusion.11
  121.1 0.0 copy-done
  121.1 0.0 collective-permute-done.refs_1_
  121.1 1.7 collective-permute-start.2
  122.8 39.6 %project.1 = (bf16[2,1152,2048]{2,1,0:T(8,128)(2,1)}, bf16[2,256,3072]{2,1,0:T(8,128)(2,1)}) custom-call(bf16[1152,3072]{1,0:T(8,128)(2,1)} %bitcast.88, bf16[1152,3072]{1,0:T(8,128)(2,1)} %get-tuple-element.421.wb_hbm, f32[3,4,96]{2,1,0:T(4,128)} %ba_ref.1, f32[3,4,96]{2,1,0:T(4,128)} %get-tuple-element.422.bb_ref, ...), custom_call_target="tpu_custom_call" | custom-call | flops 28991029248 | bytes 52428800 | tf_op jit(solution)/shard_map/project/pallas_call | solution.py:605
  162.4 0.0 collective-permute-done.3.refs_6_
  162.4 0.0 collective-permute-done.1.refs_2_
  162.4 0.0 collective-permute-done.2.refs_5_
  162.4 50.0 %attend.1 = bf16[2,256,3072]{2,1,0:T(8,128)(2,1)} custom-call(bf16[2,3,4,96,2048]{4,3,2,1,0:T(8,128)(2,1)} %bitcast.86, bf16[2,256,3072]{2,1,0:T(8,128)(2,1)} %get-tuple-element.712.emb_hbm, f32[1,3072]{1,0:T(1,128)} %bitcast.98, bf16[384,3072]{1,0:T(8,128)(2,1)} %bitcast.84, bf16[192,3072]{1,0:T(8,128)(2,1)} %collective-permute-done.refs_1_, ...), custom_call_target="tpu_custom_call" | custom-call | tf_op jit(solution)/shard_map/attend/pallas_call | solution.py:748
  212.4 3.8 %copy.62 = bf16[2,256,3072]{2,1,0:T(8,128)(2,1)} copy(bf16[2,256,3072]{2,1,0:T(8,128)(2,1)} %attend.1) | data formatting | bytes 6291456
  (1 shorter events, 0.0 us)
Async XLA Ops:
  3.0 25.8 %copy-start.1 = (f32[3072]{0:T(1024)S(1)}, f32[3072]{0:T(1024)}, u32[]{:S(2)}) copy-start(f32[3072]{0:T(1024)} %param.16) | copy-start | bytes 36868
  3.0 25.8 %copy-start.2 = (f32[3072]{0:T(1024)S(1)}, f32[3072]{0:T(1024)}, u32[]{:S(2)}) copy-start(f32[3072]{0:T(1024)} %param.17) | copy-start | bytes 36868
  3.0 118.1 %collective-permute-start = (bf16[192,3072]{1,0:T(8,128)(2,1)}, bf16[192,3072]{1,0:T(8,128)(2,1)}, u32[]{:S(2)}, u32[]{:S(2)}) collective-permute-start(bf16[192,3072]{1,0:T(8,128)(2,1)} %bitcast.30), channel_id=1, source_target_pairs={{0,2},{1,3},{2,4},{3,5},{4,6},{5,7},{6,0},{7,1},{8,10},{9,11},{10,... | collective-permute-start | bytes 3538952 | tf_op jit(solution)/shard_map/ppermute | solution.py:801
  5.2 157.2 %collective-permute-start.1 = (bf16[192,3072]{1,0:T(8,128)(2,1)}, bf16[192,3072]{1,0:T(8,128)(2,1)}, u32[]{:S(2)}, u32[]{:S(2)}) collective-permute-start(bf16[192,3072]{1,0:T(8,128)(2,1)} %bitcast.30), channel_id=1, source_target_pairs={{0,6},{1,7},{2,0},{3,1},{4,2},{5,3},{6,4},{7,5},{8,14},{9,15},{10,... | collective-permute-start | bytes 3538952 | tf_op jit(solution)/shard_map/ppermute | solution.py:801
  28.8 89.8 %copy-start.3 = (s32[2,128]{1,0:T(2,128)S(1)}, s32[2,128]{1,0:T(2,128)}, u32[]{:S(2)}) copy-start(s32[2,128]{1,0:T(2,128)} %get-tuple-element.425) | copy-start | bytes 3076
  28.8 92.3 %copy-start = (s32[2,2048]{1,0:T(2,128)S(1)}, s32[2,2048]{1,0:T(2,128)}, u32[]{:S(2)}) copy-start(s32[2,2048]{1,0:T(2,128)} %ids_ref.1) | copy-start | bytes 49156
  118.5 43.9 %collective-permute-start.3 = (bf16[192,3072]{1,0:T(8,128)(2,1)}, bf16[192,3072]{1,0:T(8,128)(2,1)}, u32[]{:S(2)}, u32[]{:S(2)}) collective-permute-start(bf16[192,3072]{1,0:T(8,128)(2,1)} %get-tuple-element.436.refs_4_), channel_id=1, source_target_pairs={{0,6},{1,7},{2,0},{3,1},{4,2},{5,3},{6,4},{7,5},{8,14},{9,15},{10,... | collective-permute-start | bytes 3538952 | tf_op jit(solution)/shard_map/ppermute | solution.py:801
  121.1 41.3 %collective-permute-start.2 = (bf16[192,3072]{1,0:T(8,128)(2,1)}, bf16[192,3072]{1,0:T(8,128)(2,1)}, u32[]{:S(2)}, u32[]{:S(2)}) collective-permute-start(bf16[192,3072]{1,0:T(8,128)(2,1)} %collective-permute-done.refs_1_), channel_id=1, source_target_pairs={{0,2},{1,3},{2,4},{3,5},{4,6},{5,7},{6,0},{7,1},{8,10},{9,11},{10,... | collective-permute-start | bytes 3538952 | tf_op jit(solution)/shard_map/ppermute | solution.py:801

commit v5 on v4

--- a/solution.py
+++ b/solution.py
@@ -449,11 +449,11 @@
 
 
 def broadcast_kernel(n, soon, early, at, rows_ref, pos_hbm, gain_ref, bias_ref, v_ref, w_ref, b_ref,
-                     h_ref, emb_ref, minus_ref, plus_ref, w_par_ref, b_par_ref, ua, ub, *rest):
-    send_sem, recv_sem, pass_send, pass_recv = rest[-4:]
+                     h_ref, emb_ref, minus_ref, plus_ref, w_par_ref, b_par_ref, rest_ref, ua, ub, *rest):
+    send_sem, recv_sem, pass_send, pass_recv, vbuf, vsem = rest[-6:]
     q = Peers(n)
     me = q.me
-    work = Norm(me, q.core, at, pos_hbm, gain_ref, bias_ref, h_ref, emb_ref, *rest[:-4])
+    work = Norm(me, q.core, at, pos_hbm, gain_ref, bias_ref, h_ref, emb_ref, *rest[:-6])
     cap = rows_ref.shape[0]
     late = cap - soon
     spans = ((ua, soon, 0, soon // 2), (ua, soon, soon // 2, soon // 2), (ub, late, 0, late))
@@ -467,7 +467,10 @@
         return ref.at[pl.ds(d * per + low, size)]
 
     moves = Spread(q, own, place, send_sem, recv_sem)
-    last_rows = v_ref.at[pl.ds(v_ref.shape[0] - minus_ref.shape[0], minus_ref.shape[0])]
+    left = vbuf.shape[0]
+    last_rows = v_ref.at[pl.ds(v_ref.shape[0] - left - minus_ref.shape[0], minus_ref.shape[0])]
+    rest_in = pltpu.make_async_copy(v_ref.at[pl.ds(v_ref.shape[0] - left, left)], vbuf, vsem)
+    rest_out = pltpu.make_async_copy(vbuf, rest_ref, vsem)
     passed = [pltpu.make_async_remote_copy(src_ref=src, dst_ref=dst, send_sem=pass_send.at[i], recv_sem=pass_recv.at[i], device_id={"tp": to}, device_id_type=MESH)
               for i, (src, dst, to) in enumerate(((last_rows, minus_ref, q.plus), (last_rows, plus_ref, q.minus), (w_ref, w_par_ref, q.partner), (b_ref, b_par_ref, q.partner)))]
     work.load(0).start()
@@ -481,6 +484,9 @@
                 ref[me * size + k * 8 + r] = rows_ref[low + k * 8 + r]
     for c in passed[2:]:
         c.start()
+    rest_in.start()
+    rest_in.wait()
+    rest_out.start()
     moves.turn(0)
     moves.turn(1)
     moves.begin(2)
@@ -509,9 +515,10 @@
     work.close(any_)
     for c in passed:
         c.wait()
-
-
-def broadcast(n, soon, early, at, rows, pos, gain, bias, v, last, w, b, cid=3):
+    rest_out.wait()
+
+
+def broadcast(n, soon, early, at, rows, pos, gain, bias, v, last, left, w, b, cid=3):
     seq, D = pos.shape
     cap, T, L = rows.shape
     A = pl.BlockSpec(memory_space=pl.ANY)
@@ -521,10 +528,10 @@
     return pl.pallas_call(
         functools.partial(broadcast_kernel, n, soon, early),
         out_shape=(jax.ShapeDtypeStruct((seq, D), jnp.bfloat16), jax.ShapeDtypeStruct((2, seq // n, D), jnp.bfloat16),
-                   of(last), of(last), jax.ShapeDtypeStruct(w.shape, w.dtype), jax.ShapeDtypeStruct(b.shape, b.dtype)),
+                   of(last), of(last), jax.ShapeDtypeStruct(w.shape, w.dtype), jax.ShapeDtypeStruct(b.shape, b.dtype), of(left)),
         grid_spec=pltpu.PrefetchScalarGridSpec(
-            num_scalar_prefetch=1, grid=(), in_specs=[V, A, V, V, A, A, V], out_specs=(A, A, A, A, A, V),
-            scratch_shapes=[pltpu.VMEM((n * soon, T, L), rows.dtype), pltpu.VMEM((n * (cap - soon), T, L), rows.dtype), *Norm.scratch(D), sems, sems, *[pltpu.SemaphoreType.DMA((4,))] * 2]),
+            num_scalar_prefetch=1, grid=(), in_specs=[V, A, V, V, A, A, V], out_specs=(A, A, A, A, A, V, A),
+            scratch_shapes=[pltpu.VMEM((n * soon, T, L), rows.dtype), pltpu.VMEM((n * (cap - soon), T, L), rows.dtype), *Norm.scratch(D), sems, sems, *[pltpu.SemaphoreType.DMA((4,))] * 2, pltpu.VMEM((left, D), v.dtype), pltpu.SemaphoreType.DMA]),
         compiler_params=pltpu.CompilerParams(vmem_limit_bytes=VMEM, collective_id=cid, has_side_effects=True),
         name="broadcast",
     )(at, rows, pos, gain, bias, v, w, b)
@@ -616,7 +623,7 @@
 
 
 def attend_kernel(n, scale, qb, nb, early, where, qkv_ref, emb_hbm, bias_ref, *refs):
-    pieces, (out_ref, kk, vv, sc, ctx, got, w, a, acc, emb, load_sem, pass_send, pass_recv, emb_sem, send_sem, recv_sem) = refs[:len(where)], refs[len(where):]
+    pieces, (out_ref, kk, vv, sc, ctx, got, w, a, acc, emb, load_sem, pass_send, pass_recv, emb_sem, send_sem, recv_sem, turn_send, turn_recv) = refs[:len(where)], refs[len(where):]
     E, S = qkv_ref.shape[3:]
     heads = got.shape[1] // E
     N = S // qb
@@ -635,6 +642,16 @@
             cs.append(pltpu.make_async_remote_copy(src_ref=ref, dst_ref=dst, send_sem=pass_send.at[i], recv_sem=pass_recv.at[i], device_id={"tp": q.partner}, device_id_type=MESH))
         return cs
 
+    rest = pieces[-1].shape[0]
+    half = rest // 2
+
+    def across(i, owner, src, to, sem):
+        dst = w.at[owner, pl.ds(w.shape[1] - rest + i * half, half)]
+        return pltpu.make_async_remote_copy(src_ref=dst if src is None else src.at[pl.ds(i * half, half)], dst_ref=dst, send_sem=turn_send.at[sem], recv_sem=turn_recv.at[sem],
+                                            device_id={"tp": to}, device_id_type=MESH)
+
+    passing = ((q.minus, pieces[-2], q.plus), (q.plus, pieces[-1], q.minus))
+
     def send(h, s):
         to = lax.rem(me + s, n)
         return pltpu.make_async_remote_copy(src_ref=ctx.at[h, to], dst_ref=got.at[me, pl.ds(pl.multiple_of(h * E, 32), E)],
@@ -645,6 +662,8 @@
     @pl.when(head == 0)
     def _():
         q.greet([lax.rem(me + s, n) for s in range(1, n)])
+        for i, (owner, src, to) in enumerate(passing):
+            across(i, owner, src, to, i).start()
         vv[E:, :] = jnp.where(lax.broadcasted_iota(jnp.int32, (vv.shape[0] - E, S), 0) == 0, 1.0, 0.0).astype(jnp.bfloat16)
 
     @pl.when(head > 0)
@@ -657,6 +676,12 @@
         for c_ in loads():
             c_.start()
         load_emb.start()
+
+    @pl.when(head == 4)
+    def _():
+        for i in range(2):
+            across(i, q.opp, None, q.partner, i).wait_recv()
+            across(i, q.opp, None, q.partner, 2 + i).start()
 
     for t in range(0, S, 128):
         kk[t:t + 128, :] = qkv_ref[0, 1, 0, :, t:t + 128].astype(jnp.float32).T.astype(jnp.bfloat16)
@@ -717,6 +742,9 @@
         for c_ in loads():
             c_.wait()
         load_emb.wait()
+        for i, (owner, src, to) in enumerate(passing):
+            across(i, owner, src, to, i).wait_send()
+            across(i, q.other(q.opp), None, q.partner, 2 + i).wait()
 
         @pl.loop(0, w.shape[2] // nb)
         def _(j):
@@ -754,7 +782,7 @@
         scratch_shapes=[pltpu.VMEM((S, E), bf), pltpu.VMEM((E + 16, S), bf), pltpu.VMEM((2, S, qb), jnp.float32),
                         pltpu.VMEM((heads, n, E, qb), bf), pltpu.VMEM((n, heads * E, qb), bf), pltpu.VMEM((n, H * E, D), bf), pltpu.VMEM((2 * qb, n * H * E), bf),
                         pltpu.VMEM((2 * qb, D), jnp.float32), pltpu.VMEM(emb.shape, bf),
-                        *[pltpu.SemaphoreType.DMA((len(pieces),))] * 3, pltpu.SemaphoreType.DMA, pltpu.SemaphoreType.DMA((n,)), pltpu.SemaphoreType.DMA((2, n))],
+                        *[pltpu.SemaphoreType.DMA((len(pieces),))] * 3, pltpu.SemaphoreType.DMA, pltpu.SemaphoreType.DMA((n,)), pltpu.SemaphoreType.DMA((2, n)), *[pltpu.SemaphoreType.DMA((4,))] * 2],
         compiler_params=pltpu.CompilerParams(collective_id=cid, has_side_effects=True, vmem_limit_bytes=VMEM),
         name="attend",
     )(qkv, emb, bias, *pieces)
@@ -804,7 +832,8 @@
         blk = seq // n
         gain, bias = ln_gain[None], ln_bias[None]
         code, at, counts, mine = pick(n, shard_rows, CAP, SOON, EARLY, token_ids, word_shard)
-        h, embed, minus1, plus1, w_par, b_par = broadcast(n, SOON, EARLY, at.reshape(-1), mine, pos_table, gain, bias, v_own, (H - 2) * E, w_own, b_qkv)
+        mine, minus0, plus0 = lax.optimization_barrier((mine, minus0, plus0))
+        h, embed, minus1, plus1, w_par, b_par, v_tail = broadcast(n, SOON, EARLY, at.reshape(-1), mine, pos_table, gain, bias, v_own, (H - 3) * E, E, w_own, b_qkv)
         counts, h = lax.optimization_barrier((counts, h))
 
         rounds = jnp.where((counts[0, 0] > CAP) | (counts[1, 0] > SOON), (counts[0, 0] + CAP - 1) // CAP, 0)
@@ -840,9 +869,9 @@
         _, h, embed = lax.while_loop(lambda c: c[0] > 0, more, (rounds, h, embed))
 
         minus0, h = lax.optimization_barrier((minus0, h))
-        opp0, opp1 = send(minus0, 1), send(plus1, -1)
-        pieces = [v_own, minus0, plus0, minus1, plus1, opp0, opp1]
-        where = ((0, 0), (-1, 0), (1, 0), (-1, 2 * E), (1, 2 * E), (2, 0), (2, 2 * E))
+        minus2, plus2, opp0, opp1 = send(v_tail, 1), send(v_tail, -1), send(minus0, 1), send(plus1, -1)
+        pieces = [v_own, minus0, plus0, minus1, plus1, opp0, opp1, minus2, plus2]
+        where = ((0, 0), (-1, 0), (1, 0), (-1, 2 * E), (1, 2 * E), (2, 0), (2, 2 * E), (-1, (H - 1) * E), (1, (H - 1) * E))
         qkv, embed = project(h, embed, w_own, w_par, b_qkv, b_par)
         resid_out = attend(n, qkv.reshape(2, 3, H, E, seq), pieces, where, embed, b_out[None])
         return resid_out, embed

time: 218 us -> 216 us (level)
  Pallas kernels: 201 us -> 193 us
  waiting for transfers between devices: 0.01 us -> 3.19 us
  starting transfers between devices: 5.6 us -> 8.31 us
    pallas_call x1, Pallas kernels: 89.6 us -> 79.5 us  [broadcast(): pl.pallas_call(functools.partial(broadcast_kernel, n, soon, early), out_s...]
    ppermute x4 -> x6, waiting for transfers between devices: 0.01 us -> 3.19 us  [local_step(): send = lambda x, step: lax.ppermute(x, 'tp', ring(step))]
    ppermute x4 -> x6, starting transfers between devices: 5.6 us -> 8.31 us  [local_step(): send = lambda x, step: lax.ppermute(x, 'tp', ring(step))]
    unnamed x9 -> x15, local copies, waits for them, and re-layouts: 3.77 us -> 4.71 us
  transfers between devices with their start and end apart: 4 -> 6, of which waited for: 0 -> 1; matrix products, arithmetic and copies ran while one was open for 0% -> 0% of each run, Pallas kernels for 70% -> 29%
where the time goes in v5:
time: 216 us; the launch traced here: 215 us
  Pallas kernels  193 us (89%)
  starting transfers between devices  8.31 us (4%)
  local copies, waits for them, and re-layouts  7.59 us (4%)
  waiting for transfers between devices  3.19 us (1%)
  between operations  2.75 us (1%)
    pallas_call x1, Pallas kernels, broadcast(): pl.pallas_call(functools.partial(broadcast_kernel, n, soon, early), out_s...  79.5 us
    pallas_call x1, Pallas kernels, attend(): pl.pallas_call(functools.partial(attend_kernel, n, E ** (-0.5), qb, nb, e...  52.1 us
    pallas_call x1, Pallas kernels, project(): pl.pallas_call(functools.partial(project_kernel, chunk), out_shape=(jax.S...  39.6 us
    pallas_call x1, Pallas kernels, pick(): pl.pallas_call(functools.partial(pick_kernel, n, shard_rows, cap, soon, e...  22 us
    ppermute x6, starting transfers between devices, local_step(): send = lambda x, step: lax.ppermute(x, 'tp', ring(step))  8.31 us
    unnamed x15, local copies, waits for them, and re-layouts  4.71 us
  transfers between devices with their start and end apart: 6, of which 1 were waited for; matrix products, arithmetic and copies ran while one was open for 0% of the time, Pallas kernels for 29%

profile of v5, /device:TPU:81, one launch (start us, length us, event | category | flops | bytes accessed | tf_op | source)
XLA Modules:
  0.0 215.1 jit_solution(4628631071799708319)
XLA Ops:
  0.6 2.4 %slice.10 = bf16[2,96,3072]{2,1,0:T(8,128)(2,1)} slice(bf16[4,96,3072]{2,1,0:T(8,128)(2,1)} %param.20), slice={[0:2], [0:96], [0:3072]} | slice | bytes 2359296 | tf_op jit(solution)/shard_map/slice | solution.py:830
  3.0 2.2 %collective-permute-start = (bf16[192,3072]{1,0:T(8,128)(2,1)}, bf16[192,3072]{1,0:T(8,128)(2,1)}, u32[]{:S(2)}, u32[]{:S(2)}) collective-permute-start(bf16[192,3072]{1,0:T(8,128)(2,1)} %bitcast.23), channel_id=1, source_target_pairs={{0,2},{1,3},{2,4},{3,5},{4,6},{5,7},{6,0},{7,1},{8,10},{9,11},{10,... | collective-permute-start | bytes 3538952 | tf_op jit(solution)/shard_map/ppermute | solution.py:829
  5.2 1.5 collective-permute-start.1
  6.7 0.0 copy-start.2
  6.7 0.0 copy-start.4
  6.7 22.0 %pick.1 = (s32[32,128]{1,0:T(8,128)S(1)}, s32[32,128]{1,0:T(8,128)}, s32[2,128]{1,0:T(2,128)}, bf16[264,24,128]{2,1,0:T(8,128)(2,1)}) custom-call(s32[2,2048]{1,0:T(2,128)} %ids_ref.1, bf16[6400,3072]{1,0:T(8,128)(2,1)} %table_ref.1), custom_call_target="tpu_custom_call" | custom-call | flops 20000000000 | bytes 12976128 | tf_op jit(solution)/shard_map/pick/pallas_call | solution.py:316
  28.7 3.1 %collective-permute-done.refs_1_ = bf16[192,3072]{1,0:T(8,128)(2,1)} collective-permute-done((bf16[192,3072]{1,0:T(8,128)(2,1)}, bf16[192,3072]{1,0:T(8,128)(2,1)}, u32[]{:S(2)}, u32[]{:S(2)}) %collective-permute-start) | collective-permute-done | bytes 1179680 | tf_op jit(solution)/shard_map/ppermute | solution.py:829
  31.9 0.0 collective-permute-done.1.refs_2_
  31.9 0.0 copy-done.2
  31.9 0.0 copy-done.4
  31.9 0.0 copy-start.6
  31.9 0.0 copy-start
  31.9 0.0 copy-start.3
  31.9 0.0 copy-start.5
  31.9 79.5 %broadcast.321 = (bf16[2048,3072]{1,0:T(8,128)(2,1)}, bf16[2,256,3072]{2,1,0:T(8,128)(2,1)}, bf16[96,3072]{1,0:T(8,128)(2,1)}, bf16[96,3072]{1,0:T(8,128)(2,1)},...) custom-call(s32[4096]{0:T(1024)} %bitcast.97, ...), custom_call_target="tpu_custom_call" | custom-call | tf_op jit(solution)/shard_map/broadcast/pallas_call | solution.py:528
  111.4 0.0 copy-done.6
  111.5 0.5 fusion.11
  113.3 0.1 collective-permute-start.4
  113.4 2.6 %collective-permute-start.5 = (bf16[96,3072]{1,0:T(8,128)(2,1)}, bf16[96,3072]{1,0:T(8,128)(2,1)}, u32[]{:S(2)}, u32[]{:S(2)}) collective-permute-start(bf16[96,3072]{1,0:T(8,128)(2,1)} %get-tuple-element.444), channel_id=1, source_target_pairs={{0,6},{1,7},{2,0},{3,1},{4,2},{5,3},{6,4},{7,5},{8,14},{9,15},{10,... | collective-permute-start | bytes 1769480 | tf_op jit(solution)/shard_map/ppermute | solution.py:829
  116.7 0.0 copy-done
  116.7 0.0 copy-done.3
  116.7 0.0 copy-done.5
  116.7 0.0 copy-start.1
  116.8 0.1 collective-permute-start.2
  116.9 0.9 copy-done.1
  117.8 1.7 collective-permute-start.3
  119.5 39.6 %project.1 = (bf16[2,1152,2048]{2,1,0:T(8,128)(2,1)}, bf16[2,256,3072]{2,1,0:T(8,128)(2,1)}) custom-call(bf16[1152,3072]{1,0:T(8,128)(2,1)} %bitcast.88, bf16[1152,3072]{1,0:T(8,128)(2,1)} %get-tuple-element.426.wb_hbm, f32[3,4,96]{2,1,0:T(4,128)} %ba_ref.1, f32[3,4,96]{2,1,0:T(4,128)} %get-tuple-element.427.bb_ref, ...), custom_call_target="tpu_custom_call" | custom-call | flops 28991029248 | bytes 52428800 | tf_op jit(solution)/shard_map/project/pallas_call | solution.py:612
  159.2 0.0 collective-permute-done.3.refs_6_
  159.2 0.0 collective-permute-done.4.refs_7_
  159.2 0.0 collective-permute-done.5.refs_8_
  159.2 0.0 collective-permute-done.2.refs_5_
  159.2 52.1 %attend.1 = bf16[2,256,3072]{2,1,0:T(8,128)(2,1)} custom-call(bf16[2,3,4,96,2048]{4,3,2,1,0:T(8,128)(2,1)} %bitcast.86, bf16[2,256,3072]{2,1,0:T(8,128)(2,1)} %get-tuple-element.720.emb_hbm, f32[1,3072]{1,0:T(1,128)} %bitcast.98, bf16[384,3072]{1,0:T(8,128)(2,1)} %bitcast.84, bf16[192,3072]{1,0:T(8,128)(2,1)} %collective-permute-done.refs_1_, ...), custom_call_target="tpu_custom_call" | custom-call | tf_op jit(solution)/shard_map/attend/pallas_call | solution.py:776
  211.3 3.8 %copy.62 = bf16[2,256,3072]{2,1,0:T(8,128)(2,1)} copy(bf16[2,256,3072]{2,1,0:T(8,128)(2,1)} %attend.1) | data formatting | bytes 6291456
  (1 shorter events, 0.0 us)
Async XLA Ops:
  3.0 28.9 %collective-permute-start = (bf16[192,3072]{1,0:T(8,128)(2,1)}, bf16[192,3072]{1,0:T(8,128)(2,1)}, u32[]{:S(2)}, u32[]{:S(2)}) collective-permute-start(bf16[192,3072]{1,0:T(8,128)(2,1)} %bitcast.23), channel_id=1, source_target_pairs={{0,2},{1,3},{2,4},{3,5},{4,6},{5,7},{6,0},{7,1},{8,10},{9,11},{10,... | collective-permute-start | bytes 3538952 | tf_op jit(solution)/shard_map/ppermute | solution.py:829
  5.2 26.7 %collective-permute-start.1 = (bf16[192,3072]{1,0:T(8,128)(2,1)}, bf16[192,3072]{1,0:T(8,128)(2,1)}, u32[]{:S(2)}, u32[]{:S(2)}) collective-permute-start(bf16[192,3072]{1,0:T(8,128)(2,1)} %bitcast.23), channel_id=1, source_target_pairs={{0,6},{1,7},{2,0},{3,1},{4,2},{5,3},{6,4},{7,5},{8,14},{9,15},{10,... | collective-permute-start | bytes 3538952 | tf_op jit(solution)/shard_map/ppermute | solution.py:829
  6.7 25.2 %copy-start.2 = (f32[3072]{0:T(1024)S(1)}, f32[3072]{0:T(1024)}, u32[]{:S(2)}) copy-start(f32[3072]{0:T(1024)} %param.16) | copy-start | bytes 36868
  6.7 25.2 %copy-start.4 = (f32[3072]{0:T(1024)S(1)}, f32[3072]{0:T(1024)}, u32[]{:S(2)}) copy-start(f32[3072]{0:T(1024)} %param.17) | copy-start | bytes 36868
  31.9 79.5 %copy-start.6 = (s32[2,128]{1,0:T(2,128)S(1)}, s32[2,128]{1,0:T(2,128)}, u32[]{:S(2)}) copy-start(s32[2,128]{1,0:T(2,128)} %get-tuple-element.430) | copy-start | bytes 3076
  31.9 84.8 %copy-start = (s32[2,2048]{1,0:T(2,128)S(1)}, s32[2,2048]{1,0:T(2,128)}, u32[]{:S(2)}) copy-start(s32[2,2048]{1,0:T(2,128)} %ids_ref.1) | copy-start | bytes 49156
  31.9 84.8 %copy-start.3 = (f32[3072]{0:T(1024)S(1)}, f32[3072]{0:T(1024)}, u32[]{:S(2)}) copy-start(f32[3072]{0:T(1024)} %param.16) | copy-start | bytes 36868
  31.9 84.8 %copy-start.5 = (f32[3072]{0:T(1024)S(1)}, f32[3072]{0:T(1024)}, u32[]{:S(2)}) copy-start(f32[3072]{0:T(1024)} %param.17) | copy-start | bytes 36868
  113.3 45.9 %collective-permute-start.4 = (bf16[96,3072]{1,0:T(8,128)(2,1)}, bf16[96,3072]{1,0:T(8,128)(2,1)}, u32[]{:S(2)}, u32[]{:S(2)}) collective-permute-start(bf16[96,3072]{1,0:T(8,128)(2,1)} %get-tuple-element.444), channel_id=1, source_target_pairs={{0,2},{1,3},{2,4},{3,5},{4,6},{5,7},{6,0},{7,1},{8,10},{9,11},{10,... | collective-permute-start | bytes 1769480 | tf_op jit(solution)/shard_map/ppermute | solution.py:829
  113.4 45.8 %collective-permute-start.5 = (bf16[96,3072]{1,0:T(8,128)(2,1)}, bf16[96,3072]{1,0:T(8,128)(2,1)}, u32[]{:S(2)}, u32[]{:S(2)}) collective-permute-start(bf16[96,3072]{1,0:T(8,128)(2,1)} %get-tuple-element.444), channel_id=1, source_target_pairs={{0,6},{1,7},{2,0},{3,1},{4,2},{5,3},{6,4},{7,5},{8,14},{9,15},{10,... | collective-permute-start | bytes 1769480 | tf_op jit(solution)/shard_map/ppermute | solution.py:829
  116.7 1.1 copy-start.1
  116.8 42.5 %collective-permute-start.2 = (bf16[192,3072]{1,0:T(8,128)(2,1)}, bf16[192,3072]{1,0:T(8,128)(2,1)}, u32[]{:S(2)}, u32[]{:S(2)}) collective-permute-start(bf16[192,3072]{1,0:T(8,128)(2,1)} %collective-permute-done.refs_1_), channel_id=1, source_target_pairs={{0,2},{1,3},{2,4},{3,5},{4,6},{5,7},{6,0},{7,1},{8,10},{9,11},{10,... | collective-permute-start | bytes 3538952 | tf_op jit(solution)/shard_map/ppermute | solution.py:829
  117.8 41.4 %collective-permute-start.3 = (bf16[96,3072]{1,0:T(8,128)(2,1)S(1)}, bf16[96,3072]{1,0:T(8,128)(2,1)}, u32[]{:S(2)}, u32[]{:S(2)}) collective-permute-start(bf16[96,3072]{1,0:T(8,128)(2,1)S(1)} %copy-done.1), channel_id=1, source_target_pairs={{0,6},{1,7},{2,0},{3,1},{4,2},{5,3},{6,4},{7,5},{8,14},{9,15},{10,... | collective-permute-start | bytes 1769480 | tf_op jit(solution)/shard_map/ppermute | solution.py:829

commit v6 on v5

--- a/solution.py
+++ b/solution.py
@@ -789,7 +789,7 @@
 
 
 CAP = 264
-SOON, EARLY = 200, 1280
+SOON, EARLY = 176, 1024
 
 
 def place_kernel(code_ref, u_ref, x_ref, out_ref, sem):

time: 216 us -> 217 us (level)
  no operation moved by 1% of the time
where the time goes in v6:
time: 217 us; the launch traced here: 216 us
  Pallas kernels  194 us (89%)
  starting transfers between devices  8.48 us (4%)
  local copies, waits for them, and re-layouts  7.44 us (3%)
  waiting for transfers between devices  3.01 us (1%)
  between operations  2.74 us (1%)
    pallas_call x1, Pallas kernels, broadcast(): pl.pallas_call(functools.partial(broadcast_kernel, n, soon, early), out_s...  80.4 us
    pallas_call x1, Pallas kernels, attend(): pl.pallas_call(functools.partial(attend_kernel, n, E ** (-0.5), qb, nb, e...  52.1 us
    pallas_call x1, Pallas kernels, project(): pl.pallas_call(functools.partial(project_kernel, chunk), out_shape=(jax.S...  39.7 us
    pallas_call x1, Pallas kernels, pick(): pl.pallas_call(functools.partial(pick_kernel, n, shard_rows, cap, soon, e...  22.2 us
    ppermute x6, starting transfers between devices, local_step(): send = lambda x, step: lax.ppermute(x, 'tp', ring(step))  8.48 us
    unnamed x15, local copies, waits for them, and re-layouts  4.56 us
  transfers between devices with their start and end apart: 6, of which 1 were waited for; matrix products, arithmetic and copies ran while one was open for 0% of the time, Pallas kernels for 29%

profile of v6, /device:TPU:81, one launch (start us, length us, event | category | flops | bytes accessed | tf_op | source)
XLA Modules:
  0.0 216.0 jit_solution(13270829575222096731)
XLA Ops:
  0.6 2.4 %slice.10 = bf16[2,96,3072]{2,1,0:T(8,128)(2,1)} slice(bf16[4,96,3072]{2,1,0:T(8,128)(2,1)} %param.20), slice={[0:2], [0:96], [0:3072]} | slice | bytes 2359296 | tf_op jit(solution)/shard_map/slice | solution.py:830
  3.0 2.2 %collective-permute-start = (bf16[192,3072]{1,0:T(8,128)(2,1)}, bf16[192,3072]{1,0:T(8,128)(2,1)}, u32[]{:S(2)}, u32[]{:S(2)}) collective-permute-start(bf16[192,3072]{1,0:T(8,128)(2,1)} %bitcast.23), channel_id=1, source_target_pairs={{0,2},{1,3},{2,4},{3,5},{4,6},{5,7},{6,0},{7,1},{8,10},{9,11},{10,... | collective-permute-start | bytes 3538952 | tf_op jit(solution)/shard_map/ppermute | solution.py:829
  5.2 1.5 collective-permute-start.1
  6.7 0.0 copy-start.2
  6.7 0.0 copy-start.4
  6.7 22.2 %pick.1 = (s32[32,128]{1,0:T(8,128)S(1)}, s32[32,128]{1,0:T(8,128)}, s32[2,128]{1,0:T(2,128)}, bf16[264,24,128]{2,1,0:T(8,128)(2,1)}) custom-call(s32[2,2048]{1,0:T(2,128)} %ids_ref.1, bf16[6400,3072]{1,0:T(8,128)(2,1)} %table_ref.1), custom_call_target="tpu_custom_call" | custom-call | flops 20000000000 | bytes 12976128 | tf_op jit(solution)/shard_map/pick/pallas_call | solution.py:316
  28.9 3.0 %collective-permute-done.refs_1_ = bf16[192,3072]{1,0:T(8,128)(2,1)} collective-permute-done((bf16[192,3072]{1,0:T(8,128)(2,1)}, bf16[192,3072]{1,0:T(8,128)(2,1)}, u32[]{:S(2)}, u32[]{:S(2)}) %collective-permute-start) | collective-permute-done | bytes 1179680 | tf_op jit(solution)/shard_map/ppermute | solution.py:829
  31.9 0.0 collective-permute-done.1.refs_2_
  31.9 0.0 copy-done.2
  31.9 0.0 copy-done.4
  31.9 0.0 copy-start.6
  31.9 0.0 copy-start
  31.9 0.0 copy-start.3
  31.9 0.0 copy-start.5
  31.9 80.4 %broadcast.321 = (bf16[2048,3072]{1,0:T(8,128)(2,1)}, bf16[2,256,3072]{2,1,0:T(8,128)(2,1)}, bf16[96,3072]{1,0:T(8,128)(2,1)}, bf16[96,3072]{1,0:T(8,128)(2,1)},...) custom-call(s32[4096]{0:T(1024)} %bitcast.97, ...), custom_call_target="tpu_custom_call" | custom-call | tf_op jit(solution)/shard_map/broadcast/pallas_call | solution.py:528
  112.4 0.0 copy-done.6
  112.4 0.5 fusion.11
  114.2 1.5 collective-permute-start.4
  115.7 1.3 collective-permute-start.5
  117.6 0.0 copy-done
  117.6 0.0 copy-done.3
  117.6 0.0 copy-done.5
  117.6 0.0 copy-start.1
  117.7 0.3 collective-permute-start.2
  117.9 0.8 copy-done.1
  118.7 1.7 collective-permute-start.3
  120.4 39.7 %project.1 = (bf16[2,1152,2048]{2,1,0:T(8,128)(2,1)}, bf16[2,256,3072]{2,1,0:T(8,128)(2,1)}) custom-call(bf16[1152,3072]{1,0:T(8,128)(2,1)} %bitcast.88, bf16[1152,3072]{1,0:T(8,128)(2,1)} %get-tuple-element.426.wb_hbm, f32[3,4,96]{2,1,0:T(4,128)} %ba_ref.1, f32[3,4,96]{2,1,0:T(4,128)} %get-tuple-element.427.bb_ref, ...), custom_call_target="tpu_custom_call" | custom-call | flops 28991029248 | bytes 52428800 | tf_op jit(solution)/shard_map/project/pallas_call | solution.py:612
  160.1 0.0 collective-permute-done.3.refs_6_
  160.1 0.0 collective-permute-done.4.refs_7_
  160.1 0.0 collective-permute-done.5.refs_8_
  160.1 0.0 collective-permute-done.2.refs_5_
  160.1 52.1 %attend.1 = bf16[2,256,3072]{2,1,0:T(8,128)(2,1)} custom-call(bf16[2,3,4,96,2048]{4,3,2,1,0:T(8,128)(2,1)} %bitcast.86, bf16[2,256,3072]{2,1,0:T(8,128)(2,1)} %get-tuple-element.720.emb_hbm, f32[1,3072]{1,0:T(1,128)} %bitcast.98, bf16[384,3072]{1,0:T(8,128)(2,1)} %bitcast.84, bf16[192,3072]{1,0:T(8,128)(2,1)} %collective-permute-done.refs_1_, ...), custom_call_target="tpu_custom_call" | custom-call | tf_op jit(solution)/shard_map/attend/pallas_call | solution.py:776
  212.3 3.8 %copy.62 = bf16[2,256,3072]{2,1,0:T(8,128)(2,1)} copy(bf16[2,256,3072]{2,1,0:T(8,128)(2,1)} %attend.1) | data formatting | bytes 6291456
  (1 shorter events, 0.0 us)
Async XLA Ops:
  3.0 28.9 %collective-permute-start = (bf16[192,3072]{1,0:T(8,128)(2,1)}, bf16[192,3072]{1,0:T(8,128)(2,1)}, u32[]{:S(2)}, u32[]{:S(2)}) collective-permute-start(bf16[192,3072]{1,0:T(8,128)(2,1)} %bitcast.23), channel_id=1, source_target_pairs={{0,2},{1,3},{2,4},{3,5},{4,6},{5,7},{6,0},{7,1},{8,10},{9,11},{10,... | collective-permute-start | bytes 3538952 | tf_op jit(solution)/shard_map/ppermute | solution.py:829
  5.2 26.7 %collective-permute-start.1 = (bf16[192,3072]{1,0:T(8,128)(2,1)}, bf16[192,3072]{1,0:T(8,128)(2,1)}, u32[]{:S(2)}, u32[]{:S(2)}) collective-permute-start(bf16[192,3072]{1,0:T(8,128)(2,1)} %bitcast.23), channel_id=1, source_target_pairs={{0,6},{1,7},{2,0},{3,1},{4,2},{5,3},{6,4},{7,5},{8,14},{9,15},{10,... | collective-permute-start | bytes 3538952 | tf_op jit(solution)/shard_map/ppermute | solution.py:829
  6.7 25.2 %copy-start.2 = (f32[3072]{0:T(1024)S(1)}, f32[3072]{0:T(1024)}, u32[]{:S(2)}) copy-start(f32[3072]{0:T(1024)} %param.16) | copy-start | bytes 36868
  6.7 25.2 %copy-start.4 = (f32[3072]{0:T(1024)S(1)}, f32[3072]{0:T(1024)}, u32[]{:S(2)}) copy-start(f32[3072]{0:T(1024)} %param.17) | copy-start | bytes 36868
  31.9 80.4 %copy-start.6 = (s32[2,128]{1,0:T(2,128)S(1)}, s32[2,128]{1,0:T(2,128)}, u32[]{:S(2)}) copy-start(s32[2,128]{1,0:T(2,128)} %get-tuple-element.430) | copy-start | bytes 3076
  31.9 85.7 %copy-start = (s32[2,2048]{1,0:T(2,128)S(1)}, s32[2,2048]{1,0:T(2,128)}, u32[]{:S(2)}) copy-start(s32[2,2048]{1,0:T(2,128)} %ids_ref.1) | copy-start | bytes 49156
  31.9 85.7 %copy-start.3 = (f32[3072]{0:T(1024)S(1)}, f32[3072]{0:T(1024)}, u32[]{:S(2)}) copy-start(f32[3072]{0:T(1024)} %param.16) | copy-start | bytes 36868
  31.9 85.7 %copy-start.5 = (f32[3072]{0:T(1024)S(1)}, f32[3072]{0:T(1024)}, u32[]{:S(2)}) copy-start(f32[3072]{0:T(1024)} %param.17) | copy-start | bytes 36868
  114.2 45.9 %collective-permute-start.4 = (bf16[96,3072]{1,0:T(8,128)(2,1)}, bf16[96,3072]{1,0:T(8,128)(2,1)}, u32[]{:S(2)}, u32[]{:S(2)}) collective-permute-start(bf16[96,3072]{1,0:T(8,128)(2,1)} %get-tuple-element.444), channel_id=1, source_target_pairs={{0,2},{1,3},{2,4},{3,5},{4,6},{5,7},{6,0},{7,1},{8,10},{9,11},{10,... | collective-permute-start | bytes 1769480 | tf_op jit(solution)/shard_map/ppermute | solution.py:829
  115.7 44.5 %collective-permute-start.5 = (bf16[96,3072]{1,0:T(8,128)(2,1)}, bf16[96,3072]{1,0:T(8,128)(2,1)}, u32[]{:S(2)}, u32[]{:S(2)}) collective-permute-start(bf16[96,3072]{1,0:T(8,128)(2,1)} %get-tuple-element.444), channel_id=1, source_target_pairs={{0,6},{1,7},{2,0},{3,1},{4,2},{5,3},{6,4},{7,5},{8,14},{9,15},{10,... | collective-permute-start | bytes 1769480 | tf_op jit(solution)/shard_map/ppermute | solution.py:829
  117.6 1.1 copy-start.1
  117.7 42.5 %collective-permute-start.2 = (bf16[192,3072]{1,0:T(8,128)(2,1)}, bf16[192,3072]{1,0:T(8,128)(2,1)}, u32[]{:S(2)}, u32[]{:S(2)}) collective-permute-start(bf16[192,3072]{1,0:T(8,128)(2,1)} %collective-permute-done.refs_1_), channel_id=1, source_target_pairs={{0,2},{1,3},{2,4},{3,5},{4,6},{5,7},{6,0},{7,1},{8,10},{9,11},{10,... | collective-permute-start | bytes 3538952 | tf_op jit(solution)/shard_map/ppermute | solution.py:829
  118.7 41.4 %collective-permute-start.3 = (bf16[96,3072]{1,0:T(8,128)(2,1)S(1)}, bf16[96,3072]{1,0:T(8,128)(2,1)}, u32[]{:S(2)}, u32[]{:S(2)}) collective-permute-start(bf16[96,3072]{1,0:T(8,128)(2,1)S(1)} %copy-done.1), channel_id=1, source_target_pairs={{0,6},{1,7},{2,0},{3,1},{4,2},{5,3},{6,4},{7,5},{8,14},{9,15},{10,... | collective-permute-start | bytes 1769480 | tf_op jit(solution)/shard_map/ppermute | solution.py:829
